TPU v7x, 256 devices: a whole 4x4x8 slice. The times are simulated.
256 devices in a mesh: batch: 4 (over x), heads: 64 (over y, z, core).
Axes of the slice: x: 4, y: 4, z: 8, core: 2. Of those that a mesh axis runs over, the one named last changes fastest.
Arguments:
- draft_ids: int32 [192, 8], P('batch'), may hold values from 0 to 50279
- accepted: int32 [192], P('batch'), may hold values from 1 to 8
- embedding: bfloat16 [50280, 2560], P(None, 'heads'), may hold values from -6 to 6
- norm_gain: float32 [2, 2560], replicated, may hold values from 0.5 to 1.5
- w_zx: bfloat16 [2, 2560, 64, 128], P(None, None, 'heads'), may hold values from -0.125 to 0.125
- w_dt: bfloat16 [2, 2560, 64], P(None, None, 'heads'), may hold values from -0.125 to 0.125
- w_bc: bfloat16 [2, 2560, 256], P(None, None, 'heads'), may hold values from -0.125 to 0.125
- dt_bias: float32 [2, 64], P(None, 'heads'), may hold values from -4 to -1
- decay_rate: float32 [2, 64], P(None, 'heads'), may hold values from 1 to 16
- skip_weight: float32 [2, 64], P(None, 'heads'), may hold values from 0.5 to 1.5
- conv_x_w: bfloat16 [2, 4, 4096], P(None, None, 'heads'), may hold values from -3 to 3
- conv_x_b: bfloat16 [2, 4096], P(None, 'heads'), may hold values from -3 to 3
- conv_bc_w: bfloat16 [2, 4, 256], P(None, None, 'heads'), may hold values from -3 to 3
- conv_bc_b: bfloat16 [2, 256], P(None, 'heads'), may hold values from -3 to 3
- gate_gain: float32 [2, 4096], P(None, 'heads'), may hold values from 0.5 to 1.5
- out_w: bfloat16 [2, 4096, 2560], P(None, 'heads'), may hold values from -0.25 to 0.25
- ssm_state: float32 [2, 192, 64, 64, 128], P(None, 'batch', 'heads'), may hold values from -1.6 to 1.6
- conv_x_state: bfloat16 [2, 192, 3, 4096], P(None, 'batch', None, 'heads'), may hold values from -6 to 6
- conv_bc_state: bfloat16 [2, 192, 3, 256], P(None, 'batch', None, 'heads'), may hold values from -6 to 6
Outputs:
- hidden_out: bfloat16 [1536, 2560], P('batch', 'heads')
- new_ssm: float32 [2, 192, 64, 64, 128], P(None, 'batch', 'heads')
- new_conv_x: bfloat16 [2, 192, 3, 4096], P(None, 'batch', None, 'heads')
- new_conv_bc: bfloat16 [2, 192, 3, 256], P(None, 'batch', None, 'heads')
Inputs may be any that keep to these rules, and one draw needn't show every extreme that they name: `accepted`: the number of a sequence's draft tokens that are kept, counted from the first.
All inputs are finite; a program needn't handle non-finite values.
Results may differ from a plain program's by a relative error of at most 0.015.
Values may be sent and summed in bfloat16 or wider, within the bound.
No kernel may reach another device: no remote copies, remote signals or barrier semaphores. Data moves between devices by JAX's collectives and lax.ppermute only.
A program may use at most 128 MiB of HBM per device.

v0:
```python
import jax
import jax.numpy as jnp
from jax import lax
from jax.sharding import PartitionSpec as P

LAYERS = 2


EPS = 1e-05


def turned_gather(arrays, axis, dims):
    turned = [jnp.moveaxis(a, dim, 0) for a, dim in zip(arrays, dims)]
    widths = [t[0].size for t in turned]
    both = jnp.concatenate([t.reshape(-1, w) for t, w in zip(turned, widths)], axis=1)
    filled = lax.all_gather(both, axis, axis=0, tiled=True)
    blocks = jnp.split(filled, [sum(widths[:k]) for k in range(1, len(widths))], axis=1)
    return tuple(
        (
            jnp.moveaxis(b.reshape(-1, *t.shape[1:]), 0, dim)
            for b, t, dim in zip(blocks, turned, dims)
        )
    )


def in_order(blocks, dim):
    blocks = jnp.moveaxis(blocks, 0, dim)
    dims = blocks.shape
    return blocks.reshape(*dims[:dim], dims[dim] * dims[dim + 1], *dims[dim + 2 :])


def sent_to_all(value, axis):
    count = lax.axis_size(axis)
    return lax.all_to_all(
        jnp.broadcast_to(value[None], (count, *value.shape)), axis, 0, 0, tiled=True
    )


def gather_directly(value, axis, dim):
    return in_order(sent_to_all(value, axis), dim)


def rms_scale(total, count):
    return lax.rsqrt(total / count + EPS)


def convolve(window, weight, bias, count):
    weight = weight.astype(jnp.float32)
    acc = window[:, 0:count] * weight[0]
    for k in range(1, weight.shape[0]):
        acc = acc + window[:, k : k + count] * weight[k]
    return jax.nn.silu(acc + bias.astype(jnp.float32))


def keep_rows(window, accepted, kept_rows):
    last_start = window.shape[1] - kept_rows
    kept = window[:, 1 : 1 + kept_rows]
    for start in range(2, last_start + 1):
        kept = jnp.where(
            (accepted == start)[:, None, None], window[:, start : start + kept_rows], kept
        )
    return kept


def recur(decay, step, values, bmat, cmat, skip, state, accepted):
    kept = state
    outputs = []
    for t in range(values.shape[1]):
        state = (
            decay[:, t, None, None] * state
            + (step[:, t, None] * values[:, t])[:, :, None] * bmat[:, t, None, :]
        )
        outputs.append(jnp.sum(state * cmat[:, t, None, :], axis=-1) + skip * values[:, t])
        kept = jnp.where((accepted == t + 1)[:, None, None], state, kept)
    return (jnp.stack(outputs, 1), kept)


def local(
    draft_ids,
    accepted,
    embedding,
    norm_gain,
    w_zx,
    w_dt,
    w_bc,
    dt_bias,
    decay_rate,
    skip_weight,
    conv_x_w,
    conv_x_b,
    conv_bc_w,
    conv_bc_b,
    gate_gain,
    out_w,
    ssm_state,
    conv_x_state,
    conv_bc_state,
):
    seq_rows, draft = draft_ids.shape
    heads_here = w_zx.shape[2]
    width = w_zx.shape[3] // 2
    local_inner = heads_here * width
    own_cols = embedding.shape[1]
    model = own_cols * lax.axis_size("heads")
    inner = local_inner * lax.axis_size("heads")
    bc_here = w_bc.shape[2]
    kernel = conv_x_w.shape[1]
    recur_heads = jax.vmap(recur, in_axes=(2, 2, 2, None, None, 0, 1, None), out_axes=(2, 1))
    whole_bc = turned_gather((w_bc, conv_bc_w, conv_bc_b, conv_bc_state), "heads", (2, 2, 1, 3))
    saved_state, saved_x, saved_bc = ([], [], [])

    def mixer(layer, stream):
        value = stream.astype(jnp.float32)
        normed = (
            value * rms_scale(jnp.sum(value * value, -1, keepdims=True), model) * norm_gain[layer]
        ).astype(jnp.bfloat16)
        zx = jnp.dot(
            normed, w_zx[layer].reshape(model, -1), preferred_element_type=jnp.float32
        ).astype(jnp.bfloat16)
        zx = zx.reshape(seq_rows, draft, heads_here, 2, width)
        gate_z = zx[:, :, :, 0].astype(jnp.float32)
        values = zx[:, :, :, 1].reshape(seq_rows, draft, local_inner)
        dt_raw = (
            jnp.dot(normed, w_dt[layer], preferred_element_type=jnp.float32)
            .astype(jnp.bfloat16)
            .reshape(seq_rows, draft, heads_here)
        )
        bc = (
            jnp.dot(normed, whole_bc[0][layer], preferred_element_type=jnp.float32)
            .astype(jnp.bfloat16)
            .reshape(seq_rows, draft, -1)
        )
        window_bc = jnp.concatenate([whole_bc[3][layer], bc], axis=1)
        bcc = convolve(
            window_bc.astype(jnp.float32), whole_bc[1][layer], whole_bc[2][layer], draft
        ).astype(jnp.bfloat16)
        kept_bc = keep_rows(window_bc, accepted, kernel - 1)
        bcc = lax.optimization_barrier(bcc).astype(jnp.float32)
        kept_bc = lax.dynamic_slice_in_dim(kept_bc, lax.axis_index("heads") * bc_here, bc_here, 2)
        states = bcc.shape[2] // 2
        bmat = bcc[..., :states]
        cmat = bcc[..., states:]
        window_x = jnp.concatenate([conv_x_state[layer], values], axis=1)
        xc = convolve(
            window_x.astype(jnp.float32), conv_x_w[layer], conv_x_b[layer], draft
        ).reshape(seq_rows, draft, heads_here, width)
        step = jax.nn.softplus(dt_raw.astype(jnp.float32) + dt_bias[layer])
        decay = jnp.exp(-step * decay_rate[layer])
        outputs, kept = recur_heads(
            decay, step, xc, bmat, cmat, skip_weight[layer], ssm_state[layer], accepted
        )
        saved_state.append(kept)
        saved_x.append(keep_rows(window_x, accepted, kernel - 1))
        saved_bc.append(kept_bc)
        gated = outputs * jax.nn.silu(gate_z)
        local_sq = jnp.sum(gated * gated, axis=(2, 3)).reshape(-1)
        u_rows = (
            (gated.reshape(seq_rows, draft, local_inner) * gate_gain[layer])
            .astype(jnp.bfloat16)
            .reshape(-1, local_inner)
        )
        return (u_rows, local_sq)

    part = embedding[draft_ids.reshape(-1)]
    stream = gather_directly(part, "heads", 1)
    where_cols = lax.axis_index("heads") * own_cols
    result = part
    for layer in range(LAYERS):
        u_rows, local_sq = mixer(layer, stream)
        term = jnp.dot(u_rows, out_w[layer], preferred_element_type=jnp.float32)
        total, ssq = lax.psum((term, local_sq), "heads")
        mix = total * rms_scale(ssq, inner)[:, None]
        if layer + 1 < LAYERS:
            stream = (stream.astype(jnp.float32) + mix).astype(jnp.bfloat16)
        else:
            own_stream = lax.dynamic_slice_in_dim(stream, where_cols, own_cols, 1)
            own_mix = lax.dynamic_slice_in_dim(mix, where_cols, own_cols, 1)
            result = (own_stream.astype(jnp.float32) + own_mix).astype(jnp.bfloat16)
    return (result, jnp.stack(saved_state), jnp.stack(saved_x), jnp.stack(saved_bc))


def solution(mesh):
    placed = (
        P("batch", None),
        P("batch"),
        P(None, "heads"),
        P(),
        P(None, None, "heads", None),
        P(None, None, "heads"),
        P(None, None, "heads"),
        P(None, "heads"),
        P(None, "heads"),
        P(None, "heads"),
        P(None, None, "heads"),
        P(None, "heads"),
        P(None, None, "heads"),
        P(None, "heads"),
        P(None, "heads"),
        P(None, "heads", None),
        P(None, "batch", "heads", None, None),
        P(None, "batch", None, "heads"),
        P(None, "batch", None, "heads"),
    )
    return jax.shard_map(
        local,
        mesh=mesh,
        in_specs=placed,
        out_specs=(
            P("batch", "heads"),
            P(None, "batch", "heads", None, None),
            P(None, "batch", None, "heads"),
            P(None, "batch", None, "heads"),
        ),
        check_vma=False,
    )
```

profile of v0, /device:TPU:2, one launch (start us, length us, event | category | flops | bytes accessed | tf_op | source)
XLA Modules:
  0.0 601.5 jit_solution(6505205176545360938)
XLA Ops:
  7.2 11.0 %copy.97 = bf16[50280,40]{1,0:T(8,128)(2,1)} copy(bf16[50280,40]{0,1:T(8,128)(2,1)} %param.21) | data formatting | bytes 8044800 | tf_op args[2]
  18.4 7.5 %gather_fusion = bf16[384,40]{1,0:T(8,128)(2,1)S(1)} fusion(bf16[50280,40]{1,0:T(8,128)(2,1)} %copy.97, s32[1024]{0:T(1024)S(1)} %pad_clamp_fusion), kind=kCustom, calls=%fused_computation | custom fusion | bytes 62976 | tf_op jit(solution)/shard_map/gather | solution.py:164
  26.0 1.4 broadcast_in_dim.263
  27.5 12.2 %all-to-all-start = ((bf16[64,384,40]{1,2,0:T(8,128)(2,1)}), bf16[64,384,40]{1,2,0:T(8,128)(2,1)S(1)}, u32[]{:S(2)}, u32[]{:S(2)}) async-start(bf16[64,384,40]{1,2,0:T(8,128)(2,1)} %broadcast_in_dim.263), calls=%async_computation | async-start | bytes 3932160 | tf_op jit(solution)/shard_map/all_to_all | solution.py:34
  45.7 43.7 %all-to-all-done = bf16[64,384,40]{1,2,0:T(8,128)(2,1)S(1)} async-done(((bf16[64,384,40]{1,2,0:T(8,128)(2,1)}), bf16[64,384,40]{1,2,0:T(8,128)(2,1)S(1)}, u32[]{:S(2)}, u32[]{:S(2)}) %all-to-all-start) | async-done | bytes 1966112 | tf_op jit(solution)/shard_map/all_to_all | solution.py:34
  90.5 1.3 copy-done.3
  93.0 2.0 convolution_reduce_fusion.1
  98.5 26.6 %all-gather.3.cloned.1.call-done = bf16[64,4,5418]{2,1,0:T(4,128)(2,1)} async-done(((bf16[1,4,5418]{2,1,0:T(4,128)(2,1)}), bf16[64,4,5418]{2,1,0:T(4,128)(2,1)}) %all-gather.3.cloned.1.call-update) | async-done | bytes 2774032 | tf_op jit(solution)/shard_map/all_gather | solution.py:16
  125.0 5.5 reshape.2596
  130.6 3.6 split.17
  134.3 4.4 copy.128
  138.8 2.7 fusion.10
  145.8 4.1 multiply_add_fusion.8
  150.6 1.7 multiply_reduce_fusion.13
  154.1 3.7 multiply_reduce_fusion.9
  160.3 2.5 fusion.27
  164.1 2.2 convert_element_type.337
  166.3 5.6 copy.109
  172.0 1.4 fusion.103
  174.7 126.8 %psum.29 = f32[384]{0:T(512)S(1)} all-reduce(f32[384]{0:T(512)S(1)} %reshape.2572), channel_id=1, replica_groups=mesh['batch'=4,'heads'=64] {'heads'}, use_global_device_ids=true, to_apply=%region_11.12 | all-reduce | flops 384 | bytes 3072 | tf_op jit(solution)/shard_map/psum | solution.py:171
  301.6 1.4 fusion.119
  303.0 9.0 %select_select_fusion.1 = f32[1,48,1,64,128]{4,3,2,1,0:T(8,128)} fusion(f32[2,48,1,64,128]{4,3,2,1,0:T(8,128)S(1)} %copy-done.1, f32[48,128]{1,0:T(8,128)} %bitcast.581, f32[48,64]{1,0:T(8,128)} %copy-done.34, f32[48,128]{1,0:T(8,128)} %bitcast.579, f32[48,64]{1,0:T(8,128)} %copy-done.35, f32[48,128]{1,0:T(8,128)S(1)} %bitcast.577, f32[48,64]{1,0:T(8,128)} %copy-done.33, ...), kind=kLoop, calls=%fused_computation.15 | loop fusion | flops 12582912 | bytes 3442560 | tf_op jit(solution)/shard_map/vmap(jit(_where))/select_n | solution.py:74
  312.0 43.2 %all-reduce.3.cloned.1.call-done = f32[384,2560]{1,0:T(8,128)} async-done(((f32[384,2560]{1,0:T(8,128)}), f32[384,2560]{1,0:T(8,128)}) %all-reduce.3.cloned.1.call-update) | async-done | bytes 3932176 | tf_op jit(solution)/shard_map/psum | solution.py:171
  355.2 4.2 fusion
  360.1 1.3 copy-done.91
  361.4 1.4 convolution_convert_fusion
  362.8 1.3 convolution_reduce_fusion
  364.1 1.7 reshape.2574
  365.8 2.1 fusion.115
  369.4 1.4 fusion.127
  371.7 1.8 fusion.113
  375.2 2.2 multiply_convert_fusion.1
  380.6 4.1 multiply_add_fusion.2
  385.4 1.7 multiply_reduce_fusion.5
  389.0 3.7 multiply_reduce_fusion.1
  394.4 1.3 constant_dynamic-update-slice_fusion.24
  396.5 2.5 fusion.25
  399.1 2.2 dynamic-slice_select_fusion.6
  401.3 1.5 copy.123
  402.8 2.1 dynamic-slice_select_fusion
  404.9 1.4 copy.124
  406.4 1.7 fusion.71
  408.9 128.1 %psum.31 = f32[384]{0:T(512)S(1)} all-reduce(f32[384]{0:T(512)S(1)} %reshape.2577), channel_id=1, replica_groups=mesh['batch'=4,'heads'=64] {'heads'}, use_global_device_ids=true, to_apply=%region_23.24 | all-reduce | flops 384 | bytes 3072 | tf_op jit(solution)/shard_map/psum | solution.py:171
  537.0 1.3 pad_maximum_fusion.6
  539.2 1.4 pad_maximum_fusion.5
  540.6 8.3 %select_select_fusion = f32[1,48,1,64,128]{4,3,2,1,0:T(8,128)S(1)} fusion(f32[2,48,1,64,128]{4,3,2,1,0:T(8,128)S(1)} %copy-done.1, f32[48,128]{1,0:T(8,128)} %bitcast.567, f32[48,64]{1,0:T(8,128)} %copy-done.40, f32[48,128]{1,0:T(8,128)} %bitcast.565, f32[48,64]{1,0:T(8,128)} %copy-done.42, f32[48,128]{1,0:T(8,128)S(1)} %bitcast.563, ...), kind=kLoop, calls=%fused_computation.14 | loop fusion | flops 12582912 | bytes 3442560 | tf_op jit(solution)/shard_map/vmap(jit(_where))/select_n | solution.py:74
  548.9 1.9 pad_maximum_fusion
  550.8 42.3 %all-reduce.5.cloned.1.call-done = f32[384,2560]{1,0:T(8,128)} async-done(((f32[384,2560]{1,0:T(8,128)}), f32[384,2560]{1,0:T(8,128)}) %all-reduce.5.cloned.1.call-update) | async-done | bytes 3932176 | tf_op jit(solution)/shard_map/psum | solution.py:171
  (282 shorter events, 39.9 us)
Async XLA Ops:
  7.2 11.0 %copy-start.78 = (s32[48,8]{0,1:T(8,128)S(1)}, s32[48,8]{0,1:T(8,128)}, u32[]{:S(2)}) copy-start(s32[48,8]{0,1:T(8,128)} %param.19) | copy-start | bytes 4612
  27.4 12.4 %copy-start.56 = (bf16[2,48,3,4]{1,3,2,0:T(4,128)(2,1)S(1)}, bf16[2,48,3,4]{1,3,2,0:T(4,128)(2,1)}, u32[]{:S(2)}) copy-start(bf16[2,48,3,4]{1,3,2,0:T(4,128)(2,1)} %param.37) | copy-start | bytes 6916
  27.4 12.8 %copy-start.92 = (bf16[2,4]{1,0:T(2,128)(2,1)S(1)}, bf16[2,4]{1,0:T(2,128)(2,1)}, u32[]{:S(2)}) copy-start(bf16[2,4]{1,0:T(2,128)(2,1)} %param.32) | copy-start | bytes 52
  27.4 12.9 %copy-start.82 = (bf16[2,4,4]{2,1,0:T(4,128)(2,1)S(1)}, bf16[2,4,4]{2,1,0:T(4,128)(2,1)}, u32[]{:S(2)}) copy-start(bf16[2,4,4]{2,1,0:T(4,128)(2,1)} %param.31) | copy-start | bytes 196
  27.4 13.0 %copy-start.48 = (bf16[2,2560,4]{1,2,0:T(4,128)(2,1)S(1)}, bf16[2,2560,4]{1,2,0:T(4,128)(2,1)}, u32[]{:S(2)}) copy-start(bf16[2,2560,4]{1,2,0:T(4,128)(2,1)} %param.25) | copy-start | bytes 122884
  27.4 13.9 %copy-start.49 = (f32[2,2560]{1,0:T(2,128)S(1)}, f32[2,2560]{1,0:T(2,128)}, u32[]{:S(2)}) copy-start(f32[2,2560]{1,0:T(2,128)} %param.22) | copy-start | bytes 61444
  27.5 14.7 %copy-start.83 = (f32[2,1]{0,1:T(1,128)S(1)}, f32[2,1]{0,1:T(1,128)}, u32[]{:S(2)}) copy-start(f32[2,1]{0,1:T(1,128)} %param.26) | copy-start | bytes 28
  27.5 15.3 %copy-start.84 = (f32[2,1]{0,1:T(1,128)S(1)}, f32[2,1]{0,1:T(1,128)}, u32[]{:S(2)}) copy-start(f32[2,1]{0,1:T(1,128)} %param.27) | copy-start | bytes 28
  27.5 15.9 %copy-start.85 = (f32[2,1]{0,1:T(1,128)S(1)}, f32[2,1]{0,1:T(1,128)}, u32[]{:S(2)}) copy-start(f32[2,1]{0,1:T(1,128)} %param.28) | copy-start | bytes 28
  27.5 16.4 %copy-start.86 = (bf16[2,64]{1,0:T(2,128)(2,1)S(1)}, bf16[2,64]{1,0:T(2,128)(2,1)}, u32[]{:S(2)}) copy-start(bf16[2,64]{1,0:T(2,128)(2,1)} %param.30) | copy-start | bytes 772
  27.5 17.0 %copy-start.88 = (f32[2,64]{1,0:T(2,128)S(1)}, f32[2,64]{1,0:T(2,128)}, u32[]{:S(2)}) copy-start(f32[2,64]{1,0:T(2,128)} %param.33) | copy-start | bytes 1540
  27.5 17.6 %copy-start.81 = (bf16[2,4,64]{2,1,0:T(4,128)(2,1)S(1)}, bf16[2,4,64]{2,1,0:T(4,128)(2,1)}, u32[]{:S(2)}) copy-start(bf16[2,4,64]{2,1,0:T(4,128)(2,1)} %param.29) | copy-start | bytes 3076
  27.5 17.6 %copy-start.47 = (bf16[2,48,3,64]{3,1,2,0:T(8,128)(2,1)S(1)}, bf16[2,48,3,64]{3,1,2,0:T(8,128)(2,1)}, u32[]{:S(2)}) copy-start(bf16[2,48,3,64]{3,1,2,0:T(8,128)(2,1)} %param.36) | copy-start | bytes 110596
  27.5 61.9 %all-to-all-start = ((bf16[64,384,40]{1,2,0:T(8,128)(2,1)}), bf16[64,384,40]{1,2,0:T(8,128)(2,1)S(1)}, u32[]{:S(2)}, u32[]{:S(2)}) async-start(bf16[64,384,40]{1,2,0:T(8,128)(2,1)} %broadcast_in_dim.263), calls=%async_computation | async-start | bytes 3932160 | tf_op jit(solution)/shard_map/all_to_all | solution.py:34
  39.8 85.3 %all-gather.3.cloned.1.call-start = ((), (), s32[]{:S(2)}) async-start(), calls=%async_computation.3 | async-start | bytes 2862080 | tf_op jit(solution)/shard_map/all_gather | solution.py:16
  41.2 314.0 %all-reduce.3.cloned.1.call-start = ((), (), s32[]{:S(2)}) async-start(), calls=%async_computation.1 | async-start | bytes 7864320 | tf_op jit(solution)/shard_map/psum | solution.py:171
  92.9 67.2 %copy-start.9 = (bf16[48,8,1,1,64]{4,3,1,0,2:T(2,128)(2,1)}, bf16[48,8,1,1,64]{4,3,1,0,2:T(2,128)(2,1)S(1)}, u32[]{:S(2)}) copy-start(bf16[48,8,1,1,64]{4,3,1,0,2:T(2,128)(2,1)S(1)} %get-tuple-element.155) | copy-start | bytes 147460
  97.6 47.0 %copy-start.62 = (f32[48]{0:T(128)}, f32[48]{0:T(128)S(1)}, u32[]{:S(2)}) copy-start(f32[48]{0:T(128)S(1)} %get-tuple-element.57) | copy-start | bytes 580
  97.6 53.0 %copy-start.54 = (f32[48]{0:T(128)}, f32[48]{0:T(128)S(1)}, u32[]{:S(2)}) copy-start(f32[48]{0:T(128)S(1)} %get-tuple-element.58) | copy-start | bytes 580
  98.5 46.1 %copy-start.36 = (f32[48,64]{1,0:T(8,128)}, f32[48,64]{1,0:T(8,128)S(1)}, u32[]{:S(2)}) copy-start(f32[48,64]{1,0:T(8,128)S(1)} %get-tuple-element.176) | copy-start | bytes 36868
  98.5 55.6 %copy-start.33 = (f32[48,64]{1,0:T(8,128)}, f32[48,64]{1,0:T(8,128)S(1)}, u32[]{:S(2)}) copy-start(f32[48,64]{1,0:T(8,128)S(1)} %get-tuple-element.173) | copy-start | bytes 36868
  98.5 55.6 %copy-start.34 = (f32[48,64]{1,0:T(8,128)}, f32[48,64]{1,0:T(8,128)S(1)}, u32[]{:S(2)}) copy-start(f32[48,64]{1,0:T(8,128)S(1)} %get-tuple-element.174) | copy-start | bytes 36868
  98.5 55.6 %copy-start.35 = (f32[48,64]{1,0:T(8,128)}, f32[48,64]{1,0:T(8,128)S(1)}, u32[]{:S(2)}) copy-start(f32[48,64]{1,0:T(8,128)S(1)} %get-tuple-element.175) | copy-start | bytes 36868
  144.6 9.5 %copy-start.27 = (f32[48,1,128]{2,1,0:T(1,128)}, f32[48,1,128]{2,1,0:T(1,128)S(1)}, u32[]{:S(2)}) copy-start(f32[48,1,128]{2,1,0:T(1,128)S(1)} %get-tuple-element.161) | copy-start | bytes 73732
  144.6 9.5 %copy-start.28 = (f32[48,1,128]{2,1,0:T(1,128)}, f32[48,1,128]{2,1,0:T(1,128)S(1)}, u32[]{:S(2)}) copy-start(f32[48,1,128]{2,1,0:T(1,128)S(1)} %get-tuple-element.162) | copy-start | bytes 73732
  152.2 7.9 %copy-start.80 = (f32[64]{0:T(128)S(1)}, f32[64]{0:T(128)}, u32[]{:S(2)}) copy-start(f32[64]{0:T(128)} %get-tuple-element.208) | copy-start | bytes 772
  152.3 8.0 %copy-start.16 = (bf16[2,64,2560]{2,1,0:T(8,128)(2,1)S(1)}, bf16[2,64,2560]{2,1,0:T(8,128)(2,1)}, u32[]{:S(2)}) copy-start(bf16[2,64,2560]{2,1,0:T(8,128)(2,1)} %param.34) | copy-start | bytes 1966084
  162.8 430.2 %all-reduce.5.cloned.1.call-start = ((), (), s32[]{:S(2)}) async-start(), calls=%async_computation.2 | async-start | bytes 7864320 | tf_op jit(solution)/shard_map/psum | solution.py:171
  166.3 136.7 %copy-start.1 = (f32[2,48,1,64,128]{4,3,2,1,0:T(8,128)S(1)}, f32[2,48,1,64,128]{4,3,2,1,0:T(8,128)}, u32[]{:S(2)}) copy-start(f32[2,48,1,64,128]{4,3,2,1,0:T(8,128)} %param.35) | copy-start | bytes 9437188
  312.0 47.4 %copy-start.51 = (f32[2560]{0:T(1024)S(1)}, f32[2560]{0:T(1024)}, u32[]{:S(2)}) copy-start(f32[2560]{0:T(1024)} %get-tuple-element.70) | copy-start | bytes 30724
  377.7 7.0 %copy-start.23 = (f32[48,1,128]{2,1,0:T(1,128)}, f32[48,1,128]{2,1,0:T(1,128)S(1)}, u32[]{:S(2)}) copy-start(f32[48,1,128]{2,1,0:T(1,128)S(1)} %get-tuple-element.137) | copy-start | bytes 73732
  377.7 7.0 %copy-start.24 = (f32[48,1,128]{2,1,0:T(1,128)}, f32[48,1,128]{2,1,0:T(1,128)S(1)}, u32[]{:S(2)}) copy-start(f32[48,1,128]{2,1,0:T(1,128)S(1)} %get-tuple-element.141) | copy-start | bytes 73732
  377.7 7.0 %copy-start.25 = (f32[48,1,128]{2,1,0:T(1,128)}, f32[48,1,128]{2,1,0:T(1,128)S(1)}, u32[]{:S(2)}) copy-start(f32[48,1,128]{2,1,0:T(1,128)S(1)} %get-tuple-element.143) | copy-start | bytes 73732
  377.7 7.0 %copy-start.26 = (f32[48,1,128]{2,1,0:T(1,128)}, f32[48,1,128]{2,1,0:T(1,128)S(1)}, u32[]{:S(2)}) copy-start(f32[48,1,128]{2,1,0:T(1,128)S(1)} %get-tuple-element.144) | copy-start | bytes 73732
  377.7 11.2 %copy-start.21 = (f32[48,1,128]{2,1,0:T(1,128)}, f32[48,1,128]{2,1,0:T(1,128)S(1)}, u32[]{:S(2)}) copy-start(f32[48,1,128]{2,1,0:T(1,128)S(1)} %get-tuple-element.134) | copy-start | bytes 73732
  377.7 11.2 %copy-start.22 = (f32[48,1,128]{2,1,0:T(1,128)}, f32[48,1,128]{2,1,0:T(1,128)S(1)}, u32[]{:S(2)}) copy-start(f32[48,1,128]{2,1,0:T(1,128)S(1)} %get-tuple-element.135) | copy-start | bytes 73732
  378.9 10.0 %copy-start.73 = (f32[48]{0:T(128)}, f32[48]{0:T(128)S(1)}, u32[]{:S(2)}) copy-start(f32[48]{0:T(128)S(1)} %get-tuple-element.237) | copy-start | bytes 580
  378.9 10.0 %copy-start.74 = (f32[48]{0:T(128)}, f32[48]{0:T(128)S(1)}, u32[]{:S(2)}) copy-start(f32[48]{0:T(128)S(1)} %get-tuple-element.238) | copy-start | bytes 580
  379.0 10.0 %copy-start.75 = (f32[48]{0:T(128)}, f32[48]{0:T(128)S(1)}, u32[]{:S(2)}) copy-start(f32[48]{0:T(128)S(1)} %get-tuple-element.239) | copy-start | bytes 580
  379.8 9.2 %copy-start.40 = (f32[48,64]{1,0:T(8,128)}, f32[48,64]{1,0:T(8,128)S(1)}, u32[]{:S(2)}) copy-start(f32[48,64]{1,0:T(8,128)S(1)} %bitcast_multiply_fusion.2) | copy-start | bytes 36868
  379.9 9.0 %copy-start.41 = (f32[48,64]{1,0:T(8,128)}, f32[48,64]{1,0:T(8,128)S(1)}, u32[]{:S(2)}) copy-start(f32[48,64]{1,0:T(8,128)S(1)} %get-tuple-element.146) | copy-start | bytes 36868
  380.0 9.0 %copy-start.42 = (f32[48,64]{1,0:T(8,128)}, f32[48,64]{1,0:T(8,128)S(1)}, u32[]{:S(2)}) copy-start(f32[48,64]{1,0:T(8,128)S(1)} %get-tuple-element.147) | copy-start | bytes 36868
  387.0 9.4 %copy-start.10 = (bf16[48,8,1,1,64]{4,3,1,0,2:T(2,128)(2,1)S(1)}, bf16[48,8,1,1,64]{4,3,1,0,2:T(2,128)(2,1)}, u32[]{:S(2)}) copy-start(bf16[48,8,1,1,64]{4,3,1,0,2:T(2,128)(2,1)} %get-tuple-element.128) | copy-start | bytes 147460
  387.1 9.4 %copy-start.79 = (f32[64]{0:T(128)S(1)}, f32[64]{0:T(128)}, u32[]{:S(2)}) copy-start(f32[64]{0:T(128)} %get-tuple-element.207) | copy-start | bytes 772
  387.1 9.4 %copy-start.17 = (bf16[2,64,2560]{2,1,0:T(8,128)(2,1)S(1)}, bf16[2,64,2560]{2,1,0:T(8,128)(2,1)}, u32[]{:S(2)}) copy-start(bf16[2,64,2560]{2,1,0:T(8,128)(2,1)} %param.34) | copy-start | bytes 1966084
  399.1 139.3 %copy-start.18 = (bf16[48,3,64]{2,0,1:T(8,128)(2,1)S(1)}, bf16[48,3,64]{2,0,1:T(8,128)(2,1)}, u32[]{:S(2)}) copy-start(bf16[48,3,64]{2,0,1:T(8,128)(2,1)} %get-tuple-element.181) | copy-start | bytes 55300
  399.1 139.2 %copy-start.6 = (bf16[48,8,1,1,64]{4,0,1,3,2:T(8,128)(2,1)S(1)}, bf16[48,8,1,1,64]{4,0,1,3,2:T(8,128)(2,1)}, u32[]{:S(2)}) copy-start(bf16[48,8,1,1,64]{4,0,1,3,2:T(8,128)(2,1)} %copy-done.5) | copy-start | bytes 147460
  540.6 8.3 %copy-start.4 = (f32[1,48,1,64,128]{4,3,2,1,0:T(8,128)S(1)}, f32[1,48,1,64,128]{4,3,2,1,0:T(8,128)}, u32[]{:S(2)}) copy-start(f32[1,48,1,64,128]{4,3,2,1,0:T(8,128)} %select_select_fusion.1) | copy-start | bytes 4718596
  (50 other events, 168.0 us)
Sparse Core Ops, SparseCore 0:
  43.9 81.1 all-gather.2
  163.0 192.1 all-reduce.2
  399.2 193.7 all-reduce.4
where the time goes:
time: 603 us; the launch traced here: 602 us
  blocking collectives  255 us (42%)
  waiting for transfers between devices  156 us (26%)
  other arithmetic  84.4 us (14%)
  local copies, waits for them, and re-layouts  64.7 us (11%)
  between operations  15.2 us (3%)
  matrix products  13.8 us (2%)
  starting transfers between devices  12.6 us (2%)
    psum x2, blocking collectives, local(): total, ssq = lax.psum((term, local_sq), 'heads')  255 us
    psum x2, waiting for transfers between devices, local(): total, ssq = lax.psum((term, local_sq), 'heads')  85.4 us
    all_to_all x1, waiting for transfers between devices, sent_to_all(): lax.all_to_all(jnp.broadcast_to(value[None], (count, *value.shape)), axis...  43.7 us
    all_gather x1, waiting for transfers between devices, turned_gather(): filled = lax.all_gather(both, axis, axis=0, tiled=True)  26.6 us
    unnamed x193, local copies, waits for them, and re-layouts  23.4 us
    select_n x2, other arithmetic, recur(): kept = jnp.where((accepted == t + 1)[:, None, None], state, kept)  17.3 us
    all_to_all x1, starting transfers between devices, sent_to_all(): lax.all_to_all(jnp.broadcast_to(value[None], (count, *value.shape)), axis...  12.2 us
  transfers between devices with their start and end apart: 4, of which 4 were waited for; matrix products, arithmetic and copies ran while one was open for 10% of the time, Pallas kernels for 0%

commit v1 on v0

v1 whole, which is shorter than its diff:
```python
import jax
import jax.numpy as jnp
from jax import lax
from jax.experimental import pallas as pl
from jax.experimental.pallas import tpu as pltpu
from jax.sharding import PartitionSpec as P

LAYERS = 2
EPS = 1e-05
BF = jnp.bfloat16
F32 = jnp.float32
LANES = 128

YS, ZS, CS = 4, 8, 2


def device_at(y, z, c):
    return (y * ZS + z) * CS + c


Z_GROUPS = [[device_at(y, z, c) for z in range(ZS)] for y in range(YS) for c in range(CS)]
Y_GROUPS = [[device_at(y, z, c) for y in range(YS)] for z in range(ZS) for c in range(CS)]
PARTNER = [(i, i ^ 1) for i in range(YS * ZS * CS)]


def swap_cores(value):
    return lax.ppermute(value, "heads", PARTNER)


def exchange(value, groups):
    return lax.all_to_all(value, "heads", 0, 0, tiled=True, axis_index_groups=groups)


def spread(value, groups):
    count = len(groups[0])
    return exchange(jnp.broadcast_to(value[None], (count, *value.shape)), groups)


def gather_planes(piece):
    rows, width = piece.shape
    over_z = spread(piece, Z_GROUPS)
    over_y = spread(over_z, Y_GROUPS)
    own = over_y.reshape(YS * ZS, rows, width)
    return own, swap_cores(own)


VMEM = pl.BlockSpec(memory_space=pltpu.VMEM)
SMEM = pl.BlockSpec(memory_space=pltpu.SMEM)
HBM = pl.BlockSpec(memory_space=pl.ANY)


def limit(mib):
    return pltpu.CompilerParams(vmem_limit_bytes=mib * 1024 * 1024)


def silu(v):
    return v / (1.0 + jnp.exp(-v))


def softplus(v):
    e = jnp.exp(-jnp.abs(v))
    grown = 1.0 + e
    small = grown == 1.0
    log1p = jnp.where(small, e, jnp.log(grown) * (e / jnp.where(small, 1.0, grown - 1.0)))
    return jnp.maximum(v, 0.0) + log1p


def lookup_kernel(ids_ref, table_ref, out_ref, tail_ref, acc_ref):
    rows, vocab = table_ref.shape
    tokens = acc_ref.shape[1]
    whole = vocab // LANES
    tail_at = whole * LANES
    lane = lax.broadcasted_iota(jnp.int32, (rows, LANES), 1)
    tail_ref[...] = jnp.zeros_like(tail_ref)
    if tail_at < vocab:
        tail_ref[:, : vocab - tail_at] = table_ref[:, tail_at:].astype(F32)
    tail = tail_ref[...]
    for tile in range(tokens // LANES):

        def one(i, acc, tile=tile):
            token = ids_ref[0, tile * LANES + i]
            block = jnp.minimum(token // LANES, whole - 1)
            at = pl.multiple_of(block * LANES, LANES)
            found = table_ref[:, pl.ds(at, LANES)].astype(F32)
            found = jnp.where(token >= tail_at, tail, found)
            moved = pltpu.roll(found, (i - token % LANES + LANES) % LANES, 1)
            return jnp.where(lane == i, moved, acc)

        acc = lax.fori_loop(0, LANES, one, jnp.zeros((rows, LANES), F32), unroll=8)
        acc_ref[:, tile * LANES : (tile + 1) * LANES] = acc
    for j in range(rows // 8):
        out_ref[:, j * tokens : (j + 1) * tokens] = acc_ref[8 * j : 8 * j + 8, :].astype(BF)


def lookup(ids, table):
    rows = table.shape[0]
    tokens = ids.shape[1]
    return pl.pallas_call(
        lookup_kernel,
        out_shape=jax.ShapeDtypeStruct((8, rows // 8 * tokens), BF),
        in_specs=[SMEM, VMEM],
        out_specs=VMEM,
        scratch_shapes=[pltpu.VMEM((rows, LANES), F32), pltpu.VMEM((rows, tokens), F32)],
        compiler_params=limit(12),
        name="lookup",
    )(ids, table)


def tdot(a, b):
    return lax.dot_general(a, b, (((0,), (0,)), ((), ())), preferred_element_type=F32)


def ndot(a, b):
    return lax.dot_general(a, b, (((1,), (1,)), ((), ())), preferred_element_type=F32)


def mdot(a, b):
    return lax.dot_general(a, b, (((1,), (0,)), ((), ())), preferred_element_type=F32)


def make_layer_kernel(layer, tokens, seqs, draft, own_cols, taps, has_base):
    model = own_cols * YS * ZS * CS
    pieces = own_cols // 8
    kept = taps - 1
    stream_lanes = pieces * tokens

    def kernel(*refs):
        (
            core_ref, scalar_ref, own_ref, oth_ref, wown_ref, woth_ref, gain_ref, zx_ref,
            small_ref, cols_ref, statex_ref, statebc_ref, acc_col_ref, acc_row_ref, outw_ref,
            ssm_ref,
        ) = refs[:16]
        rest = refs[17:] if has_base else refs[16:]
        (
            keep_ref, send_ref, newx_ref, newbc_ref, newssm_ref,
            xs, nb, h_in, h_out, xw_all, sem_in, sem_out,
        ) = rest
        core = core_ref[0]
        first = core == 0
        bias_dt = scalar_ref[0, layer]
        rate = scalar_ref[1, layer]
        skip = scalar_ref[2, layer]
        load = pltpu.make_async_copy(ssm_ref.at[layer], h_in, sem_in)
        load.start()

        total = jnp.zeros((8, tokens), F32)
        for k in range(YS * ZS):
            for j in range(pieces):
                lanes = slice(j * tokens, (j + 1) * tokens)
                a = own_ref[k, :, lanes].astype(F32)
                b = oth_ref[k, :, lanes].astype(F32)
                total = total + a * a + b * b
                at = 2 * k * own_cols + 8 * j
                xs[at : at + 8, :] = jnp.where(first, a, b)
                xs[at + own_cols : at + own_cols + 8, :] = jnp.where(first, b, a)
        scale = lax.rsqrt(jnp.sum(total, axis=0, keepdims=True) / model + EPS)
        gains = jnp.transpose(gain_ref[...])
        for j in range(model // LANES):
            at = slice(j * LANES, (j + 1) * LANES)
            col = gains[:, layer * (model // LANES) + j :][:, :1]
            nb[at, :] = ((xs[at, :] * scale) * col).astype(BF)

        normed = nb[...]
        take_own = core == layer
        wl = wown_ref.shape[2] - (model + 2 * LANES)
        states = YS * ZS * 8 // 2

        def bc_rows(lo, hi):
            a = wown_ref[:, :, lo + wl : hi + wl].astype(F32)
            b = woth_ref[:, :, lo + wl : hi + wl].astype(F32)
            return jnp.where(take_own, a, b).reshape(2 * states, hi - lo)

        zx = tdot(zx_ref[layer], normed).astype(BF)
        bc = mdot(bc_rows(0, model).astype(BF), normed).astype(BF).astype(F32)
        mine = mdot(small_ref[layer], normed).astype(BF)
        width = zx.shape[0] // 2
        gate_z = zx[:width].astype(F32)
        values = zx[width:].astype(F32)
        cols = cols_ref[layer]

        lane = lax.broadcasted_iota(jnp.int32, (1, tokens), 1)
        t0 = lane % draft

        def saved_at(j):
            seq = lax.broadcasted_iota(jnp.int32, (seqs, tokens), 0)
            at = lax.broadcasted_iota(jnp.int32, (seqs, tokens), 1)
            return (at == seq * draft + (draft - kept) + j).astype(F32).astype(BF)

        places = [saved_at(j) for j in range(kept)]
        place = jnp.concatenate(places, axis=0)
        before_x = sum(tdot(statex_ref[layer, j], places[j]) for j in range(kept))
        extra = bc_rows(model, model + 2 * LANES)
        before_bc = mdot(extra[:, : kept * seqs].astype(BF), place)
        before_mine = mdot(statebc_ref[layer], place)

        def convolve(now, before, weights, bias):
            acc = None
            for k in range(taps):
                d = taps - 1 - k
                if d:
                    shifted = jnp.where(
                        t0 >= d,
                        pltpu.roll(now, d, 1),
                        pltpu.roll(before, tokens - (draft - d), 1),
                    )
                else:
                    shifted = now
                term = shifted * weights[k]
                acc = term if acc is None else acc + term
            return silu(acc + bias)

        xc = convolve(values, before_x, [cols[:, k : k + 1] for k in range(taps)], cols[:, taps : taps + 1])
        base = kept * seqs
        bcc = convolve(
            bc,
            before_bc,
            [extra[:, base + k : base + k + 1] for k in range(taps)],
            extra[:, base + taps : base + taps + 1],
        ).astype(BF)

        acc_col = acc_col_ref[...]
        seq = lax.broadcasted_iota(jnp.int32, (seqs, tokens), 0)
        at = lax.broadcasted_iota(jnp.int32, (seqs, tokens), 1)
        values_b, before_b = zx[width:], before_x.astype(BF)
        before_mb = before_mine.astype(BF)
        for i in range(kept):
            row = acc_col + i
            new = ((at == seq * draft + row - kept) & (row >= kept)).astype(F32).astype(BF)
            old = ((at == seq * draft + (draft - kept) + row) & (row < kept)).astype(F32).astype(BF)
            newx_ref[i] = (ndot(new, values_b) + ndot(old, before_b)).astype(BF)
            newbc_ref[i] = (ndot(mine, new) + ndot(before_mb, old)).astype(BF)

        step = softplus(mine[4:5, :].astype(F32) + bias_dt)
        cum = step
        for d in (1, 2, 4):
            cum = cum + jnp.where(t0 >= d, pltpu.roll(cum, d, 1), 0.0)
        accepted = acc_row_ref[...]
        cut = jnp.where(t0 < accepted, step, 0.0)
        for d in (1, 2, 4):
            cut = cut + jnp.where((t0 & d) != 0, pltpu.roll(cut, d, 1), pltpu.roll(cut, tokens - d, 1))
        weight = jnp.where(t0 < accepted, jnp.exp(-rate * (cut - cum)) * step, 0.0)
        fall = jnp.exp(-rate * cum)
        fall_cut = jnp.exp(-rate * cut)
        xb = xc.astype(BF)
        xw_all[...] = (xc * weight).astype(BF)
        load.wait()

        per_tile = LANES // draft
        sub = lax.broadcasted_iota(jnp.int32, (LANES, LANES), 0)
        lan = lax.broadcasted_iota(jnp.int32, (LANES, LANES), 1)
        causal = (sub // draft == lan // draft) & (sub <= lan)
        group = lax.broadcasted_iota(jnp.int32, (1, LANES), 1) // draft
        pick16 = lax.broadcasted_iota(jnp.int32, (per_tile, LANES), 0) * draft == (
            lax.broadcasted_iota(jnp.int32, (per_tile, LANES), 1)
        )
        parts = []
        for tile in range(tokens // LANES):
            ls = slice(tile * LANES, (tile + 1) * LANES)
            bmat = bcc[:states, ls]
            cmat = bcc[states:, ls]
            cum_r = jnp.broadcast_to(cum[:, ls], (LANES, LANES))
            step_c = jnp.transpose(jnp.broadcast_to(step[:, ls], (LANES, LANES)))
            cum_c = jnp.transpose(cum_r)
            gram = tdot(bmat, cmat)
            within = jnp.where(causal, gram * (jnp.exp(-rate * (cum_r - cum_c)) * step_c), 0.0)
            y_new = mdot(xb[:, ls], within.astype(BF))
            y_old = jnp.zeros((width, LANES), F32)
            falls = jnp.sum(jnp.where(pick16, fall_cut[:, ls], 0.0), axis=1, keepdims=True)
            xw = xw_all[:, ls]
            for s in range(per_tile):
                n = tile * per_tile + s
                h0 = h_in[n]
                here = group == s
                y_old = jnp.where(here, mdot(h0.astype(BF), cmat), y_old)
                add = ndot(jnp.where(here, xw, jnp.zeros_like(xw)), bmat)
                h_out[n] = h0 * falls[s : s + 1, :] + add
            parts.append(fall[:, ls] * y_old + y_new)
        store = pltpu.make_async_copy(h_out, newssm_ref.at[layer], sem_out)
        store.start()
        y = jnp.concatenate(parts, axis=1) + skip * xc
        gated = y * silu(gate_z)
        ssq = jnp.sum(gated * gated, axis=0, keepdims=True)
        u = (gated * cols[:, taps + 1 : taps + 2]).astype(BF)

        high = ssq.astype(BF)
        low = (ssq - high.astype(F32)).astype(BF)
        row8 = lax.broadcasted_iota(jnp.int32, (8, tokens), 0)
        tail = jnp.where(row8 == 0, high.astype(F32), jnp.where(row8 == 1, low.astype(F32), 0.0))
        block = own_cols * CS * ZS
        for y_at in range(YS):
            out = tdot(outw_ref[layer, :, y_at * block : (y_at + 1) * block], u)
            out = out.reshape(ZS, CS, pieces, 8, tokens)
            for z in range(ZS):
                even, odd = out[z, 0], out[z, 1]
                rows = slice(z * pieces, (z + 1) * pieces)
                keep_ref[y_at, rows] = jnp.where(first, even, odd)
                send_ref[y_at, rows] = jnp.where(first, odd, even).astype(BF)
            keep_ref[y_at, ZS * pieces] = tail
            send_ref[y_at, ZS * pieces] = tail.astype(BF)
        store.wait()

    return kernel


def add_cores_kernel(keep_ref, got_ref, out_ref):
    tiles = keep_ref.shape[1]
    for y in range(YS):
        out_ref[y, : tiles - 1] = (
            keep_ref[y, : tiles - 1] + got_ref[y, : tiles - 1].astype(F32)
        ).astype(BF)
    tail = keep_ref[0, tiles - 1] + got_ref[0, tiles - 1].astype(F32)
    for y in range(YS):
        out_ref[y, tiles - 1] = split_tail(tail)


def split_tail(tail):
    row8 = lax.broadcasted_iota(jnp.int32, tail.shape, 0)
    ssq = tail[0:1] + tail[1:2]
    high = ssq.astype(BF).astype(F32)
    return jnp.where(row8 == 0, high, jnp.where(row8 == 1, ssq - high, 0.0)).astype(BF)


def add_y_kernel(got_ref, out_ref):
    tiles = got_ref.shape[1]
    pieces = (tiles - 1) // ZS

    def summed(rows):
        acc = got_ref[0, rows].astype(F32)
        for y in range(1, YS):
            acc = acc + got_ref[y, rows].astype(F32)
        return acc

    tail = split_tail(summed(slice(tiles - 1, tiles))[0])
    for z in range(ZS):
        out_ref[z, :pieces] = summed(slice(z * pieces, (z + 1) * pieces)).astype(BF)
        out_ref[z, pieces] = tail


def make_finish_kernel(inner, last):
    def finish_kernel(got_ref, stream_ref, out_ref):
        tiles = got_ref.shape[1]
        tokens = got_ref.shape[3]
        acc = got_ref[0].astype(F32)
        for z in range(1, ZS):
            acc = acc + got_ref[z].astype(F32)
        ssq = acc[tiles - 1, 0:1] + acc[tiles - 1, 1:2]
        scale = lax.rsqrt(ssq / inner + EPS)
        for j in range(tiles - 1):
            lanes = slice(j * tokens, (j + 1) * tokens)
            new = (stream_ref[:, lanes].astype(F32) + acc[j] * scale).astype(BF)
            if last:
                out_ref[j] = new
            else:
                out_ref[:, lanes] = new

    return finish_kernel


def call(kernel, out_shape, count, name):
    return pl.pallas_call(
        kernel,
        out_shape=out_shape,
        in_specs=[VMEM] * count,
        out_specs=VMEM,
        compiler_params=limit(10),
        name=name,
    )


def local(
    draft_ids,
    accepted,
    embedding,
    norm_gain,
    w_zx,
    w_dt,
    w_bc,
    dt_bias,
    decay_rate,
    skip_weight,
    conv_x_w,
    conv_x_b,
    conv_bc_w,
    conv_bc_b,
    gate_gain,
    out_w,
    ssm_state,
    conv_x_state,
    conv_bc_state,
):
    seqs, draft = draft_ids.shape
    tokens = seqs * draft
    own_cols = embedding.shape[1]
    model = own_cols * YS * ZS * CS
    width = w_zx.shape[3] // 2
    inner = width * YS * ZS * CS
    bc_here = w_bc.shape[2]
    taps = conv_x_w.shape[1]
    kept = taps - 1
    pieces = own_cols // 8
    states = ssm_state.shape[4]
    core = lax.axis_index("heads") % CS

    w_rows = jnp.swapaxes(w_bc, 1, 2)
    state_rows = jnp.transpose(conv_bc_state, (0, 3, 2, 1)).reshape(LAYERS, bc_here, kept * seqs)
    tap_rows = jnp.swapaxes(conv_bc_w, 1, 2)
    room = 2 * LANES - kept * seqs - taps - 1
    bc_rows = jnp.concatenate(
        [w_rows, state_rows, tap_rows, conv_bc_b[:, :, None], jnp.zeros((LAYERS, bc_here, room), BF)],
        axis=2,
    )
    first = core == 0
    kept_rows = jnp.where(first, bc_rows[0], bc_rows[1])
    got_rows = swap_cores(jnp.where(first, bc_rows[1], bc_rows[0]))
    pair_rows = jnp.concatenate(
        [jnp.where(first, kept_rows, got_rows), jnp.where(first, got_rows, kept_rows)], axis=0
    )

    small = jnp.concatenate(
        [w_rows, jnp.swapaxes(w_dt, 1, 2), jnp.zeros((LAYERS, 7 - bc_here, model), BF)], axis=1
    )
    state_own = jnp.pad(state_rows, ((0, 0), (0, 8 - bc_here), (0, 0)))
    cols = jnp.stack(
        [conv_x_w[:, k].astype(F32) for k in range(taps)]
        + [conv_x_b.astype(F32), gate_gain]
        + [jnp.zeros_like(gate_gain)] * (6 - taps),
        axis=2,
    )
    gains = jnp.pad(norm_gain.reshape(-1, LANES), ((0, LANES - LAYERS * model // LANES), (0, 0)))
    scalars = jnp.stack([dt_bias[:, 0], decay_rate[:, 0], skip_weight[:, 0]])
    acc_col = accepted[:, None]
    acc_row = jnp.repeat(accepted, draft)[None]
    state_x = jnp.swapaxes(conv_x_state, 1, 2)
    states_in = ssm_state.reshape(LAYERS, seqs, width, states)
    zx_w = w_zx.reshape(LAYERS, model, 2 * width)

    stream = lookup(draft_ids.reshape(1, tokens), embedding.T)
    own, oth = gather_planes(jnp.concatenate([stream, pair_rows], axis=1))
    w_own, w_oth = own, oth
    new_ssm = None
    new_x, new_bc = [], []
    tiles = ZS * pieces + 1
    for layer in range(LAYERS):
        args = [
            core.reshape(1), scalars, own, oth, w_own, w_oth, gains, zx_w,
            small, cols, state_x, state_own, acc_col, acc_row, out_w, states_in,
        ]
        specs = [SMEM, SMEM] + [VMEM] * 13 + [HBM]
        aliases = {}
        if new_ssm is not None:
            args.append(new_ssm)
            specs.append(HBM)
            aliases = {16: 4}
        keep, send, x_rows, bc_kept, new_ssm = pl.pallas_call(
            make_layer_kernel(layer, tokens, seqs, draft, own_cols, taps, new_ssm is not None),
            out_shape=(
                jax.ShapeDtypeStruct((YS, tiles, 8, tokens), F32),
                jax.ShapeDtypeStruct((YS, tiles, 8, tokens), BF),
                jax.ShapeDtypeStruct((kept, seqs, width), BF),
                jax.ShapeDtypeStruct((kept, 8, seqs), BF),
                jax.ShapeDtypeStruct(states_in.shape, F32),
            ),
            in_specs=specs,
            out_specs=(VMEM, VMEM, VMEM, VMEM, HBM),
            scratch_shapes=[
                pltpu.VMEM((model, tokens), F32),
                pltpu.VMEM((model, tokens), BF),
                pltpu.VMEM(states_in.shape[1:], F32),
                pltpu.VMEM(states_in.shape[1:], F32),
                pltpu.VMEM((width, tokens), BF),
                pltpu.SemaphoreType.DMA,
                pltpu.SemaphoreType.DMA,
            ],
            input_output_aliases=aliases,
            compiler_params=limit(34),
            name=f"layer_{layer}",
        )(*args)
        new_x.append(x_rows)
        new_bc.append(bc_kept[:, :bc_here])
        summed = call(
            add_cores_kernel, jax.ShapeDtypeStruct((YS, tiles, 8, tokens), BF), 2, "add_cores"
        )(keep, swap_cores(send))
        summed = call(
            add_y_kernel, jax.ShapeDtypeStruct((ZS, pieces + 1, 8, tokens), BF), 1, "add_y"
        )(exchange(summed, Y_GROUPS))
        last = layer + 1 == LAYERS
        shape = (pieces, 8, tokens) if last else (8, pieces * tokens)
        stream = call(
            make_finish_kernel(inner, last), jax.ShapeDtypeStruct(shape, BF), 2, "finish"
        )(exchange(summed, Z_GROUPS), stream)
        if not last:
            own, oth = gather_planes(stream)
    hidden = stream.reshape(own_cols, tokens).T
    kept_x = jnp.swapaxes(jnp.stack(new_x), 1, 2)
    kept_bc = jnp.transpose(jnp.stack(new_bc), (0, 3, 1, 2))
    return (hidden, new_ssm.reshape(ssm_state.shape), kept_x, kept_bc)


def solution(mesh):
    placed = (
        P("batch", None),
        P("batch"),
        P(None, "heads"),
        P(),
        P(None, None, "heads", None),
        P(None, None, "heads"),
        P(None, None, "heads"),
        P(None, "heads"),
        P(None, "heads"),
        P(None, "heads"),
        P(None, None, "heads"),
        P(None, "heads"),
        P(None, None, "heads"),
        P(None, "heads"),
        P(None, "heads"),
        P(None, "heads", None),
        P(None, "batch", "heads", None, None),
        P(None, "batch", None, "heads"),
        P(None, "batch", None, "heads"),
    )
    return jax.shard_map(
        local,
        mesh=mesh,
        in_specs=placed,
        out_specs=(
            P("batch", "heads"),
            P(None, "batch", "heads", None, None),
            P(None, "batch", None, "heads"),
            P(None, "batch", None, "heads"),
        ),
        check_vma=False,
    )
```

time: 603 us -> 209 us (0.35)
  waiting for transfers between devices: 156 us -> 17.9 us
  blocking collectives: 255 us -> 140 us
  other arithmetic: 84.4 us -> 2.86 us
  local copies, waits for them, and re-layouts: 64.7 us -> 15.1 us
  Pallas kernels: 0 us -> 26.5 us
  between operations: 15.2 us -> 1.01 us
  matrix products: 13.8 us -> 0 us
  starting transfers between devices: 12.6 us -> 4.33 us
    psum x2 -> x0, blocking collectives: 255 us -> none  [local(): total, ssq = lax.psum((term, local_sq), 'heads')]
    all_to_all x0 -> x7, blocking collectives: none -> 140 us  [exchange(): lax.all_to_all(value, 'heads', 0, 0, tiled=True, axis_index_groups=groups)]
    psum x2 -> x0, waiting for transfers between devices: 85.4 us -> none  [local(): total, ssq = lax.psum((term, local_sq), 'heads')]
    all_to_all x1, waiting for transfers between devices: 43.7 us -> 10.6 us  [exchange(): lax.all_to_all(value, 'heads', 0, 0, tiled=True, axis_index_groups=groups)]
    all_gather x1 -> x0, waiting for transfers between devices: 26.6 us -> none  [turned_gather(): filled = lax.all_gather(both, axis, axis=0, tiled=True)]
    pallas_call x0 -> x9, Pallas kernels: none -> 26.5 us  [the longest x2 16.5 us: local(): pl.pallas_call(make_layer_kernel(layer, tokens, seqs, draft, own_cols, ta...]
    select_n x5 -> x2, other arithmetic: 21.6 us -> 0.05 us  [the longest x1 0.03 us: local(): jnp.where(first, kept_rows, got_rows)]
    reduce_sum x8 -> x0, other arithmetic: 18.2 us -> none  [the longest x4 10.7 us: recur(): jnp.sum(state * cmat[:, t, None, :], axis=-1) + skip * values[:, t]]
  transfers between devices with their start and end apart: 4 -> 6, of which waited for: 4 -> 4; matrix products, arithmetic and copies ran while one was open for 10% -> 4% of each run, Pallas kernels for 0% -> 4%
where the time goes in v1:
time: 209 us; the launch traced here: 208 us
  blocking collectives  140 us (67%)
  Pallas kernels  26.5 us (13%)
  waiting for transfers between devices  17.9 us (9%)
  local copies, waits for them, and re-layouts  15.1 us (7%)
  starting transfers between devices  4.33 us (2%)
  other arithmetic  2.86 us (1%)
    all_to_all x7, blocking collectives, exchange(): lax.all_to_all(value, 'heads', 0, 0, tiled=True, axis_index_groups=groups)  140 us
    pallas_call x2, Pallas kernels, local(): pl.pallas_call(make_layer_kernel(layer, tokens, seqs, draft, own_cols, ta...  16.5 us
    all_to_all x1, waiting for transfers between devices, exchange(): lax.all_to_all(value, 'heads', 0, 0, tiled=True, axis_index_groups=groups)  10.6 us
    pallas_call x1, Pallas kernels, lookup(): pl.pallas_call(lookup_kernel, out_shape=jax.ShapeDtypeStruct((8, rows //...  7.78 us
    ppermute x5, waiting for transfers between devices, swap_cores(): return lax.ppermute(value, 'heads', PARTNER)  7.26 us
    unnamed x28, local copies, waits for them, and re-layouts  6.96 us
  transfers between devices with their start and end apart: 6, of which 4 were waited for; matrix products, arithmetic and copies ran while one was open for 4% of the time, Pallas kernels for 4%

profile of v1, /device:TPU:2, one launch (start us, length us, event | category | flops | bytes accessed | tf_op | source)
XLA Modules:
  0.0 207.9 jit_solution(16062722269657396113)
XLA Ops:
  0.6 0.8 copy.69
  1.4 0.8 copy.70
  2.2 0.7 copy.68
  2.9 0.1 reshape.97
  3.0 0.9 concatenate.12
  3.9 0.1 collective-permute-start
  4.0 0.8 copy.67
  4.7 0.1 reshape.96.ids_ref
  4.8 2.1 %copy-done.2 = bf16[50280,40]{0,1:T(8,128)(2,1)S(1)} copy-done((bf16[50280,40]{0,1:T(8,128)(2,1)S(1)}, bf16[50280,40]{0,1:T(8,128)(2,1)}, u32[]{:S(2)}) %copy-start.2) | copy-done | bytes 4022424
  7.0 7.8 %lookup.1.stream_ref = bf16[8,1920]{1,0:T(8,128)(2,1)S(1)} custom-call(s32[1,384]{1,0:T(1,128)S(1)} %reshape.96.ids_ref, bf16[40,50280]{1,0:T(8,128)(2,1)S(1)} %bitcast.53), custom_call_target="tpu_custom_call" | custom-call | tf_op jit(solution)/shard_map/lookup/pallas_call | solution.py:98
  14.9 28.2 %all_to_all.40 = bf16[8,8,4736]{2,1,0:T(8,128)(2,1)S(1)} all-to-all(bf16[8,8,4736]{2,1,0:T(8,128)(2,1)S(1)} %broadcast_in_dim.20), channel_id=1, replica_groups={{0,2,4,6,8,10,12,14},{1,3,5,7,9,11,13,15},{16,18,20,22,24,26,28,30},{17..., dimensions={0} | all-to-all | bytes 1212416 | tf_op jit(solution)/shard_map/all_to_all | solution.py:31
  43.1 0.2 broadcast_in_dim.42
  43.4 34.4 %all_to_all.41 = bf16[4,8,8,4736]{3,2,1,0:T(8,128)(2,1)S(1)} all-to-all(bf16[4,8,8,4736]{3,2,1,0:T(8,128)(2,1)S(1)} %broadcast_in_dim.42), channel_id=1, replica_groups={{0,16,32,48},{1,17,33,49},{2,18,34,50},{3,19,35,51},{4,20,36,52},{5,21,..., dimensions={0} | all-to-all | bytes 4849664 | tf_op jit(solution)/shard_map/all_to_all | solution.py:31
  77.9 0.1 copy.78.refs_12_
  78.1 0.1 broadcast_in_dim_reshape.3.refs_13_
  78.2 0.1 copy.73
  78.3 0.1 copy.75
  78.4 0.7 copy.76
  79.2 0.7 copy.72
  79.9 0.7 copy.74
  80.6 0.7 copy.77
  81.5 0.6 stack.44
  82.1 1.1 stack.45.refs_9_
  83.2 0.7 pad_maximum_fusion.refs_1_
  83.9 0.9 maximum_maximum_fusion.refs_8_
  84.8 1.9 copy-done
  86.7 1.3 copy-done.1
  88.0 8.6 %layer_0.1 = (f32[4,41,8,384]{3,2,1,0:T(8,128)S(1)}, bf16[4,41,8,384]{3,2,1,0:T(8,128)(2,1)S(1)}, bf16[3,48,64]{2,1,0:T(8,128)(2,1)S(1)}, bf16[3,8,48]{2,1,0:T(8,128)(2,1)S(1)}, f32[2,48,64,128]{3,2,1,0:T(8,128)}) custom-call(s32[1]{0:T(128)} %bitcast.refs_0_, f32[3,2]{1,0:T(4,128)S(1)} %pad_maximum_fusion.refs_1_, bf16[32,8,4736]{2,1,0:T(8,128)(2,1)S(1)} %bitcast.46, ...), custom_call_target="tpu_custom_call" | custom-call | tf_op jit(solution)/shard_map/layer_0/pallas_call | solution.py:454
  96.7 0.6 collective-permute-start.2
  97.2 2.2 %collective-permute-done.2.got_ref = bf16[4,41,8,384]{3,2,1,0:T(8,128)(2,1)S(1)} collective-permute-done((bf16[4,41,8,384]{3,2,1,0:T(8,128)(2,1)S(1)}, bf16[4,41,8,384]{3,2,1,0:T(8,128)(2,1)S(1)}, u32[]{:S(2)}, u32[]{:S(2)}) %collective-permute-start.2) | collective-permute-done | bytes 1007648 | tf_op jit(solution)/shard_map/ppermute | solution.py:27
  99.5 0.2 add_cores.2
  99.7 17.9 %all_to_all.42.got_ref = bf16[4,41,8,384]{3,2,1,0:T(8,128)(2,1)S(1)} all-to-all(bf16[4,41,8,384]{3,2,1,0:T(8,128)(2,1)S(1)} %add_cores.2), channel_id=1, replica_groups={{0,16,32,48},{1,17,33,49},{2,18,34,50},{3,19,35,51},{4,20,36,52},{5,21,..., dimensions={0} | all-to-all | bytes 2015232 | tf_op jit(solution)/shard_map/all_to_all | solution.py:31
  117.6 0.1 add_y.2
  117.7 14.9 %all_to_all.43.got_ref = bf16[8,6,8,384]{3,2,1,0:T(8,128)(2,1)S(1)} all-to-all(bf16[8,6,8,384]{3,2,1,0:T(8,128)(2,1)S(1)} %add_y.2), channel_id=1, replica_groups={{0,2,4,6,8,10,12,14},{1,3,5,7,9,11,13,15},{16,18,20,22,24,26,28,30},{17..., dimensions={0} | all-to-all | bytes 589824 | tf_op jit(solution)/shard_map/all_to_all | solution.py:31
  132.7 12.9 %all_to_all.44 = bf16[8,8,1920]{2,1,0:T(8,128)(2,1)S(1)} all-to-all(bf16[8,8,1920]{2,1,0:T(8,128)(2,1)S(1)} %broadcast_in_dim.46), channel_id=1, replica_groups={{0,2,4,6,8,10,12,14},{1,3,5,7,9,11,13,15},{16,18,20,22,24,26,28,30},{17..., dimensions={0} | all-to-all | bytes 491520 | tf_op jit(solution)/shard_map/all_to_all | solution.py:31
  145.7 14.3 %all_to_all.45 = bf16[4,8,8,1920]{3,2,1,0:T(8,128)(2,1)S(1)} all-to-all(bf16[4,8,8,1920]{3,2,1,0:T(8,128)(2,1)S(1)} %broadcast_in_dim.47), channel_id=1, replica_groups={{0,16,32,48},{1,17,33,49},{2,18,34,50},{3,19,35,51},{4,20,36,52},{5,21,..., dimensions={0} | all-to-all | bytes 1966080 | tf_op jit(solution)/shard_map/all_to_all | solution.py:31
  160.0 2.6 %collective-permute-done.3.refs_3_ = bf16[32,8,1920]{2,1,0:T(8,128)(2,1)S(1)} collective-permute-done((bf16[32,8,1920]{2,1,0:T(8,128)(2,1)S(1)}, bf16[32,8,1920]{2,1,0:T(8,128)(2,1)S(1)}, u32[]{:S(2)}, u32[]{:S(2)}) %collective-permute-start.3) | collective-permute-done | bytes 983072 | tf_op jit(solution)/shard_map/ppermute | solution.py:27
  162.5 7.9 %layer_1.1 = (f32[4,41,8,384]{3,2,1,0:T(8,128)S(1)}, bf16[4,41,8,384]{3,2,1,0:T(8,128)(2,1)S(1)}, bf16[3,48,64]{2,1,0:T(8,128)(2,1)S(1)}, bf16[3,8,48]{2,1,0:T(8,128)(2,1)S(1)}, f32[2,48,64,128]{3,2,1,0:T(8,128)}) custom-call(s32[1]{0:T(128)} %bitcast.refs_0_, f32[3,2]{1,0:T(4,128)S(1)} %pad_maximum_fusion.refs_1_, ...), custom_call_target="tpu_custom_call", output_to_operand_aliasing={{4}: (16, {})} | custom-call | tf_op jit(solution)/shard_map/layer_1/pallas_call | solution.py:454
  170.4 0.2 collective-permute-start.4
  170.7 2.5 %collective-permute-done.4.got_ref = bf16[4,41,8,384]{3,2,1,0:T(8,128)(2,1)S(1)} collective-permute-done((bf16[4,41,8,384]{3,2,1,0:T(8,128)(2,1)S(1)}, bf16[4,41,8,384]{3,2,1,0:T(8,128)(2,1)S(1)}, u32[]{:S(2)}, u32[]{:S(2)}) %collective-permute-start.4) | collective-permute-done | bytes 1007648 | tf_op jit(solution)/shard_map/ppermute | solution.py:27
  173.1 0.2 add_cores.3
  173.4 17.6 %all_to_all.46.got_ref = bf16[4,41,8,384]{3,2,1,0:T(8,128)(2,1)S(1)} all-to-all(bf16[4,41,8,384]{3,2,1,0:T(8,128)(2,1)S(1)} %add_cores.3), channel_id=1, replica_groups={{0,16,32,48},{1,17,33,49},{2,18,34,50},{3,19,35,51},{4,20,36,52},{5,21,..., dimensions={0} | all-to-all | bytes 2015232 | tf_op jit(solution)/shard_map/all_to_all | solution.py:31
  191.0 0.8 add_y.3
  191.9 3.4 %all-to-all-start.7 = ((bf16[8,6,8,384]{3,2,1,0:T(8,128)(2,1)}), bf16[8,6,8,384]{3,2,1,0:T(8,128)(2,1)S(1)}, u32[]{:S(2)}, u32[]{:S(2)}) async-start(bf16[8,6,8,384]{3,2,1,0:T(8,128)(2,1)} %add_y.3), calls=%async_computation.7 | async-start | bytes 589824 | tf_op jit(solution)/shard_map/all_to_all | solution.py:31
  195.3 0.6 maximum_bitcast_fusion.1
  195.9 0.6 maximum_bitcast_fusion
  196.6 10.6 %all-to-all-done.7.got_ref = bf16[8,6,8,384]{3,2,1,0:T(8,128)(2,1)S(1)} async-done(((bf16[8,6,8,384]{3,2,1,0:T(8,128)(2,1)}), bf16[8,6,8,384]{3,2,1,0:T(8,128)(2,1)S(1)}, u32[]{:S(2)}, u32[]{:S(2)}) %all-to-all-start.7) | async-done | bytes 294944 | tf_op jit(solution)/shard_map/all_to_all | solution.py:31
  207.2 0.7 finish.3
  (46 shorter events, 0.6 us)
Async XLA Ops:
  3.9 10.9 %collective-permute-start = (bf16[4,2816]{1,0:T(4,128)(2,1)S(1)}, bf16[4,2816]{1,0:T(4,128)(2,1)S(1)}, u32[]{:S(2)}, u32[]{:S(2)}) collective-permute-start(bf16[4,2816]{1,0:T(4,128)(2,1)S(1)} %select_bitcast_fusion), channel_id=1, source_target_pairs={{0,1},{1,0},{2,3},{3,2},{4,5},{5,4},{6,7},{7,6},{8,9},{9,8},{10,11... | collective-permute-start | bytes 67592 | tf_op jit(solution)/shard_map/ppermute | solution.py:27
  4.8 2.1 %copy-start.2 = (bf16[50280,40]{0,1:T(8,128)(2,1)S(1)}, bf16[50280,40]{0,1:T(8,128)(2,1)}, u32[]{:S(2)}) copy-start(bf16[50280,40]{0,1:T(8,128)(2,1)} %param.21) | copy-start | bytes 12067204
  43.2 34.6 %copy-start.5 = (f32[2,2560]{1,0:T(2,128)S(1)}, f32[2,2560]{1,0:T(2,128)}, u32[]{:S(2)}) copy-start(f32[2,2560]{1,0:T(2,128)} %param.22) | copy-start | bytes 61444
  43.2 34.6 %copy-start.6 = (bf16[2,2560,1]{1,0,2:T(2,128)(2,1)S(1)}, bf16[2,2560,1]{1,0,2:T(2,128)(2,1)}, u32[]{:S(2)}) copy-start(bf16[2,2560,1]{1,0,2:T(2,128)(2,1)} %param.24) | copy-start | bytes 30724
  43.3 34.6 %copy-start.8 = (s32[48]{0:T(128)S(1)}, s32[48]{0:T(128)}, u32[]{:S(2)}) copy-start(s32[48]{0:T(128)} %param.20) | copy-start | bytes 580
  43.3 34.9 %copy-start.7 = (bf16[2,4,64]{2,1,0:T(4,128)(2,1)S(1)}, bf16[2,4,64]{2,1,0:T(4,128)(2,1)}, u32[]{:S(2)}) copy-start(bf16[2,4,64]{2,1,0:T(4,128)(2,1)} %param.29) | copy-start | bytes 3076
  43.3 35.1 %copy-start.12 = (bf16[2,64]{1,0:T(2,128)(2,1)S(1)}, bf16[2,64]{1,0:T(2,128)(2,1)}, u32[]{:S(2)}) copy-start(bf16[2,64]{1,0:T(2,128)(2,1)} %param.30) | copy-start | bytes 772
  43.3 37.4 %copy-start.9 = (f32[2,64]{1,0:T(2,128)S(1)}, f32[2,64]{1,0:T(2,128)}, u32[]{:S(2)}) copy-start(f32[2,64]{1,0:T(2,128)} %param.33) | copy-start | bytes 1540
  43.3 39.9 %copy-start.10 = (f32[2,1]{0,1:T(1,128)S(1)}, f32[2,1]{0,1:T(1,128)}, u32[]{:S(2)}) copy-start(f32[2,1]{0,1:T(1,128)} %param.28) | copy-start | bytes 28
  43.3 39.9 %copy-start.11 = (f32[2,1]{0,1:T(1,128)S(1)}, f32[2,1]{0,1:T(1,128)}, u32[]{:S(2)}) copy-start(f32[2,1]{0,1:T(1,128)} %param.27) | copy-start | bytes 28
  43.3 41.5 %copy-start.3 = (bf16[2,64,2560]{2,1,0:T(8,128)(2,1)S(1)}, bf16[2,64,2560]{2,1,0:T(8,128)(2,1)}, u32[]{:S(2)}) copy-start(bf16[2,64,2560]{2,1,0:T(8,128)(2,1)} %refs_14_.3) | copy-start | bytes 1966084
  43.3 41.5 %copy-start.4 = (bf16[2,48,3,64]{3,1,2,0:T(8,128)(2,1)S(1)}, bf16[2,48,3,64]{3,1,2,0:T(8,128)(2,1)}, u32[]{:S(2)}) copy-start(bf16[2,48,3,64]{3,1,2,0:T(8,128)(2,1)} %param.36) | copy-start | bytes 110596
  77.8 7.0 %collective-permute-start.1 = (bf16[32,8,4736]{2,1,0:T(8,128)(2,1)S(1)}, bf16[32,8,4736]{2,1,0:T(8,128)(2,1)}, u32[]{:S(2)}, u32[]{:S(2)}) collective-permute-start(bf16[32,8,4736]{2,1,0:T(8,128)(2,1)S(1)} %bitcast.45), channel_id=1, source_target_pairs={{0,1},{1,0},{2,3},{3,2},{4,5},{5,4},{6,7},{7,6},{8,9},{9,8},{10,11... | collective-permute-start | bytes 7274504 | tf_op jit(solution)/shard_map/ppermute | solution.py:27
  84.8 1.9 copy-start
  86.7 1.3 copy-start.1
  96.7 2.8 %collective-permute-start.2 = (bf16[4,41,8,384]{3,2,1,0:T(8,128)(2,1)S(1)}, bf16[4,41,8,384]{3,2,1,0:T(8,128)(2,1)S(1)}, u32[]{:S(2)}, u32[]{:S(2)}) collective-permute-start(bf16[4,41,8,384]{3,2,1,0:T(8,128)(2,1)S(1)} %get-tuple-element.15), channel_id=1, source_target_pairs={{0,1},{1,0},{2,3},{3,2},{4,5},{5,4},{6,7},{7,6},{8,9},{9,8},{10,11... | collective-permute-start | bytes 3022856 | tf_op jit(solution)/shard_map/ppermute | solution.py:27
  160.0 2.6 %collective-permute-start.3 = (bf16[32,8,1920]{2,1,0:T(8,128)(2,1)S(1)}, bf16[32,8,1920]{2,1,0:T(8,128)(2,1)S(1)}, u32[]{:S(2)}, u32[]{:S(2)}) collective-permute-start(bf16[32,8,1920]{2,1,0:T(8,128)(2,1)S(1)} %bitcast.54), channel_id=1, source_target_pairs={{0,1},{1,0},{2,3},{3,2},{4,5},{5,4},{6,7},{7,6},{8,9},{9,8},{10,11... | collective-permute-start | bytes 2949128 | tf_op jit(solution)/shard_map/ppermute | solution.py:27
  170.4 2.7 %collective-permute-start.4 = (bf16[4,41,8,384]{3,2,1,0:T(8,128)(2,1)S(1)}, bf16[4,41,8,384]{3,2,1,0:T(8,128)(2,1)S(1)}, u32[]{:S(2)}, u32[]{:S(2)}) collective-permute-start(bf16[4,41,8,384]{3,2,1,0:T(8,128)(2,1)S(1)} %get-tuple-element.18), channel_id=1, source_target_pairs={{0,1},{1,0},{2,3},{3,2},{4,5},{5,4},{6,7},{7,6},{8,9},{9,8},{10,11... | collective-permute-start | bytes 3022856 | tf_op jit(solution)/shard_map/ppermute | solution.py:27
  191.9 15.4 %all-to-all-start.7 = ((bf16[8,6,8,384]{3,2,1,0:T(8,128)(2,1)}), bf16[8,6,8,384]{3,2,1,0:T(8,128)(2,1)S(1)}, u32[]{:S(2)}, u32[]{:S(2)}) async-start(bf16[8,6,8,384]{3,2,1,0:T(8,128)(2,1)} %add_y.3), calls=%async_computation.7 | async-start | bytes 589824 | tf_op jit(solution)/shard_map/all_to_all | solution.py:31

commit v2 on v1

v2 whole, which is shorter than its diff:
```python
import jax
import jax.numpy as jnp
from jax import lax
from jax.experimental import pallas as pl
from jax.experimental.pallas import tpu as pltpu
from jax.sharding import PartitionSpec as P


LAYERS = 2
EPS = 1e-05
BF = jnp.bfloat16
F32 = jnp.float32
LANES = 128

YS, ZS, CS = 4, 8, 2
XS = 4


def device_at(y, z, c):
    return (y * ZS + z) * CS + c


Z_GROUPS = [[device_at(y, z, c) for z in range(ZS)] for y in range(YS) for c in range(CS)]
Y_GROUPS = [[device_at(y, z, c) for y in range(YS)] for z in range(ZS) for c in range(CS)]
PARTNER = [(i, i ^ 1) for i in range(YS * ZS * CS)]


PLACES = [(x, y, z, c) for x in range(XS) for y in range(YS) for z in range(ZS) for c in range(CS)]


def index_of(x, y, z, c):
    return x * YS * ZS * CS + device_at(y % YS, z % ZS, c)


def fetch(value, source):
    pairs = [(index_of(*source(*place)), index_of(*place)) for place in PLACES]
    return lax.ppermute(value, ("batch", "heads"), pairs)


def swap_cores(value):
    return lax.ppermute(value, "heads", PARTNER)


def exchange(value, groups):
    return lax.all_to_all(value, "heads", 0, 0, tiled=True, axis_index_groups=groups)


def spread(value, groups):
    count = len(groups[0])
    return exchange(jnp.broadcast_to(value[None], (count, *value.shape)), groups)


def gather_planes(piece):
    rows, width = piece.shape
    over_z = spread(piece, Z_GROUPS)
    over_y = spread(over_z, Y_GROUPS)
    own = over_y.reshape(YS * ZS, rows, width)
    return own, swap_cores(own)


VMEM = pl.BlockSpec(memory_space=pltpu.VMEM)
SMEM = pl.BlockSpec(memory_space=pltpu.SMEM)
HBM = pl.BlockSpec(memory_space=pltpu.HBM)


def limit(mib):
    return pltpu.CompilerParams(vmem_limit_bytes=mib * 1024 * 1024)


def silu(v):
    return v / (1.0 + jnp.exp(-v))


def softplus(v):
    e = jnp.exp(-jnp.abs(v))
    grown = 1.0 + e
    small = grown == 1.0
    log1p = jnp.where(small, e, jnp.log(grown) * (e / jnp.where(small, 1.0, grown - 1.0)))
    return jnp.maximum(v, 0.0) + log1p


SHIFT = LANES.bit_length() - 1


def position():
    at = lax.axis_index("heads")
    return lax.axis_index("batch"), at // (ZS * CS), at // CS % ZS, at % CS


def lookup_kernel(ids_ref, table_ref, beside_ref, out_ref, tail_ref, acc_ref):
    rows, vocab = table_ref.shape
    draft = ids_ref.shape[0]
    tokens = acc_ref.shape[1]
    whole = vocab // LANES
    tail_at = whole * LANES
    lane = lax.broadcasted_iota(jnp.int32, (rows, LANES), 1)
    tail_ref[...] = jnp.zeros_like(tail_ref)
    if tail_at < vocab:
        tail_ref[:, : vocab - tail_at] = table_ref[:, tail_at:].astype(F32)
    tail = tail_ref[...]
    seqs_a_tile = LANES // draft
    for tile in range(tokens // LANES):

        def one(s, acc, tile=tile):
            for t in range(draft):
                token = ids_ref[t, tile * seqs_a_tile + s]
                i = s * draft + t
                block = jnp.minimum(token >> SHIFT, whole - 1)
                at = pl.multiple_of(block << SHIFT, LANES)
                found = table_ref[:, pl.ds(at, LANES)].astype(F32)
                found = jnp.where(token >= tail_at, tail, found)
                moved = pltpu.roll(found, (i - token) & (LANES - 1), 1)
                acc = jnp.where(lane == i, moved, acc)
            return acc

        acc = lax.fori_loop(0, seqs_a_tile, one, jnp.zeros((rows, LANES), F32), unroll=2)
        acc_ref[:, tile * LANES : (tile + 1) * LANES] = acc
    for j in range(rows // 8):
        out_ref[:, j * tokens : (j + 1) * tokens] = acc_ref[8 * j : 8 * j + 8, :].astype(BF)
    out_ref[:, rows // 8 * tokens :] = beside_ref[...]


def lookup(ids, table, beside):
    rows = table.shape[0]
    tokens = ids.size
    return pl.pallas_call(
        lookup_kernel,
        out_shape=jax.ShapeDtypeStruct((8, rows // 8 * tokens + beside.shape[1]), BF),
        in_specs=[SMEM, VMEM, VMEM],
        out_specs=VMEM,
        scratch_shapes=[pltpu.VMEM((rows, LANES), F32), pltpu.VMEM((rows, tokens), F32)],
        compiler_params=limit(12),
        name="lookup",
    )(ids, table, beside)


def tdot(a, b):
    return lax.dot_general(a, b, (((0,), (0,)), ((), ())), preferred_element_type=F32)


def ndot(a, b):
    return lax.dot_general(a, b, (((1,), (1,)), ((), ())), preferred_element_type=F32)


def mdot(a, b):
    return lax.dot_general(a, b, (((1,), (0,)), ((), ())), preferred_element_type=F32)


SLOT = 64
AT_TAPS, AT_ACCEPTED, AT_BIAS, AT_RATE, AT_SKIP = 24, 32, 33, 34, 35


def saved_at(j, kept, seqs, draft):
    seq = lax.broadcasted_iota(jnp.int32, (seqs, seqs * draft), 0)
    at = lax.broadcasted_iota(jnp.int32, (seqs, seqs * draft), 1)
    return (at == seq * draft + (draft - kept) + j).astype(F32).astype(BF)


def setup_kernel(
    bias_ref, rate_ref, skip_ref, w_ref, wdt_ref, state_ref, taps_ref, tapb_ref, gain_ref,
    xtaps_ref, xtapb_ref, gate_ref, statex_ref, accepted_ref,
    keep_ref, send_ref, table_ref, own8_ref, beforex_ref, beforebc_ref, spread_ref, table,
):
    model = w_ref.shape[2]
    here = w_ref.shape[1]
    kept, seqs = state_ref.shape[1], state_ref.shape[3]
    draft = spread_ref.shape[1] // seqs
    taps = taps_ref.shape[1]
    width = xtaps_ref.shape[2]
    first = position()[3] == 0
    places = [saved_at(j, kept, seqs, draft) for j in range(kept)]
    outs, rows = [], []
    for layer in range(LAYERS):
        table[...] = jnp.zeros_like(table)
        table[0:taps, 0:here] = taps_ref[layer].astype(F32)
        table[taps : taps + 1, 0:here] = tapb_ref[layer : layer + 1].astype(F32)
        turned = jnp.transpose(table[...])[:8]
        tiles = []
        for j in range(kept):
            table[...] = jnp.zeros_like(table)
            table[0:here, 0:seqs] = state_ref[layer, j].astype(F32)
            tiles.append(table[0:8, :])
        outs.append((turned, tiles[0] + pltpu.roll(tiles[1], SLOT, 1), tiles[2]))
        row = w_ref[layer].astype(F32)
        rows.append(jnp.concatenate([row, jnp.zeros((8 - here, model), F32)], axis=0))
        own8_ref[layer] = jnp.concatenate(
            [row, wdt_ref[layer : layer + 1, :].astype(F32), jnp.zeros((7 - here, model), F32)], axis=0
        ).astype(BF)
    for ref, pick in ((keep_ref, first), (send_ref, jnp.logical_not(first))):
        for lo, values in (
            (0, rows),
            (model, [o[0] for o in outs]),
            (model + LANES, [o[1] for o in outs]),
            (model + 2 * LANES, [o[2] for o in outs]),
        ):
            value = jnp.where(pick, values[0], values[1])
            value = jnp.where(first, value, pltpu.roll(value, here, 0))
            ref[:, lo : lo + value.shape[1]] = value.astype(BF)
    for layer in range(LAYERS):
        table[...] = jnp.zeros_like(table)
        for j in range(model // LANES):
            table[j : j + 1, :] = gain_ref[layer : layer + 1, j * LANES : (j + 1) * LANES]
        table[AT_TAPS : AT_TAPS + taps, :width] = xtaps_ref[layer].astype(F32)
        table[AT_TAPS + taps : AT_TAPS + taps + 1, :width] = xtapb_ref[layer : layer + 1].astype(F32)
        table[AT_TAPS + taps + 1 : AT_TAPS + taps + 2, :width] = gate_ref[layer : layer + 1]
        table[AT_ACCEPTED : AT_ACCEPTED + 1, :seqs] = accepted_ref[...].astype(F32)
        table[AT_BIAS : AT_BIAS + 1, :] = jnp.full((1, LANES), bias_ref[0, layer], F32)
        table[AT_RATE : AT_RATE + 1, :] = jnp.full((1, LANES), rate_ref[0, layer], F32)
        table[AT_SKIP : AT_SKIP + 1, :] = jnp.full((1, LANES), skip_ref[0, layer], F32)
        table_ref[layer] = jnp.transpose(table[...])
        beforex_ref[layer] = sum(tdot(statex_ref[layer, j], places[j]) for j in range(kept)).astype(BF)
        beforebc_ref[layer] = jnp.concatenate(
            [
                sum(mdot(state_ref[layer, j], places[j]) for j in range(kept)),
                jnp.zeros((8 - here, seqs * draft), F32),
            ],
            axis=0,
        ).astype(BF)
    seq = lax.broadcasted_iota(jnp.int32, (seqs, seqs * draft), 0)
    at = lax.broadcasted_iota(jnp.int32, (seqs, seqs * draft), 1)
    owner = (at // draft == seq).astype(F32).astype(BF)
    spread_ref[...] = mdot(
        jnp.broadcast_to(accepted_ref[...].astype(F32), (8, seqs)).astype(BF), owner
    ).astype(jnp.int32)


def pair_kernel(keep_ref, got_ref, rows_ref, states_ref):
    cut = rows_ref.shape[1]
    rows_ref[...] = (keep_ref[:, :cut].astype(F32) + got_ref[:, :cut].astype(F32)).astype(BF)
    states_ref[...] = (keep_ref[:, cut:].astype(F32) + got_ref[:, cut:].astype(F32)).astype(BF)


def join_kernel(*refs):
    *pieces, out_ref = refs
    at = 0
    for piece in pieces:
        count = piece.shape[0]
        out_ref[at : at + count] = piece[...]
        at += count


def join(pieces):
    shape = (sum(p.shape[0] for p in pieces), *pieces[0].shape[1:])
    return call(join_kernel, jax.ShapeDtypeStruct(shape, BF), len(pieces))(*pieces)


def make_layer_kernel(layer, tokens, seqs, draft, own_cols, taps, last):
    model = own_cols * YS * ZS * CS
    pieces = own_cols // 8
    kept = taps - 1

    def kernel(*refs):
        own_ref, oth_ref, sown_ref, soth_ref, *w_refs = refs[: 4 + 2 * XS]
        (
            table_ref, own8_ref, beforex_ref, beforebc_ref, spread_ref, zx_ref, outw_ref, ssm_ref,
        ) = refs[4 + 2 * XS : 12 + 2 * XS]
        rest = refs[12 + 2 * XS :]
        if last:
            old_x_ref, old_bc_ref, _, *rest = rest
        (
            keep_ref, send_ref, newx_ref, newbc_ref, newssm_ref,
            xs, nb, wb, h_in, h_out, xw_all, zx_w, out_w, sems,
        ) = rest
        x_at, y_at0, z_at0, core = position()
        first = core == 0
        load_w = pltpu.make_async_copy(zx_ref.at[layer], zx_w, sems.at[0])
        load = pltpu.make_async_copy(ssm_ref.at[layer], h_in, sems.at[1])
        load_o = pltpu.make_async_copy(outw_ref.at[layer], out_w, sems.at[2])
        load_w.start()
        load.start()
        load_o.start()

        turned = table_ref[layer]
        width = beforex_ref.shape[1]
        here = newbc_ref.shape[-2]
        acc_col = turned[:seqs, AT_ACCEPTED : AT_ACCEPTED + 1].astype(jnp.int32)
        cols = turned[:width, AT_TAPS : AT_TAPS + 8]
        bias_dt = turned[:1, AT_BIAS : AT_BIAS + 1]
        rate = turned[:1, AT_RATE : AT_RATE + 1]
        skip = turned[:1, AT_SKIP : AT_SKIP + 1]

        take_own = core == layer
        for dx in range(XS):
            at_x = lax.rem(x_at + dx, XS)
            for dy in range(YS):
                at_y = lax.rem(y_at0 + dy, YS)
                for j in range(2):
                    at_z = lax.rem(z_at0 + 2 * at_x + j, ZS)
                    block = jnp.where(take_own, w_refs[dx][dy * 2 + j], w_refs[XS + dx][dy * 2 + j])
                    wb[at_y * ZS + at_z] = block

        total = jnp.zeros((8, tokens), F32)
        for k in range(YS * ZS):
            for j in range(pieces):
                lanes = slice(j * tokens, (j + 1) * tokens)
                a = own_ref[k, :, lanes].astype(F32)
                b = oth_ref[k, :, lanes].astype(F32)
                total = total + a * a + b * b
                at = 2 * k * own_cols + 8 * j
                xs[at : at + 8, :] = jnp.where(first, a, b)
                xs[at + own_cols : at + own_cols + 8, :] = jnp.where(first, b, a)
        scale = lax.rsqrt(jnp.sum(total, axis=0, keepdims=True) / model + EPS)
        for j in range(model // LANES):
            at = slice(j * LANES, (j + 1) * LANES)
            col = turned[:, j : j + 1]
            nb[at, :] = ((xs[at, :] * scale) * col).astype(BF)

        normed = nb[...]
        states = YS * ZS * 8 // 2

        def bc_rows(lo, hi):
            return wb[:, :, lo:hi].astype(F32).reshape(2 * states, hi - lo)

        mine = mdot(own8_ref[layer], normed).astype(BF)
        bc = mdot(bc_rows(0, model).astype(BF), normed).astype(BF).astype(F32)
        load_w.wait()
        zx = tdot(zx_w[...], normed).astype(BF)
        gate_z = zx[:width].astype(F32)
        values = zx[width:].astype(F32)

        lane = lax.broadcasted_iota(jnp.int32, (1, tokens), 1)
        t0 = lane % draft

        slot = lax.broadcasted_iota(jnp.int32, (2 * LANES, tokens), 0)
        slot_lane = lax.broadcasted_iota(jnp.int32, (2 * LANES, tokens), 1)
        slot_seq, slot_j = slot & (SLOT - 1), slot // SLOT
        place = (
            (slot_seq < seqs) & (slot_j < kept) & (slot_lane == slot_seq * draft + (draft - kept) + slot_j)
        ).astype(F32).astype(BF)
        lanes = slice(pieces * tokens, pieces * tokens + 2 * LANES)
        saved_bc = jnp.where(
            take_own, sown_ref[:, :, lanes].astype(F32), soth_ref[:, :, lanes].astype(F32)
        ).reshape(2 * states, 2 * LANES)
        before_bc = mdot(saved_bc.astype(BF), place)
        extra = bc_rows(model, model + LANES)
        before_b, before_mb = beforex_ref[layer], beforebc_ref[layer]
        before_x = before_b.astype(F32)

        def convolve(now, before, weights, bias):
            acc = None
            for k in range(taps):
                d = taps - 1 - k
                if d:
                    shifted = jnp.where(
                        t0 >= d,
                        pltpu.roll(now, d, 1),
                        pltpu.roll(before, tokens - (draft - d), 1),
                    )
                else:
                    shifted = now
                term = shifted * weights[k]
                acc = term if acc is None else acc + term
            return silu(acc + bias)

        xc = convolve(values, before_x, [cols[:, k : k + 1] for k in range(taps)], cols[:, taps : taps + 1])
        bcc = convolve(
            bc,
            before_bc,
            [extra[:, k : k + 1] for k in range(taps)],
            extra[:, taps : taps + 1],
        ).astype(BF)

        seq = lax.broadcasted_iota(jnp.int32, (seqs, tokens), 0)
        at = lax.broadcasted_iota(jnp.int32, (seqs, tokens), 1)
        values_b = zx[width:]
        for i in range(kept):
            row = acc_col + i
            new = ((at == seq * draft + row - kept) & (row >= kept)).astype(F32).astype(BF)
            old = ((at == seq * draft + (draft - kept) + row) & (row < kept)).astype(F32).astype(BF)
            rows_x = (ndot(new, values_b) + ndot(old, before_b)).astype(BF)
            rows_bc = (ndot(mine, new) + ndot(before_mb, old))[:here].astype(BF)
            if last:
                newx_ref[layer, i], newbc_ref[layer, i] = rows_x, rows_bc
                for l in range(layer):
                    newx_ref[l, i], newbc_ref[l, i] = old_x_ref[i], old_bc_ref[i]
            else:
                newx_ref[i], newbc_ref[i] = rows_x, rows_bc

        step = softplus(mine[here : here + 1, :].astype(F32) + bias_dt)
        cum = step
        for d in (1, 2, 4):
            cum = cum + jnp.where(t0 >= d, pltpu.roll(cum, d, 1), 0.0)
        accepted = spread_ref[:1]
        cut = jnp.where(t0 < accepted, step, 0.0)
        for d in (1, 2, 4):
            cut = cut + jnp.where((t0 & d) != 0, pltpu.roll(cut, d, 1), pltpu.roll(cut, tokens - d, 1))
        weight = jnp.where(t0 < accepted, jnp.exp(-rate * (cut - cum)) * step, 0.0)
        fall = jnp.exp(-rate * cum)
        fall_cut = jnp.exp(-rate * cut)
        xb = xc.astype(BF)
        xw_all[...] = (xc * weight).astype(BF)
        load.wait()

        per_tile = LANES // draft
        sub = lax.broadcasted_iota(jnp.int32, (LANES, LANES), 0)
        lan = lax.broadcasted_iota(jnp.int32, (LANES, LANES), 1)
        causal = (sub // draft == lan // draft) & (sub <= lan)
        group = lax.broadcasted_iota(jnp.int32, (1, LANES), 1) // draft
        pick16 = lax.broadcasted_iota(jnp.int32, (per_tile, LANES), 0) * draft == (
            lax.broadcasted_iota(jnp.int32, (per_tile, LANES), 1)
        )
        parts = []
        for tile in range(tokens // LANES):
            ls = slice(tile * LANES, (tile + 1) * LANES)
            bmat = bcc[:states, ls]
            cmat = bcc[states:, ls]
            cum_r = jnp.broadcast_to(cum[:, ls], (LANES, LANES))
            step_c = jnp.transpose(jnp.broadcast_to(step[:, ls], (LANES, LANES)))
            cum_c = jnp.transpose(cum_r)
            gram = tdot(bmat, cmat)
            within = jnp.where(causal, gram * (jnp.exp(-rate * (cum_r - cum_c)) * step_c), 0.0)
            y_new = mdot(xb[:, ls], within.astype(BF))
            y_old = jnp.zeros((width, LANES), F32)
            falls = jnp.sum(jnp.where(pick16, fall_cut[:, ls], 0.0), axis=1, keepdims=True)
            xw = xw_all[:, ls]
            for s in range(per_tile):
                n = tile * per_tile + s
                h0 = h_in[n]
                here = group == s
                y_old = jnp.where(here, mdot(h0.astype(BF), cmat), y_old)
                add = ndot(jnp.where(here, xw, jnp.zeros_like(xw)), bmat)
                h_out[n] = h0 * falls[s : s + 1, :] + add
            parts.append(fall[:, ls] * y_old + y_new)
        store = pltpu.make_async_copy(h_out, newssm_ref.at[layer], sems.at[3])
        store.start()
        y = jnp.concatenate(parts, axis=1) + skip * xc
        gated = y * silu(gate_z)
        ssq = jnp.sum(gated * gated, axis=0, keepdims=True)
        u = (gated * cols[:, taps + 1 : taps + 2]).astype(BF)

        high = ssq.astype(BF)
        low = (ssq - high.astype(F32)).astype(BF)
        row8 = lax.broadcasted_iota(jnp.int32, (8, tokens), 0)
        tail = jnp.where(row8 == 0, high.astype(F32), jnp.where(row8 == 1, low.astype(F32), 0.0))
        block = own_cols * CS * ZS
        load_o.wait()
        for y_at in range(YS):
            out = tdot(out_w[:, y_at * block : (y_at + 1) * block], u)
            out = out.reshape(ZS, CS, pieces, 8, tokens)
            for z in range(ZS):
                even, odd = out[z, 0], out[z, 1]
                rows = slice(z * pieces, (z + 1) * pieces)
                keep_ref[y_at, rows] = jnp.where(first, even, odd)
                send_ref[y_at, rows] = jnp.where(first, odd, even).astype(BF)
            keep_ref[y_at, ZS * pieces] = tail
            send_ref[y_at, ZS * pieces] = tail.astype(BF)
        store.wait()

    return kernel


def add_cores_kernel(keep_ref, got_ref, out_ref):
    tiles = keep_ref.shape[1]
    for y in range(YS):
        out_ref[y, : tiles - 1] = (
            keep_ref[y, : tiles - 1] + got_ref[y, : tiles - 1].astype(F32)
        ).astype(BF)
    tail = keep_ref[0, tiles - 1] + got_ref[0, tiles - 1].astype(F32)
    for y in range(YS):
        out_ref[y, tiles - 1] = split_tail(tail)


def split_tail(tail):
    row8 = lax.broadcasted_iota(jnp.int32, tail.shape, 0)
    ssq = tail[0:1] + tail[1:2]
    high = ssq.astype(BF).astype(F32)
    return jnp.where(row8 == 0, high, jnp.where(row8 == 1, ssq - high, 0.0)).astype(BF)


def add_y_kernel(got_ref, out_ref):
    tiles = got_ref.shape[1]
    pieces = (tiles - 1) // ZS

    def summed(rows):
        acc = got_ref[0, rows].astype(F32)
        for y in range(1, YS):
            acc = acc + got_ref[y, rows].astype(F32)
        return acc

    tail = split_tail(summed(slice(tiles - 1, tiles))[0])
    for z in range(ZS):
        out_ref[z, :pieces] = summed(slice(z * pieces, (z + 1) * pieces)).astype(BF)
        out_ref[z, pieces] = tail


def make_finish_kernel(inner, last):
    def finish_kernel(got_ref, stream_ref, out_ref):
        tiles = got_ref.shape[1]
        tokens = got_ref.shape[3]
        acc = got_ref[0].astype(F32)
        for z in range(1, ZS):
            acc = acc + got_ref[z].astype(F32)
        ssq = acc[tiles - 1, 0:1] + acc[tiles - 1, 1:2]
        scale = lax.rsqrt(ssq / inner + EPS)
        for j in range(tiles - 1):
            lanes = slice(j * tokens, (j + 1) * tokens)
            new = (stream_ref[:, lanes].astype(F32) + acc[j] * scale).astype(BF)
            if last:
                out_ref[j] = new
            else:
                out_ref[:, lanes] = new

    return finish_kernel


def call(kernel, out_shape, count):
    return pl.pallas_call(
        kernel,
        out_shape=out_shape,
        in_specs=[VMEM] * count,
        out_specs=jax.tree.map(lambda _: VMEM, out_shape),
        compiler_params=limit(10),
    )


def local(
    draft_ids,
    accepted,
    embedding,
    norm_gain,
    w_zx,
    w_dt,
    w_bc,
    dt_bias,
    decay_rate,
    skip_weight,
    conv_x_w,
    conv_x_b,
    conv_bc_w,
    conv_bc_b,
    gate_gain,
    out_w,
    ssm_state,
    conv_x_state,
    conv_bc_state,
):
    seqs, draft = draft_ids.shape
    tokens = seqs * draft
    own_cols = embedding.shape[1]
    model = own_cols * YS * ZS * CS
    width = w_zx.shape[3] // 2
    inner = width * YS * ZS * CS
    bc_here = w_bc.shape[2]
    taps = conv_x_w.shape[1]
    kept = taps - 1
    pieces = own_cols // 8
    states = ssm_state.shape[4]

    tokens_ids = draft_ids.T
    state_shape = (LAYERS, seqs, width, states)

    w_rows = jnp.swapaxes(w_bc, 1, 2)
    row_shape = jax.ShapeDtypeStruct((8, model + 3 * LANES), BF)
    keep, send, table, own8, before_x, before_bc, spread_acc = pl.pallas_call(
        setup_kernel,
        out_shape=(
            row_shape,
            row_shape,
            jax.ShapeDtypeStruct((LAYERS, LANES, LANES), F32),
            jax.ShapeDtypeStruct((LAYERS, 8, model), BF),
            jax.ShapeDtypeStruct((LAYERS, width, tokens), BF),
            jax.ShapeDtypeStruct((LAYERS, 8, tokens), BF),
            jax.ShapeDtypeStruct((8, tokens), jnp.int32),
        ),
        in_specs=[SMEM] * 3 + [VMEM] * 11,
        out_specs=(VMEM,) * 7,
        scratch_shapes=[pltpu.VMEM((LANES, LANES), F32)],
        compiler_params=limit(60),
        name="setup",
    )(
        *[v.reshape(1, LAYERS) for v in (dt_bias, decay_rate, skip_weight)],
        w_rows,
        w_dt.reshape(LAYERS, model),
        jnp.transpose(conv_bc_state, (0, 2, 3, 1)),
        conv_bc_w,
        conv_bc_b,
        norm_gain,
        conv_x_w,
        conv_x_b,
        gate_gain,
        jnp.swapaxes(conv_x_state, 1, 2),
        accepted.reshape(1, seqs),
    )
    pair_rows, pair_states = call(
        pair_kernel,
        (
            jax.ShapeDtypeStruct((8, model + LANES), BF),
            jax.ShapeDtypeStruct((8, 2 * LANES), BF),
        ),
        2,
    )(keep, swap_cores(send))
    pair_rows = pair_rows[None]
    near = join(
        [fetch(pair_rows, lambda x, y, z, c, j=j: (x, y, z + 2 * x + j, c)) for j in range(2)]
    )
    stream = lookup(tokens_ids, embedding.T, pair_states)
    plane = join(
        [near] + [fetch(near, lambda x, y, z, c, d=d: (x, y + d, z, c)) for d in range(1, YS)]
    )
    stream, plane = lax.optimization_barrier((stream, plane))
    w_own = [plane]
    for d in range(1, XS):
        w_own.append(fetch(plane, lambda x, y, z, c, d=d: ((x + d) % XS, y, z, c)))
    own, oth = gather_planes(stream)
    w_oth = [swap_cores(w) for w in w_own]
    first_own, first_oth = own, oth

    tables = [table, own8, before_x, before_bc, spread_acc] + [
        pltpu.with_memory_space_constraint(v, pltpu.HBM)
        for v in (w_zx.reshape(LAYERS, model, 2 * width), out_w, ssm_state.reshape(state_shape))
    ]
    table_specs = [VMEM] * 5 + [HBM] * 3
    saved = ()
    tiles = ZS * pieces + 1
    for layer in range(LAYERS):
        last = layer + 1 == LAYERS
        lead = (LAYERS,) if last else ()
        args = [own, oth, first_own, first_oth, *w_own, *w_oth, *tables, *saved]
        specs = [VMEM] * (4 + 2 * XS) + table_specs + [VMEM, VMEM, HBM][: len(saved)]
        keep, send, *saved = pl.pallas_call(
            make_layer_kernel(layer, tokens, seqs, draft, own_cols, taps, last),
            out_shape=(
                jax.ShapeDtypeStruct((YS, tiles, 8, tokens), F32),
                jax.ShapeDtypeStruct((YS, tiles, 8, tokens), BF),
                jax.ShapeDtypeStruct((*lead, kept, seqs, width), BF),
                jax.ShapeDtypeStruct((*lead, kept, bc_here, seqs), BF),
                jax.ShapeDtypeStruct(state_shape, F32),
            ),
            in_specs=specs,
            out_specs=(VMEM, VMEM, VMEM, VMEM, HBM),
            scratch_shapes=[
                pltpu.VMEM((model, tokens), F32),
                pltpu.VMEM((model, tokens), BF),
                pltpu.VMEM((YS * ZS, 8, model + LANES), BF),
                pltpu.VMEM(state_shape[1:], F32),
                pltpu.VMEM(state_shape[1:], F32),
                pltpu.VMEM((width, tokens), BF),
                pltpu.VMEM((model, 2 * width), BF),
                pltpu.VMEM((width, model), BF),
                pltpu.SemaphoreType.DMA((4,)),
            ],
            input_output_aliases={len(args) - 1: 4} if last else {},
            compiler_params=limit(34),
        )(*args)
        summed = call(
            add_cores_kernel, jax.ShapeDtypeStruct((YS, tiles, 8, tokens), BF), 2
        )(keep, swap_cores(send))
        summed = call(
            add_y_kernel, jax.ShapeDtypeStruct((ZS, pieces + 1, 8, tokens), BF), 1
        )(exchange(summed, Y_GROUPS))
        shape = (pieces, 8, tokens) if last else (8, pieces * tokens)
        stream = call(
            make_finish_kernel(inner, last), jax.ShapeDtypeStruct(shape, BF), 2
        )(exchange(summed, Z_GROUPS), stream)
        if not last:
            own, oth = gather_planes(stream)
    new_x, new_bc, new_ssm = saved
    hidden = stream.reshape(own_cols, tokens).T
    kept_x = jnp.swapaxes(new_x, 1, 2)
    kept_bc = jnp.transpose(new_bc, (0, 3, 1, 2))
    return (hidden, new_ssm.reshape(ssm_state.shape), kept_x, kept_bc)


def solution(mesh):
    placed = (
        P("batch", None),
        P("batch"),
        P(None, "heads"),
        P(),
        P(None, None, "heads", None),
        P(None, None, "heads"),
        P(None, None, "heads"),
        P(None, "heads"),
        P(None, "heads"),
        P(None, "heads"),
        P(None, None, "heads"),
        P(None, "heads"),
        P(None, None, "heads"),
        P(None, "heads"),
        P(None, "heads"),
        P(None, "heads", None),
        P(None, "batch", "heads", None, None),
        P(None, "batch", None, "heads"),
        P(None, "batch", None, "heads"),
    )
    return jax.shard_map(
        local,
        mesh=mesh,
        in_specs=placed,
        out_specs=(
            P("batch", "heads"),
            P(None, "batch", "heads", None, None),
            P(None, "batch", None, "heads"),
            P(None, "batch", None, "heads"),
        ),
        check_vma=False,
    )
```

time: 209 us -> 201 us (0.962)
  blocking collectives: 140 us -> 121 us
  starting transfers between devices: 4.33 us -> 22.5 us
  waiting for transfers between devices: 17.9 us -> 29.9 us
  local copies, waits for them, and re-layouts: 15.1 us -> 3.84 us
  Pallas kernels: 26.5 us -> 22.6 us
  other arithmetic: 2.86 us -> 0 us
    ppermute x0 -> x8, starting transfers between devices: none -> 21.4 us  [fetch(): return lax.ppermute(value, ('batch', 'heads'), pairs)]
    all_to_all x7 -> x8, blocking collectives: 140 us -> 121 us  [exchange(): lax.all_to_all(value, 'heads', 0, 0, tiled=True, axis_index_groups=groups)]
    ppermute x0 -> x8, waiting for transfers between devices: none -> 19.3 us  [fetch(): return lax.ppermute(value, ('batch', 'heads'), pairs)]
    all_to_all x1 -> x0, waiting for transfers between devices: 10.6 us -> none  [exchange(): lax.all_to_all(value, 'heads', 0, 0, tiled=True, axis_index_groups=groups)]
    pallas_call x1, Pallas kernels: 7.78 us -> 4.3 us  [lookup(): pl.pallas_call(lookup_kernel, out_shape=jax.ShapeDtypeStruct((8, rows //...]
    all_to_all x1 -> x0, starting transfers between devices: 3.42 us -> none  [exchange(): lax.all_to_all(value, 'heads', 0, 0, tiled=True, axis_index_groups=groups)]
    another operation x7 -> x0, local copies, waits for them, and re-layouts: 3.33 us -> none  [the longest x4 3.23 us: local(): jnp.stack([conv_x_w[:, k].astype(F32) for k in range(taps)] + [conv_x_b.a...]
    unnamed x28 -> x16, local copies, waits for them, and re-layouts: 6.96 us -> 3.64 us
  transfers between devices with their start and end apart: 6 -> 17, of which waited for: 4 -> 9; matrix products, arithmetic and copies ran while one was open for 4% -> 0% of each run, Pallas kernels for 4% -> 2%
where the time goes in v2:
time: 201 us; the launch traced here: 200 us
  blocking collectives  121 us (60%)
  waiting for transfers between devices  29.9 us (15%)
  Pallas kernels  22.6 us (11%)
  starting transfers between devices  22.5 us (11%)
  local copies, waits for them, and re-layouts  3.84 us (2%)
    all_to_all x8, blocking collectives, exchange(): lax.all_to_all(value, 'heads', 0, 0, tiled=True, axis_index_groups=groups)  121 us
    ppermute x8, starting transfers between devices, fetch(): return lax.ppermute(value, ('batch', 'heads'), pairs)  21.4 us
    ppermute x8, waiting for transfers between devices, fetch(): return lax.ppermute(value, ('batch', 'heads'), pairs)  19.3 us
    pallas_call x2, Pallas kernels, local(): pl.pallas_call(make_layer_kernel(layer, tokens, seqs, draft, own_cols, ta...  14.8 us
    ppermute x9, waiting for transfers between devices, swap_cores(): return lax.ppermute(value, 'heads', PARTNER)  10.6 us
    pallas_call x1, Pallas kernels, lookup(): pl.pallas_call(lookup_kernel, out_shape=jax.ShapeDtypeStruct((8, rows //...  4.3 us
  transfers between devices with their start and end apart: 17, of which 9 were waited for; matrix products, arithmetic and copies ran while one was open for 0% of the time, Pallas kernels for 2%

profile of v2, /device:TPU:2, one launch (start us, length us, event | category | flops | bytes accessed | tf_op | source)
XLA Modules:
  0.0 200.2 jit_solution(8123580562238403300)
XLA Ops:
  0.6 2.0 setup.1
  2.6 0.1 collective-permute-start
  2.7 1.4 collective-permute-done.got_ref
  4.1 0.8 copy-done.6
  4.9 6.8 %collective-permute-start.2 = (bf16[1,8,2688]{2,1,0:T(8,128)(2,1)S(1)}, bf16[1,8,2688]{2,1,0:T(8,128)(2,1)S(1)}, u32[]{:S(2)}, u32[]{:S(2)}) collective-permute-start(bf16[1,8,2688]{2,1,0:T(8,128)(2,1)S(1)} %bitcast.31), channel_id=1, source_target_pairs={{2,0},{3,1},{4,2},{5,3},{6,4},{7,5},{8,6},{9,7},{10,8},{11,9},{12,... | collective-permute-start | bytes 129032 | tf_op jit(solution)/shard_map/ppermute | solution.py:37
  11.8 2.4 %collective-permute-start.1 = (bf16[1,8,2688]{2,1,0:T(8,128)(2,1)S(1)}, bf16[1,8,2688]{2,1,0:T(8,128)(2,1)S(1)}, u32[]{:S(2)}, u32[]{:S(2)}) collective-permute-start(bf16[1,8,2688]{2,1,0:T(8,128)(2,1)S(1)} %bitcast.32), channel_id=1, source_target_pairs={{0,0},{1,1},{2,2},{3,3},{4,4},{5,5},{6,6},{7,7},{8,8},{9,9},{10,10... | collective-permute-start | bytes 129032 | tf_op jit(solution)/shard_map/ppermute | solution.py:37
  14.2 0.8 collective-permute-done.2.refs_1_
  15.0 3.6 %collective-permute-done.1.refs_0_ = bf16[1,8,2688]{2,1,0:T(8,128)(2,1)S(1)} collective-permute-done((bf16[1,8,2688]{2,1,0:T(8,128)(2,1)S(1)}, bf16[1,8,2688]{2,1,0:T(8,128)(2,1)S(1)}, u32[]{:S(2)}, u32[]{:S(2)}) %collective-permute-start.1) | collective-permute-done | bytes 43040 | tf_op jit(solution)/shard_map/ppermute | solution.py:37
  18.6 1.6 collective-permute-start.5
  20.2 2.9 %collective-permute-start.4 = (bf16[2,8,2688]{2,1,0:T(8,128)(2,1)S(1)}, bf16[2,8,2688]{2,1,0:T(8,128)(2,1)S(1)}, u32[]{:S(2)}, u32[]{:S(2)}) collective-permute-start(bf16[2,8,2688]{2,1,0:T(8,128)(2,1)S(1)} %shard_map.211.refs_0_), channel_id=1, source_target_pairs={{32,0},{33,1},{34,2},{35,3},{36,4},{37,5},{38,6},{39,7},{40,8},{41... | collective-permute-start | bytes 258056 | tf_op jit(solution)/shard_map/ppermute | solution.py:37
  23.1 1.3 collective-permute-start.3
  24.5 2.1 %copy-done = bf16[50280,40]{0,1:T(8,128)(2,1)S(1)} copy-done((bf16[50280,40]{0,1:T(8,128)(2,1)S(1)}, bf16[50280,40]{0,1:T(8,128)(2,1)}, u32[]{:S(2)}) %copy-start) | copy-done | bytes 4022424
  26.6 0.7 copy-done.7
  27.3 4.3 %lookup.1.stream_ref = bf16[8,2176]{1,0:T(8,128)(2,1)S(1)} custom-call(s32[8,48]{1,0:T(8,128)S(1)} %bitcast.30, bf16[40,50280]{1,0:T(8,128)(2,1)S(1)} %bitcast.27, bf16[8,256]{1,0:T(8,128)(2,1)S(1)} %get-tuple-element.27.beside_ref), custom_call_target="tpu_custom_call" | custom-call | tf_op jit(solution)/shard_map/lookup/pallas_call | solution.py:126
  31.6 0.0 collective-permute-done.4.refs_2_
  31.7 0.0 copy-start.1
  31.7 0.0 copy-start.4
  31.8 14.5 %all_to_all.40 = bf16[8,8,2176]{2,1,0:T(8,128)(2,1)S(1)} all-to-all(bf16[8,8,2176]{2,1,0:T(8,128)(2,1)S(1)} %broadcast_in_dim.11), channel_id=1, replica_groups={{0,2,4,6,8,10,12,14},{1,3,5,7,9,11,13,15},{16,18,20,22,24,26,28,30},{17..., dimensions={0} | all-to-all | bytes 557056 | tf_op jit(solution)/shard_map/all_to_all | solution.py:45
  46.3 0.1 broadcast_in_dim.12
  46.4 15.1 %all_to_all.41 = bf16[4,8,8,2176]{3,2,1,0:T(8,128)(2,1)S(1)} all-to-all(bf16[4,8,8,2176]{3,2,1,0:T(8,128)(2,1)S(1)} %broadcast_in_dim.12), channel_id=1, replica_groups={{0,16,32,48},{1,17,33,49},{2,18,34,50},{3,19,35,51},{4,20,36,52},{5,21,..., dimensions={0} | all-to-all | bytes 2228224 | tf_op jit(solution)/shard_map/all_to_all | solution.py:45
  61.5 4.2 %collective-permute-start.9 = (bf16[8,8,2688]{2,1,0:T(8,128)(2,1)S(1)}, bf16[8,8,2688]{2,1,0:T(8,128)(2,1)S(1)}, u32[]{:S(2)}, u32[]{:S(2)}) collective-permute-start(bf16[8,8,2688]{2,1,0:T(8,128)(2,1)S(1)} %shard_map.212.refs_4_), channel_id=1, source_target_pairs={{192,0},{193,1},{194,2},{195,3},{196,4},{197,5},{198,6},{199,7},{2... | collective-permute-start | bytes 1032200 | tf_op jit(solution)/shard_map/ppermute | solution.py:37
  65.7 2.1 %collective-permute-start.7 = (bf16[8,8,2688]{2,1,0:T(8,128)(2,1)S(1)}, bf16[8,8,2688]{2,1,0:T(8,128)(2,1)S(1)}, u32[]{:S(2)}, u32[]{:S(2)}) collective-permute-start(bf16[8,8,2688]{2,1,0:T(8,128)(2,1)S(1)} %shard_map.212.refs_4_), channel_id=1, source_target_pairs={{64,0},{65,1},{66,2},{67,3},{68,4},{69,5},{70,6},{71,7},{72,8},{73... | collective-permute-start | bytes 1032200 | tf_op jit(solution)/shard_map/ppermute | solution.py:37
  67.8 13.3 %collective-permute-done.9.refs_7_ = bf16[8,8,2688]{2,1,0:T(8,128)(2,1)S(1)} collective-permute-done((bf16[8,8,2688]{2,1,0:T(8,128)(2,1)S(1)}, bf16[8,8,2688]{2,1,0:T(8,128)(2,1)S(1)}, u32[]{:S(2)}, u32[]{:S(2)}) %collective-permute-start.9) | collective-permute-done | bytes 344096 | tf_op jit(solution)/shard_map/ppermute | solution.py:37
  81.1 0.5 collective-permute-start.12
  81.6 1.7 collective-permute-done.7.refs_5_
  83.3 0.0 collective-permute-start.11
  83.3 1.6 collective-permute-done.11.refs_9_
  85.0 7.1 %shard_map.213 = (f32[4,41,8,384]{3,2,1,0:T(8,128)S(1)}, bf16[4,41,8,384]{3,2,1,0:T(8,128)(2,1)S(1)}, bf16[3,48,64]{2,1,0:T(8,128)(2,1)S(1)}, bf16[3,4,48]{2,1,0:T(4,128)(2,1)S(1)}, f32[2,48,64,128]{3,2,1,0:T(8,128)}) custom-call(bf16[32,8,2176]{2,1,0:T(8,128)(2,1)S(1)} %bitcast.24, bf16[32,8,2176]{2,1,0:T(8,128)(2,1)S(1)} %collective-permute-done.6.refs_1_.refs_3_, ...), custom_call_target="tpu_custom_call" | custom-call | tf_op jit(solution)/shard_map/pallas_call | solution.py:620
  92.1 0.2 collective-permute-start.14
  92.3 2.5 %collective-permute-done.14.got_ref = bf16[4,41,8,384]{3,2,1,0:T(8,128)(2,1)S(1)} collective-permute-done((bf16[4,41,8,384]{3,2,1,0:T(8,128)(2,1)S(1)}, bf16[4,41,8,384]{3,2,1,0:T(8,128)(2,1)S(1)}, u32[]{:S(2)}, u32[]{:S(2)}) %collective-permute-start.14) | collective-permute-done | bytes 1007648 | tf_op jit(solution)/shard_map/ppermute | solution.py:41
  94.8 0.2 shard_map.214
  95.0 17.6 %all_to_all.42.got_ref = bf16[4,41,8,384]{3,2,1,0:T(8,128)(2,1)S(1)} all-to-all(bf16[4,41,8,384]{3,2,1,0:T(8,128)(2,1)S(1)} %shard_map.214), channel_id=1, replica_groups={{0,16,32,48},{1,17,33,49},{2,18,34,50},{3,19,35,51},{4,20,36,52},{5,21,..., dimensions={0} | all-to-all | bytes 2015232 | tf_op jit(solution)/shard_map/all_to_all | solution.py:45
  112.6 0.1 shard_map.215
  112.8 14.4 %all_to_all.43.got_ref = bf16[8,6,8,384]{3,2,1,0:T(8,128)(2,1)S(1)} all-to-all(bf16[8,6,8,384]{3,2,1,0:T(8,128)(2,1)S(1)} %shard_map.215), channel_id=1, replica_groups={{0,2,4,6,8,10,12,14},{1,3,5,7,9,11,13,15},{16,18,20,22,24,26,28,30},{17..., dimensions={0} | all-to-all | bytes 589824 | tf_op jit(solution)/shard_map/all_to_all | solution.py:45
  127.2 0.1 shard_map.216.stream_ref
  127.2 12.7 %all_to_all.44 = bf16[8,8,1920]{2,1,0:T(8,128)(2,1)S(1)} all-to-all(bf16[8,8,1920]{2,1,0:T(8,128)(2,1)S(1)} %broadcast_in_dim.13), channel_id=1, replica_groups={{0,2,4,6,8,10,12,14},{1,3,5,7,9,11,13,15},{16,18,20,22,24,26,28,30},{17..., dimensions={0} | all-to-all | bytes 491520 | tf_op jit(solution)/shard_map/all_to_all | solution.py:45
  140.0 0.1 broadcast_in_dim.14
  140.0 14.2 %all_to_all.45 = bf16[4,8,8,1920]{3,2,1,0:T(8,128)(2,1)S(1)} all-to-all(bf16[4,8,8,1920]{3,2,1,0:T(8,128)(2,1)S(1)} %broadcast_in_dim.14), channel_id=1, replica_groups={{0,16,32,48},{1,17,33,49},{2,18,34,50},{3,19,35,51},{4,20,36,52},{5,21,..., dimensions={0} | all-to-all | bytes 1966080 | tf_op jit(solution)/shard_map/all_to_all | solution.py:45
  154.2 0.0 collective-permute-start.15
  154.2 2.6 %collective-permute-done.15.refs_1_ = bf16[32,8,1920]{2,1,0:T(8,128)(2,1)S(1)} collective-permute-done((bf16[32,8,1920]{2,1,0:T(8,128)(2,1)S(1)}, bf16[32,8,1920]{2,1,0:T(8,128)(2,1)S(1)}, u32[]{:S(2)}, u32[]{:S(2)}) %collective-permute-start.15) | collective-permute-done | bytes 983072 | tf_op jit(solution)/shard_map/ppermute | solution.py:41
  156.8 7.7 %shard_map.217 = (f32[4,41,8,384]{3,2,1,0:T(8,128)S(1)}, bf16[4,41,8,384]{3,2,1,0:T(8,128)(2,1)S(1)}, bf16[2,3,48,64]{3,2,1,0:T(8,128)(2,1)}, bf16[2,3,4,48]{3,2,1,0:T(4,128)(2,1)}, f32[2,48,64,128]{3,2,1,0:T(8,128)}) custom-call(bf16[32,8,1920]{2,1,0:T(8,128)(2,1)S(1)} %bitcast.29, ...), custom_call_target="tpu_custom_call", output_to_operand_aliasing={{4}: (22, {})} | custom-call | tf_op jit(solution)/shard_map/pallas_call | solution.py:620
  164.5 0.2 collective-permute-start.16
  164.7 2.5 %collective-permute-done.16.got_ref = bf16[4,41,8,384]{3,2,1,0:T(8,128)(2,1)S(1)} collective-permute-done((bf16[4,41,8,384]{3,2,1,0:T(8,128)(2,1)S(1)}, bf16[4,41,8,384]{3,2,1,0:T(8,128)(2,1)S(1)}, u32[]{:S(2)}, u32[]{:S(2)}) %collective-permute-start.16) | collective-permute-done | bytes 1007648 | tf_op jit(solution)/shard_map/ppermute | solution.py:41
  167.2 0.2 shard_map.218
  167.4 17.6 %all_to_all.46.got_ref = bf16[4,41,8,384]{3,2,1,0:T(8,128)(2,1)S(1)} all-to-all(bf16[4,41,8,384]{3,2,1,0:T(8,128)(2,1)S(1)} %shard_map.218), channel_id=1, replica_groups={{0,16,32,48},{1,17,33,49},{2,18,34,50},{3,19,35,51},{4,20,36,52},{5,21,..., dimensions={0} | all-to-all | bytes 2015232 | tf_op jit(solution)/shard_map/all_to_all | solution.py:45
  185.0 0.1 shard_map.219
  185.2 14.4 %all_to_all.47.got_ref = bf16[8,6,8,384]{3,2,1,0:T(8,128)(2,1)S(1)} all-to-all(bf16[8,6,8,384]{3,2,1,0:T(8,128)(2,1)S(1)} %shard_map.219), channel_id=1, replica_groups={{0,2,4,6,8,10,12,14},{1,3,5,7,9,11,13,15},{16,18,20,22,24,26,28,30},{17..., dimensions={0} | all-to-all | bytes 589824 | tf_op jit(solution)/shard_map/all_to_all | solution.py:45
  199.5 0.7 shard_map.220
  (27 shorter events, 0.1 us)
Async XLA Ops:
  2.6 1.5 collective-permute-start
  4.1 0.8 copy-start.6
  4.9 10.1 %collective-permute-start.2 = (bf16[1,8,2688]{2,1,0:T(8,128)(2,1)S(1)}, bf16[1,8,2688]{2,1,0:T(8,128)(2,1)S(1)}, u32[]{:S(2)}, u32[]{:S(2)}) collective-permute-start(bf16[1,8,2688]{2,1,0:T(8,128)(2,1)S(1)} %bitcast.31), channel_id=1, source_target_pairs={{2,0},{3,1},{4,2},{5,3},{6,4},{7,5},{8,6},{9,7},{10,8},{11,9},{12,... | collective-permute-start | bytes 129032 | tf_op jit(solution)/shard_map/ppermute | solution.py:37
  11.8 6.8 %collective-permute-start.1 = (bf16[1,8,2688]{2,1,0:T(8,128)(2,1)S(1)}, bf16[1,8,2688]{2,1,0:T(8,128)(2,1)S(1)}, u32[]{:S(2)}, u32[]{:S(2)}) collective-permute-start(bf16[1,8,2688]{2,1,0:T(8,128)(2,1)S(1)} %bitcast.32), channel_id=1, source_target_pairs={{0,0},{1,1},{2,2},{3,3},{4,4},{5,5},{6,6},{7,7},{8,8},{9,9},{10,10... | collective-permute-start | bytes 129032 | tf_op jit(solution)/shard_map/ppermute | solution.py:37
  18.6 13.0 %collective-permute-start.5 = (bf16[2,8,2688]{2,1,0:T(8,128)(2,1)S(1)}, bf16[2,8,2688]{2,1,0:T(8,128)(2,1)S(1)}, u32[]{:S(2)}, u32[]{:S(2)}) collective-permute-start(bf16[2,8,2688]{2,1,0:T(8,128)(2,1)S(1)} %shard_map.211.refs_0_), channel_id=1, source_target_pairs={{48,0},{49,1},{50,2},{51,3},{52,4},{53,5},{54,6},{55,7},{56,8},{57... | collective-permute-start | bytes 258056 | tf_op jit(solution)/shard_map/ppermute | solution.py:37
  20.2 11.4 %collective-permute-start.4 = (bf16[2,8,2688]{2,1,0:T(8,128)(2,1)S(1)}, bf16[2,8,2688]{2,1,0:T(8,128)(2,1)S(1)}, u32[]{:S(2)}, u32[]{:S(2)}) collective-permute-start(bf16[2,8,2688]{2,1,0:T(8,128)(2,1)S(1)} %shard_map.211.refs_0_), channel_id=1, source_target_pairs={{32,0},{33,1},{34,2},{35,3},{36,4},{37,5},{38,6},{39,7},{40,8},{41... | collective-permute-start | bytes 258056 | tf_op jit(solution)/shard_map/ppermute | solution.py:37
  23.1 8.5 %collective-permute-start.3 = (bf16[2,8,2688]{2,1,0:T(8,128)(2,1)S(1)}, bf16[2,8,2688]{2,1,0:T(8,128)(2,1)S(1)}, u32[]{:S(2)}, u32[]{:S(2)}) collective-permute-start(bf16[2,8,2688]{2,1,0:T(8,128)(2,1)S(1)} %shard_map.211.refs_0_), channel_id=1, source_target_pairs={{16,0},{17,1},{18,2},{19,3},{20,4},{21,5},{22,6},{23,7},{24,8},{25... | collective-permute-start | bytes 258056 | tf_op jit(solution)/shard_map/ppermute | solution.py:37
  24.5 2.1 %copy-start = (bf16[50280,40]{0,1:T(8,128)(2,1)S(1)}, bf16[50280,40]{0,1:T(8,128)(2,1)}, u32[]{:S(2)}) copy-start(bf16[50280,40]{0,1:T(8,128)(2,1)} %param.21) | copy-start | bytes 12067204
  26.6 0.7 copy-start.7
  31.7 53.2 %copy-start.1 = (f32[2,128,128]{2,1,0:T(8,128)S(1)}, f32[2,128,128]{2,1,0:T(8,128)}, u32[]{:S(2)}) copy-start(f32[2,128,128]{2,1,0:T(8,128)} %get-tuple-element.31.refs_12_) | copy-start | bytes 393220
  31.7 53.2 %copy-start.2 = (bf16[2,64,384]{2,1,0:T(8,128)(2,1)S(1)}, bf16[2,64,384]{2,1,0:T(8,128)(2,1)}, u32[]{:S(2)}) copy-start(bf16[2,64,384]{2,1,0:T(8,128)(2,1)} %get-tuple-element.33.refs_14_) | copy-start | bytes 294916
  31.7 53.2 %copy-start.3 = (bf16[2,8,2560]{2,1,0:T(8,128)(2,1)S(1)}, bf16[2,8,2560]{2,1,0:T(8,128)(2,1)}, u32[]{:S(2)}) copy-start(bf16[2,8,2560]{2,1,0:T(8,128)(2,1)} %get-tuple-element.32.refs_13_) | copy-start | bytes 245764
  31.7 53.2 %copy-start.4 = (bf16[2,8,384]{2,1,0:T(8,128)(2,1)S(1)}, bf16[2,8,384]{2,1,0:T(8,128)(2,1)}, u32[]{:S(2)}) copy-start(bf16[2,8,384]{2,1,0:T(8,128)(2,1)} %get-tuple-element.34.refs_15_) | copy-start | bytes 36868
  31.8 53.2 %copy-start.5 = (s32[8,384]{1,0:T(8,128)S(1)}, s32[8,384]{1,0:T(8,128)}, u32[]{:S(2)}) copy-start(s32[8,384]{1,0:T(8,128)} %get-tuple-element.35.refs_16_) | copy-start | bytes 36868
  61.5 23.4 %collective-permute-start.6 = (bf16[32,8,2176]{2,1,0:T(8,128)(2,1)S(1)}, bf16[32,8,2176]{2,1,0:T(8,128)(2,1)S(1)}, u32[]{:S(2)}, u32[]{:S(2)}) collective-permute-start(bf16[32,8,2176]{2,1,0:T(8,128)(2,1)S(1)} %bitcast.23), channel_id=1, source_target_pairs={{0,1},{1,0},{2,3},{3,2},{4,5},{5,4},{6,7},{7,6},{8,9},{9,8},{10,11... | collective-permute-start | bytes 3342344 | tf_op jit(solution)/shard_map/ppermute | solution.py:41
  61.5 19.6 %collective-permute-start.9 = (bf16[8,8,2688]{2,1,0:T(8,128)(2,1)S(1)}, bf16[8,8,2688]{2,1,0:T(8,128)(2,1)S(1)}, u32[]{:S(2)}, u32[]{:S(2)}) collective-permute-start(bf16[8,8,2688]{2,1,0:T(8,128)(2,1)S(1)} %shard_map.212.refs_4_), channel_id=1, source_target_pairs={{192,0},{193,1},{194,2},{195,3},{196,4},{197,5},{198,6},{199,7},{2... | collective-permute-start | bytes 1032200 | tf_op jit(solution)/shard_map/ppermute | solution.py:37
  65.7 15.4 %collective-permute-start.8 = (bf16[8,8,2688]{2,1,0:T(8,128)(2,1)S(1)}, bf16[8,8,2688]{2,1,0:T(8,128)(2,1)S(1)}, u32[]{:S(2)}, u32[]{:S(2)}) collective-permute-start(bf16[8,8,2688]{2,1,0:T(8,128)(2,1)S(1)} %shard_map.212.refs_4_), channel_id=1, source_target_pairs={{128,0},{129,1},{130,2},{131,3},{132,4},{133,5},{134,6},{135,7},{1... | collective-permute-start | bytes 1032200 | tf_op jit(solution)/shard_map/ppermute | solution.py:37
  65.7 17.6 %collective-permute-start.7 = (bf16[8,8,2688]{2,1,0:T(8,128)(2,1)S(1)}, bf16[8,8,2688]{2,1,0:T(8,128)(2,1)S(1)}, u32[]{:S(2)}, u32[]{:S(2)}) collective-permute-start(bf16[8,8,2688]{2,1,0:T(8,128)(2,1)S(1)} %shard_map.212.refs_4_), channel_id=1, source_target_pairs={{64,0},{65,1},{66,2},{67,3},{68,4},{69,5},{70,6},{71,7},{72,8},{73... | collective-permute-start | bytes 1032200 | tf_op jit(solution)/shard_map/ppermute | solution.py:37
  67.8 15.5 %collective-permute-start.10 = (bf16[8,8,2688]{2,1,0:T(8,128)(2,1)S(1)}, bf16[8,8,2688]{2,1,0:T(8,128)(2,1)S(1)}, u32[]{:S(2)}, u32[]{:S(2)}) collective-permute-start(bf16[8,8,2688]{2,1,0:T(8,128)(2,1)S(1)} %shard_map.212.refs_4_), channel_id=1, source_target_pairs={{0,1},{1,0},{2,3},{3,2},{4,5},{5,4},{6,7},{7,6},{8,9},{9,8},{10,11... | collective-permute-start | bytes 1032200 | tf_op jit(solution)/shard_map/ppermute | solution.py:41
  81.1 2.2 %collective-permute-start.13 = (bf16[8,8,2688]{2,1,0:T(8,128)(2,1)S(1)}, bf16[8,8,2688]{2,1,0:T(8,128)(2,1)S(1)}, u32[]{:S(2)}, u32[]{:S(2)}) collective-permute-start(bf16[8,8,2688]{2,1,0:T(8,128)(2,1)S(1)} %collective-permute-done.9.refs_7_), channel_id=1, source_target_pairs={{0,1},{1,0},{2,3},{3,2},{4,5},{5,4},{6,7},{7,6},{8,9},{9,8},{10,11... | collective-permute-start | bytes 1032200 | tf_op jit(solution)/shard_map/ppermute | solution.py:41
  81.1 2.2 %collective-permute-start.12 = (bf16[8,8,2688]{2,1,0:T(8,128)(2,1)S(1)}, bf16[8,8,2688]{2,1,0:T(8,128)(2,1)S(1)}, u32[]{:S(2)}, u32[]{:S(2)}) collective-permute-start(bf16[8,8,2688]{2,1,0:T(8,128)(2,1)S(1)} %collective-permute-done.8.refs_6_), channel_id=1, source_target_pairs={{0,1},{1,0},{2,3},{3,2},{4,5},{5,4},{6,7},{7,6},{8,9},{9,8},{10,11... | collective-permute-start | bytes 1032200 | tf_op jit(solution)/shard_map/ppermute | solution.py:41
  83.3 1.7 collective-permute-start.11
  92.1 2.7 %collective-permute-start.14 = (bf16[4,41,8,384]{3,2,1,0:T(8,128)(2,1)S(1)}, bf16[4,41,8,384]{3,2,1,0:T(8,128)(2,1)S(1)}, u32[]{:S(2)}, u32[]{:S(2)}) collective-permute-start(bf16[4,41,8,384]{3,2,1,0:T(8,128)(2,1)S(1)} %get-tuple-element.37), channel_id=1, source_target_pairs={{0,1},{1,0},{2,3},{3,2},{4,5},{5,4},{6,7},{7,6},{8,9},{9,8},{10,11... | collective-permute-start | bytes 3022856 | tf_op jit(solution)/shard_map/ppermute | solution.py:41
  154.2 2.6 %collective-permute-start.15 = (bf16[32,8,1920]{2,1,0:T(8,128)(2,1)S(1)}, bf16[32,8,1920]{2,1,0:T(8,128)(2,1)S(1)}, u32[]{:S(2)}, u32[]{:S(2)}) collective-permute-start(bf16[32,8,1920]{2,1,0:T(8,128)(2,1)S(1)} %bitcast.28), channel_id=1, source_target_pairs={{0,1},{1,0},{2,3},{3,2},{4,5},{5,4},{6,7},{7,6},{8,9},{9,8},{10,11... | collective-permute-start | bytes 2949128 | tf_op jit(solution)/shard_map/ppermute | solution.py:41
  164.5 2.7 %collective-permute-start.16 = (bf16[4,41,8,384]{3,2,1,0:T(8,128)(2,1)S(1)}, bf16[4,41,8,384]{3,2,1,0:T(8,128)(2,1)S(1)}, u32[]{:S(2)}, u32[]{:S(2)}) collective-permute-start(bf16[4,41,8,384]{3,2,1,0:T(8,128)(2,1)S(1)} %get-tuple-element.42), channel_id=1, source_target_pairs={{0,1},{1,0},{2,3},{3,2},{4,5},{5,4},{6,7},{7,6},{8,9},{9,8},{10,11... | collective-permute-start | bytes 3022856 | tf_op jit(solution)/shard_map/ppermute | solution.py:41

commit v3 on v2

v3 whole, which is shorter than its diff:
```python
import jax
import jax.numpy as jnp
from jax import lax
from jax.experimental import pallas as pl
from jax.experimental.pallas import tpu as pltpu
from jax.sharding import PartitionSpec as P


LAYERS = 2
EPS = 1e-05
BF = jnp.bfloat16
F32 = jnp.float32
LANES = 128

YS, ZS, CS = 4, 8, 2


def device_at(y, z, c):
    return (y * ZS + z) * CS + c


Z_GROUPS = [[device_at(y, z, c) for z in range(ZS)] for y in range(YS) for c in range(CS)]
Y_GROUPS = [[device_at(y, z, c) for y in range(YS)] for z in range(ZS) for c in range(CS)]
PARTNER = [(i, i ^ 1) for i in range(YS * ZS * CS)]


PLACES = [(y, z, c) for y in range(YS) for z in range(ZS) for c in range(CS)]


def from_y(value, shift):
    pairs = [(device_at((y + shift) % YS, z, c), device_at(y, z, c)) for y, z, c in PLACES]
    return lax.ppermute(value, "heads", pairs)


def swap_cores(value):
    return lax.ppermute(value, "heads", PARTNER)


def exchange(value, groups):
    return lax.all_to_all(value, "heads", 0, 0, tiled=True, axis_index_groups=groups)


def spread(value, groups):
    count = len(groups[0])
    return exchange(jnp.broadcast_to(value[None], (count, *value.shape)), groups)


def gather_planes(piece, ring):
    rows, width = piece.shape
    half = ZS // 2
    over_z = spread(piece, Z_GROUPS)
    if ring:
        below = from_y(over_z, -1)
        above = from_y(over_z, 1)
        far_low = from_y(below[:half], -1)
        far_high = from_y(above[half:], 1)
        own = call(
            ring_join_kernel, jax.ShapeDtypeStruct((YS * ZS, rows, width), BF), 5
        )(over_z, below, above, far_low, far_high)
    else:
        own = spread(over_z, Y_GROUPS).reshape(YS * ZS, rows, width)
    return own, swap_cores(own)


def ring_join_kernel(here_ref, below_ref, above_ref, low_ref, high_ref, out_ref):
    y = position()[0]
    half = ZS // 2
    for shift, ref in ((0, here_ref), (1, above_ref), (3, below_ref)):
        out_ref[pl.ds(lax.rem(y + shift, YS) * ZS, ZS)] = ref[...]
    far = lax.rem(y + 2, YS) * ZS
    out_ref[pl.ds(far, half)] = low_ref[...]
    out_ref[pl.ds(far + half, half)] = high_ref[...]


VMEM = pl.BlockSpec(memory_space=pltpu.VMEM)
SMEM = pl.BlockSpec(memory_space=pltpu.SMEM)
HBM = pl.BlockSpec(memory_space=pltpu.HBM)


def limit(mib):
    return pltpu.CompilerParams(vmem_limit_bytes=mib * 1024 * 1024)


def silu(v):
    return v / (1.0 + jnp.exp(-v))


def softplus(v):
    e = jnp.exp(-jnp.abs(v))
    grown = 1.0 + e
    small = grown == 1.0
    log1p = jnp.where(small, e, jnp.log(grown) * (e / jnp.where(small, 1.0, grown - 1.0)))
    return jnp.maximum(v, 0.0) + log1p


SHIFT = LANES.bit_length() - 1


def position():
    at = lax.axis_index("heads")
    return at // (ZS * CS), at // CS % ZS, at % CS


def lookup_kernel(ids_ref, table_ref, out_ref, tail_ref, acc_ref):
    rows, vocab = table_ref.shape
    draft = ids_ref.shape[0]
    tokens = acc_ref.shape[1]
    whole = vocab // LANES
    tail_at = whole * LANES
    lane = lax.broadcasted_iota(jnp.int32, (rows, LANES), 1)
    tail_ref[...] = jnp.zeros_like(tail_ref)
    if tail_at < vocab:
        tail_ref[:, : vocab - tail_at] = table_ref[:, tail_at:].astype(F32)
    tail = tail_ref[...]
    seqs_a_tile = LANES // draft
    for tile in range(tokens // LANES):

        def one(s, acc, tile=tile):
            for t in range(draft):
                token = ids_ref[t, tile * seqs_a_tile + s]
                i = s * draft + t
                block = jnp.minimum(token >> SHIFT, whole - 1)
                at = pl.multiple_of(block << SHIFT, LANES)
                found = table_ref[:, pl.ds(at, LANES)].astype(F32)
                found = jnp.where(token >= tail_at, tail, found)
                moved = pltpu.roll(found, (i - token) & (LANES - 1), 1)
                acc = jnp.where(lane == i, moved, acc)
            return acc

        acc = lax.fori_loop(0, seqs_a_tile, one, jnp.zeros((rows, LANES), F32), unroll=2)
        acc_ref[:, tile * LANES : (tile + 1) * LANES] = acc
    for j in range(rows // 8):
        out_ref[:, j * tokens : (j + 1) * tokens] = acc_ref[8 * j : 8 * j + 8, :].astype(BF)


def lookup(ids, table):
    rows = table.shape[0]
    tokens = ids.size
    return pl.pallas_call(
        lookup_kernel,
        out_shape=jax.ShapeDtypeStruct((8, rows // 8 * tokens), BF),
        in_specs=[SMEM, VMEM],
        out_specs=VMEM,
        scratch_shapes=[pltpu.VMEM((rows, LANES), F32), pltpu.VMEM((rows, tokens), F32)],
        compiler_params=limit(12),
        name="lookup",
    )(ids, table)


def tdot(a, b):
    return lax.dot_general(a, b, (((0,), (0,)), ((), ())), preferred_element_type=F32)


def ndot(a, b):
    return lax.dot_general(a, b, (((1,), (1,)), ((), ())), preferred_element_type=F32)


def mdot(a, b):
    return lax.dot_general(a, b, (((1,), (0,)), ((), ())), preferred_element_type=F32)


SLOT = 64
AT_TAPS, AT_ACCEPTED, AT_BIAS, AT_RATE, AT_SKIP = 24, 32, 33, 34, 35


def saved_at(j, kept, seqs, draft):
    seq = lax.broadcasted_iota(jnp.int32, (seqs, seqs * draft), 0)
    at = lax.broadcasted_iota(jnp.int32, (seqs, seqs * draft), 1)
    return (at == seq * draft + (draft - kept) + j).astype(F32).astype(BF)


def setup_kernel(
    bias_ref, rate_ref, skip_ref, w_ref, wdt_ref, state_ref, taps_ref, tapb_ref, gain_ref,
    xtaps_ref, xtapb_ref, gate_ref, statex_ref, accepted_ref,
    vocab_ref,
    keep_ref, send_ref, table_ref, own8_ref, beforex_ref, beforebc_ref, spread_ref, near_ref,
    table, sem,
):
    bring = pltpu.make_async_copy(vocab_ref, near_ref, sem)
    bring.start()
    model = w_ref.shape[2]
    here = w_ref.shape[1]
    kept, seqs = state_ref.shape[1], state_ref.shape[3]
    draft = spread_ref.shape[1] // seqs
    taps = taps_ref.shape[1]
    width = xtaps_ref.shape[2]
    first = position()[2] == 0
    places = [saved_at(j, kept, seqs, draft) for j in range(kept)]
    outs, rows = [], []
    for layer in range(LAYERS):
        table[...] = jnp.zeros_like(table)
        table[0:taps, 0:here] = taps_ref[layer].astype(F32)
        table[taps : taps + 1, 0:here] = tapb_ref[layer : layer + 1].astype(F32)
        turned = jnp.transpose(table[...])[:8]
        tiles = []
        for j in range(kept):
            table[...] = jnp.zeros_like(table)
            table[0:here, 0:seqs] = state_ref[layer, j].astype(F32)
            tiles.append(table[0:8, :])
        outs.append((turned, tiles[0] + pltpu.roll(tiles[1], SLOT, 1), tiles[2]))
        row = w_ref[layer].astype(F32)
        rows.append(jnp.concatenate([row, jnp.zeros((8 - here, model), F32)], axis=0))
        own8_ref[layer] = jnp.concatenate(
            [row, wdt_ref[layer : layer + 1, :].astype(F32), jnp.zeros((7 - here, model), F32)], axis=0
        ).astype(BF)
    for ref, pick in ((keep_ref, first), (send_ref, jnp.logical_not(first))):
        for lo, values in (
            (0, rows),
            (model, [o[0] for o in outs]),
            (model + LANES, [o[1] for o in outs]),
            (model + 2 * LANES, [o[2] for o in outs]),
        ):
            value = jnp.where(pick, values[0], values[1])
            value = jnp.where(first, value, pltpu.roll(value, here, 0))
            ref[:, lo : lo + value.shape[1]] = value.astype(BF)
    for layer in range(LAYERS):
        table[...] = jnp.zeros_like(table)
        for j in range(model // LANES):
            table[j : j + 1, :] = gain_ref[layer : layer + 1, j * LANES : (j + 1) * LANES]
        table[AT_TAPS : AT_TAPS + taps, :width] = xtaps_ref[layer].astype(F32)
        table[AT_TAPS + taps : AT_TAPS + taps + 1, :width] = xtapb_ref[layer : layer + 1].astype(F32)
        table[AT_TAPS + taps + 1 : AT_TAPS + taps + 2, :width] = gate_ref[layer : layer + 1]
        table[AT_ACCEPTED : AT_ACCEPTED + 1, :seqs] = accepted_ref[...].astype(F32)
        table[AT_BIAS : AT_BIAS + 1, :] = jnp.broadcast_to(bias_ref[0:1, layer : layer + 1], (1, LANES))
        table[AT_RATE : AT_RATE + 1, :] = jnp.broadcast_to(rate_ref[0:1, layer : layer + 1], (1, LANES))
        table[AT_SKIP : AT_SKIP + 1, :] = jnp.broadcast_to(skip_ref[0:1, layer : layer + 1], (1, LANES))
        table_ref[layer] = jnp.transpose(table[...])
        beforex_ref[layer] = sum(tdot(statex_ref[layer, j], places[j]) for j in range(kept)).astype(BF)
        beforebc_ref[layer] = jnp.concatenate(
            [
                sum(mdot(state_ref[layer, j], places[j]) for j in range(kept)),
                jnp.zeros((8 - here, seqs * draft), F32),
            ],
            axis=0,
        ).astype(BF)
    seq = lax.broadcasted_iota(jnp.int32, (seqs, seqs * draft), 0)
    at = lax.broadcasted_iota(jnp.int32, (seqs, seqs * draft), 1)
    owner = (at // draft == seq).astype(F32).astype(BF)
    spread_ref[...] = mdot(
        jnp.broadcast_to(accepted_ref[...].astype(F32), (8, seqs)).astype(BF), owner
    ).astype(jnp.int32)
    bring.wait()


def pair_kernel(keep_ref, got_ref, rows_ref):
    rows_ref[...] = (keep_ref[...].astype(F32) + got_ref[...].astype(F32)).astype(BF)


def convolve(now, before, weights, bias, draft):
    tokens = now.shape[1]
    taps = len(weights)
    t0 = lax.broadcasted_iota(jnp.int32, (1, tokens), 1) % draft
    acc = None
    for k in range(taps):
        d = taps - 1 - k
        shifted = now
        if d:
            shifted = jnp.where(
                t0 >= d, pltpu.roll(now, d, 1), pltpu.roll(before, tokens - (draft - d), 1)
            )
        term = shifted * weights[k]
        acc = term if acc is None else acc + term
    return silu(acc + bias)


def make_project_kernel(layer, tokens, seqs, draft, own_cols, taps):
    model = own_cols * YS * ZS * CS
    pieces = own_cols // 8
    kept = taps - 1

    def kernel(
        own_ref, oth_ref, wown_ref, woth_ref, table_ref, own8_ref, nb_ref, mine_ref, bcc_ref, xs
    ):
        core = position()[2]
        first = core == 0
        turned = table_ref[layer]

        total = jnp.zeros((8, tokens), F32)
        for k in range(YS * ZS):
            for j in range(pieces):
                lanes = slice(j * tokens, (j + 1) * tokens)
                a = own_ref[k, :, lanes].astype(F32)
                b = oth_ref[k, :, lanes].astype(F32)
                total = total + a * a + b * b
                at = 2 * k * own_cols + 8 * j
                xs[at : at + 8, :] = jnp.where(first, a, b)
                xs[at + own_cols : at + own_cols + 8, :] = jnp.where(first, b, a)
        scale = lax.rsqrt(jnp.sum(total, axis=0, keepdims=True) / model + EPS)
        for j in range(model // LANES):
            at = slice(j * LANES, (j + 1) * LANES)
            nb_ref[at, :] = ((xs[at, :] * scale) * turned[:, j : j + 1]).astype(BF)

        take_own = core == layer
        count = ZS * 8
        rows = jnp.where(take_own, wown_ref[...].astype(F32), woth_ref[...].astype(F32)).reshape(
            count, model + 3 * LANES
        )
        left = jnp.concatenate([rows[:, :model], own8_ref[layer].astype(F32)], axis=0).astype(BF)
        out = mdot(left, nb_ref[...]).astype(BF)
        mine_ref[...] = out[count:]
        slot = lax.broadcasted_iota(jnp.int32, (2 * LANES, tokens), 0)
        slot_lane = lax.broadcasted_iota(jnp.int32, (2 * LANES, tokens), 1)
        slot_seq, slot_j = slot & (SLOT - 1), slot // SLOT
        place = (
            (slot_seq < seqs) & (slot_j < kept) & (slot_lane == slot_seq * draft + (draft - kept) + slot_j)
        ).astype(F32).astype(BF)
        before = mdot(rows[:, model + LANES :].astype(BF), place)
        extra = rows[:, model : model + LANES]
        bcc = convolve(
            out[:count].astype(F32),
            before,
            [extra[:, k : k + 1] for k in range(taps)],
            extra[:, taps : taps + 1],
            draft,
        )
        bcc_ref[...] = bcc.astype(BF)

    return kernel


def make_values_kernel(layer, tokens, seqs, draft, taps, last):
    kept = taps - 1

    def kernel(*refs):
        (
            nb_ref, mine_ref, table_ref, beforex_ref, beforebc_ref, spread_ref, zx_ref, *rest,
        ) = refs
        if last:
            old_x_ref, old_bc_ref, *rest = rest
        gate_ref, xc_ref, rows_ref, newx_ref, newbc_ref, zx_w, sem = rest
        load_w = pltpu.make_async_copy(zx_ref.at[layer], zx_w, sem)
        load_w.start()
        turned = table_ref[layer]
        width = beforex_ref.shape[1]
        here = newbc_ref.shape[-2]
        acc_col = turned[:seqs, AT_ACCEPTED : AT_ACCEPTED + 1].astype(jnp.int32)
        cols = turned[:width, AT_TAPS : AT_TAPS + 8]
        bias_dt = turned[:1, AT_BIAS : AT_BIAS + 1]
        rate = turned[:1, AT_RATE : AT_RATE + 1]
        lane = lax.broadcasted_iota(jnp.int32, (1, tokens), 1)
        t0 = lane % draft
        mine = mine_ref[...]
        before_b, before_mb = beforex_ref[layer], beforebc_ref[layer]

        step = softplus(mine[here : here + 1, :].astype(F32) + bias_dt)
        cum = step
        for d in (1, 2, 4):
            cum = cum + jnp.where(t0 >= d, pltpu.roll(cum, d, 1), 0.0)
        accepted = spread_ref[:1]
        cut = jnp.where(t0 < accepted, step, 0.0)
        for d in (1, 2, 4):
            cut = cut + jnp.where((t0 & d) != 0, pltpu.roll(cut, d, 1), pltpu.roll(cut, tokens - d, 1))
        weight = jnp.where(t0 < accepted, jnp.exp(-rate * (cut - cum)) * step, 0.0)
        rows = (step, cum, jnp.exp(-rate * cum), jnp.exp(-rate * cut), weight)
        for i, row in enumerate(rows):
            rows_ref[i : i + 1, :] = row
        rows_ref[len(rows) :, :] = jnp.zeros((8 - len(rows), tokens), F32)

        load_w.wait()
        zx = tdot(zx_w[...], nb_ref[...]).astype(BF)
        gate_ref[...] = silu(zx[:width].astype(F32))
        values_b = zx[width:]
        xc_ref[...] = convolve(
            values_b.astype(F32),
            before_b.astype(F32),
            [cols[:, k : k + 1] for k in range(taps)],
            cols[:, taps : taps + 1],
            draft,
        )

        seq = lax.broadcasted_iota(jnp.int32, (seqs, tokens), 0)
        at = lax.broadcasted_iota(jnp.int32, (seqs, tokens), 1)
        for i in range(kept):
            row = acc_col + i
            new = ((at == seq * draft + row - kept) & (row >= kept)).astype(F32).astype(BF)
            old = ((at == seq * draft + (draft - kept) + row) & (row < kept)).astype(F32).astype(BF)
            rows_x = (ndot(new, values_b) + ndot(old, before_b)).astype(BF)
            rows_bc = (ndot(mine, new) + ndot(before_mb, old))[:here].astype(BF)
            if last:
                newx_ref[layer, i], newbc_ref[layer, i] = rows_x, rows_bc
                for l in range(layer):
                    newx_ref[l, i], newbc_ref[l, i] = old_x_ref[i], old_bc_ref[i]
            else:
                newx_ref[i], newbc_ref[i] = rows_x, rows_bc

    return kernel


def make_recur_kernel(layer, tokens, draft, own_cols, taps, last):
    pieces = own_cols // 8

    def kernel(*refs):
        got_refs = refs[:YS]
        gate_ref, xc_ref, rows_ref, table_ref, outw_ref, ssm_ref, *rest = refs[YS:]
        if last:
            _, *rest = rest
        keep_ref, send_ref, newssm_ref, h_in, h_out, xw_all, out_w, channels, sems = rest
        y_here, _, core = position()
        first = core == 0
        tiles = xc_ref.shape[1] // LANES
        part = h_in.shape[0] // tiles
        loads = []
        for i in range(tiles):
            at = pl.ds(i * part, part)
            loads.append(pltpu.make_async_copy(ssm_ref.at[layer, at], h_in.at[at], sems.at[i]))
            loads[-1].start()
        load_o = pltpu.make_async_copy(outw_ref.at[layer], out_w, sems.at[tiles])
        load_o.start()
        turned = table_ref[layer]
        width = xc_ref.shape[0]
        rate = turned[:1, AT_RATE : AT_RATE + 1]
        skip = turned[:1, AT_SKIP : AT_SKIP + 1]
        gain = turned[:width, AT_TAPS + taps + 1 : AT_TAPS + taps + 2]
        xc = xc_ref[...]
        step, cum, fall, fall_cut, weight = [rows_ref[i : i + 1, :] for i in range(5)]
        for d, ref in enumerate(got_refs):
            channels[lax.rem(y_here + d, YS)] = ref[...].astype(F32)
        bcc = channels[...].reshape(-1, xc_ref.shape[1]).astype(BF)
        states = bcc.shape[0] // 2
        xb = xc.astype(BF)
        xw_all[...] = (xc * weight).astype(BF)

        per_tile = LANES // draft
        sub = lax.broadcasted_iota(jnp.int32, (LANES, LANES), 0)
        lan = lax.broadcasted_iota(jnp.int32, (LANES, LANES), 1)
        causal = (sub // draft == lan // draft) & (sub <= lan)
        group = lax.broadcasted_iota(jnp.int32, (1, LANES), 1) // draft
        pick16 = lax.broadcasted_iota(jnp.int32, (per_tile, LANES), 0) * draft == (
            lax.broadcasted_iota(jnp.int32, (per_tile, LANES), 1)
        )
        parts = []
        for tile in range(tokens // LANES):
            ls = slice(tile * LANES, (tile + 1) * LANES)
            bmat = bcc[:states, ls]
            cmat = bcc[states:, ls]
            cum_r = jnp.broadcast_to(cum[:, ls], (LANES, LANES))
            step_c = jnp.transpose(jnp.broadcast_to(step[:, ls], (LANES, LANES)))
            cum_c = jnp.transpose(cum_r)
            gram = tdot(bmat, cmat)
            within = jnp.where(causal, gram * (jnp.exp(-rate * (cum_r - cum_c)) * step_c), 0.0)
            y_new = mdot(xb[:, ls], within.astype(BF))
            y_old = jnp.zeros((width, LANES), F32)
            falls = jnp.sum(jnp.where(pick16, fall_cut[:, ls], 0.0), axis=1, keepdims=True)
            xw = xw_all[:, ls]
            loads[tile].wait()
            for s in range(per_tile):
                n = tile * per_tile + s
                h0 = h_in[n]
                here = group == s
                y_old = jnp.where(here, mdot(h0.astype(BF), cmat), y_old)
                add = ndot(jnp.where(here, xw, jnp.zeros_like(xw)), bmat)
                h_out[n] = h0 * falls[s : s + 1, :] + add
            parts.append(fall[:, ls] * y_old + y_new)
        store = pltpu.make_async_copy(h_out, newssm_ref.at[layer], sems.at[tiles + 1])
        store.start()
        y = jnp.concatenate(parts, axis=1) + skip * xc
        gated = y * gate_ref[...]
        ssq = jnp.sum(gated * gated, axis=0, keepdims=True)
        u = (gated * gain).astype(BF)

        high = ssq.astype(BF)
        low = (ssq - high.astype(F32)).astype(BF)
        row8 = lax.broadcasted_iota(jnp.int32, (8, tokens), 0)
        tail = jnp.where(row8 == 0, high.astype(F32), jnp.where(row8 == 1, low.astype(F32), 0.0))
        block = own_cols * CS * ZS
        load_o.wait()
        for y_at in range(YS):
            out = tdot(out_w[:, y_at * block : (y_at + 1) * block], u)
            out = out.reshape(ZS, CS, pieces, 8, tokens)
            for z in range(ZS):
                even, odd = out[z, 0], out[z, 1]
                rows = slice(z * pieces, (z + 1) * pieces)
                keep_ref[y_at, rows] = jnp.where(first, even, odd)
                send_ref[y_at, rows] = jnp.where(first, odd, even).astype(BF)
            keep_ref[y_at, ZS * pieces] = tail
            send_ref[y_at, ZS * pieces] = tail.astype(BF)
        store.wait()

    return kernel


def add_cores_kernel(keep_ref, got_ref, *out_refs):
    tiles = keep_ref.shape[1]
    y = position()[0]
    tail = split_tail(keep_ref[0, tiles - 1] + got_ref[0, tiles - 1].astype(F32))
    for shift, out_ref in enumerate(out_refs):
        at = lax.rem(y + shift, YS)
        out_ref[: tiles - 1] = (
            keep_ref[at, : tiles - 1] + got_ref[at, : tiles - 1].astype(F32)
        ).astype(BF)
        out_ref[tiles - 1] = tail


def split_tail(tail):
    row8 = lax.broadcasted_iota(jnp.int32, tail.shape, 0)
    ssq = tail[0:1] + tail[1:2]
    high = ssq.astype(BF).astype(F32)
    return jnp.where(row8 == 0, high, jnp.where(row8 == 1, ssq - high, 0.0)).astype(BF)


def add_y_kernel(*refs):
    *got_refs, out_ref = refs
    tiles = got_refs[0].shape[0]
    pieces = (tiles - 1) // ZS

    def summed(rows):
        acc = got_refs[0][rows].astype(F32)
        for ref in got_refs[1:]:
            acc = acc + ref[rows].astype(F32)
        return acc

    tail = split_tail(summed(slice(tiles - 1, tiles))[0])
    for z in range(ZS):
        out_ref[z, :pieces] = summed(slice(z * pieces, (z + 1) * pieces)).astype(BF)
        out_ref[z, pieces] = tail


def make_finish_kernel(inner, last):
    def finish_kernel(got_ref, stream_ref, out_ref):
        tiles = got_ref.shape[1]
        tokens = got_ref.shape[3]
        acc = got_ref[0].astype(F32)
        for z in range(1, ZS):
            acc = acc + got_ref[z].astype(F32)
        ssq = acc[tiles - 1, 0:1] + acc[tiles - 1, 1:2]
        scale = lax.rsqrt(ssq / inner + EPS)
        for j in range(tiles - 1):
            lanes = slice(j * tokens, (j + 1) * tokens)
            new = (stream_ref[:, lanes].astype(F32) + acc[j] * scale).astype(BF)
            if last:
                out_ref[j] = new
            else:
                out_ref[:, lanes] = new

    return finish_kernel


def call(kernel, out_shape, count):
    return pl.pallas_call(
        kernel,
        out_shape=out_shape,
        in_specs=[VMEM] * count,
        out_specs=jax.tree.map(lambda _: VMEM, out_shape),
        compiler_params=limit(10),
    )


def local(
    draft_ids,
    accepted,
    embedding,
    norm_gain,
    w_zx,
    w_dt,
    w_bc,
    dt_bias,
    decay_rate,
    skip_weight,
    conv_x_w,
    conv_x_b,
    conv_bc_w,
    conv_bc_b,
    gate_gain,
    out_w,
    ssm_state,
    conv_x_state,
    conv_bc_state,
):
    seqs, draft = draft_ids.shape
    tokens = seqs * draft
    own_cols = embedding.shape[1]
    model = own_cols * YS * ZS * CS
    width = w_zx.shape[3] // 2
    inner = width * YS * ZS * CS
    bc_here = w_bc.shape[2]
    taps = conv_x_w.shape[1]
    kept = taps - 1
    pieces = own_cols // 8
    states = ssm_state.shape[4]

    tokens_ids = draft_ids.T
    state_shape = (LAYERS, seqs, width, states)

    w_rows = jnp.swapaxes(w_bc, 1, 2)
    row_shape = jax.ShapeDtypeStruct((8, model + 3 * LANES), BF)
    keep, send, table, own8, before_x, before_bc, spread_acc, vocab = pl.pallas_call(
        setup_kernel,
        out_shape=(
            row_shape,
            row_shape,
            jax.ShapeDtypeStruct((LAYERS, LANES, LANES), F32),
            jax.ShapeDtypeStruct((LAYERS, 8, model), BF),
            jax.ShapeDtypeStruct((LAYERS, width, tokens), BF),
            jax.ShapeDtypeStruct((LAYERS, 8, tokens), BF),
            jax.ShapeDtypeStruct((8, tokens), jnp.int32),
            jax.ShapeDtypeStruct(embedding.shape[::-1], BF),
        ),
        in_specs=[VMEM] * 14 + [HBM],
        out_specs=(VMEM,) * 8,
        scratch_shapes=[pltpu.VMEM((LANES, LANES), F32), pltpu.SemaphoreType.DMA],
        compiler_params=limit(16),
        name="setup",
    )(
        *[
            pltpu.with_memory_space_constraint(v, pltpu.HBM)
            for v in (
                *[v.reshape(1, LAYERS) for v in (dt_bias, decay_rate, skip_weight)],
                w_rows,
                w_dt.reshape(LAYERS, model),
                jnp.transpose(conv_bc_state, (0, 2, 3, 1)),
                conv_bc_w,
                conv_bc_b,
                norm_gain,
                conv_x_w,
                conv_x_b,
                gate_gain,
                jnp.swapaxes(conv_x_state, 1, 2),
                accepted.reshape(1, seqs),
                embedding.T,
            )
        ],
    )
    pair_rows = call(pair_kernel, row_shape, 2)(keep, swap_cores(send))
    stream = lookup(tokens_ids, vocab)
    w_own = spread(pair_rows, Z_GROUPS)
    w_oth = swap_cores(w_own)
    own, oth = gather_planes(stream, True)

    zx_w, outer_w, state_in = [
        pltpu.with_memory_space_constraint(v, pltpu.HBM)
        for v in (w_zx.reshape(LAYERS, model, 2 * width), out_w, ssm_state.reshape(state_shape))
    ]
    saved, saved_ssm = (), ()
    tiles = ZS * pieces + 1
    for layer in range(LAYERS):
        last = layer + 1 == LAYERS
        lead = (LAYERS,) if last else ()
        normed, mine, bcc = pl.pallas_call(
            make_project_kernel(layer, tokens, seqs, draft, own_cols, taps),
            out_shape=(
                jax.ShapeDtypeStruct((model, tokens), BF),
                jax.ShapeDtypeStruct((8, tokens), BF),
                jax.ShapeDtypeStruct((ZS * 8, tokens), BF),
            ),
            in_specs=[VMEM] * 6,
            out_specs=(VMEM,) * 3,
            scratch_shapes=[pltpu.VMEM((model, tokens), F32)],
            compiler_params=limit(20),
        )(own, oth, w_own, w_oth, table, own8)
        got = [bcc] + [from_y(bcc, d) for d in range(1, YS)]
        gate, xc, rows, *saved = pl.pallas_call(
            make_values_kernel(layer, tokens, seqs, draft, taps, last),
            out_shape=(
                jax.ShapeDtypeStruct((width, tokens), F32),
                jax.ShapeDtypeStruct((width, tokens), F32),
                jax.ShapeDtypeStruct((8, tokens), F32),
                jax.ShapeDtypeStruct((*lead, kept, seqs, width), BF),
                jax.ShapeDtypeStruct((*lead, kept, bc_here, seqs), BF),
            ),
            in_specs=[VMEM] * 6 + [HBM] + [VMEM] * len(saved),
            out_specs=(VMEM,) * 5,
            scratch_shapes=[
                pltpu.VMEM((model, 2 * width), BF),
                pltpu.SemaphoreType.DMA,
            ],
            compiler_params=limit(16),
            cost_estimate=pl.CostEstimate(
                flops=2 * model * tokens * 4 * width, bytes_accessed=4 << 20, transcendentals=0
            ),
        )(
            normed, mine, table, before_x, before_bc, spread_acc, zx_w, *saved
        )
        keep, send, *saved_ssm = pl.pallas_call(
            make_recur_kernel(layer, tokens, draft, own_cols, taps, last),
            out_shape=(
                jax.ShapeDtypeStruct((YS, tiles, 8, tokens), F32),
                jax.ShapeDtypeStruct((YS, tiles, 8, tokens), BF),
                jax.ShapeDtypeStruct(state_shape, F32),
            ),
            in_specs=[VMEM] * 8 + [HBM] * (2 + len(saved_ssm)),
            out_specs=(VMEM, VMEM, HBM),
            scratch_shapes=[
                pltpu.VMEM(state_shape[1:], F32),
                pltpu.VMEM(state_shape[1:], F32),
                pltpu.VMEM((width, tokens), BF),
                pltpu.VMEM((width, model), BF),
                pltpu.VMEM((YS, ZS * 8, tokens), F32),
                pltpu.SemaphoreType.DMA((tokens // LANES + 2,)),
            ],
            input_output_aliases={10: 2} if last else {},
            compiler_params=limit(24),
        )(*got, gate, xc, rows, table, outer_w, state_in, *saved_ssm)
        block = jax.ShapeDtypeStruct((tiles, 8, tokens), BF)
        here, *blocks = call(add_cores_kernel, (block,) * YS, 2)(keep, swap_cores(send))
        got = {d: from_y(blocks[d - 1], -d) for d in (2, 1, 3)}
        summed = call(
            add_y_kernel, jax.ShapeDtypeStruct((ZS, pieces + 1, 8, tokens), BF), YS
        )(here, *[got[d] for d in range(1, YS)])
        shape = (pieces, 8, tokens) if last else (8, pieces * tokens)
        stream = call(
            make_finish_kernel(inner, last), jax.ShapeDtypeStruct(shape, BF), 2
        )(exchange(summed, Z_GROUPS), stream)
        if not last:
            own, oth = gather_planes(stream, False)
    (new_x, new_bc), (new_ssm,) = saved, saved_ssm
    hidden = stream.reshape(own_cols, tokens).T
    kept_x = jnp.swapaxes(new_x, 1, 2)
    kept_bc = jnp.transpose(new_bc, (0, 3, 1, 2))
    return (hidden, new_ssm.reshape(ssm_state.shape), kept_x, kept_bc)


def solution(mesh):
    placed = (
        P("batch", None),
        P("batch"),
        P(None, "heads"),
        P(),
        P(None, None, "heads", None),
        P(None, None, "heads"),
        P(None, None, "heads"),
        P(None, "heads"),
        P(None, "heads"),
        P(None, "heads"),
        P(None, None, "heads"),
        P(None, "heads"),
        P(None, None, "heads"),
        P(None, "heads"),
        P(None, "heads"),
        P(None, "heads", None),
        P(None, "batch", "heads", None, None),
        P(None, "batch", None, "heads"),
        P(None, "batch", None, "heads"),
    )
    return jax.shard_map(
        local,
        mesh=mesh,
        in_specs=placed,
        out_specs=(
            P("batch", "heads"),
            P(None, "batch", "heads", None, None),
            P(None, "batch", None, "heads"),
            P(None, "batch", None, "heads"),
        ),
        check_vma=False,
    )
```

time: 201 us -> 190 us (0.945)
  blocking collectives: 121 us -> 80.7 us
  waiting for transfers between devices: 29.9 us -> 53.5 us
  starting transfers between devices: 22.5 us -> 28.2 us
  local copies, waits for them, and re-layouts: 3.84 us -> 0.91 us
  Pallas kernels: 22.6 us -> 24.9 us
    all_to_all x8 -> x5, blocking collectives: 121 us -> 80.7 us  [exchange(): lax.all_to_all(value, 'heads', 0, 0, tiled=True, axis_index_groups=groups)]
    all_to_all x0 -> x1, waiting for transfers between devices: none -> 14.1 us  [exchange(): lax.all_to_all(value, 'heads', 0, 0, tiled=True, axis_index_groups=groups)]
    ppermute x8 -> x16, waiting for transfers between devices: 19.3 us -> 28.7 us  [from_y(): return lax.ppermute(value, 'heads', pairs)]
    unnamed x16 -> x2, local copies, waits for them, and re-layouts: 3.64 us -> 0.01 us
    all_to_all x0 -> x1, starting transfers between devices: none -> 3.45 us  [exchange(): lax.all_to_all(value, 'heads', 0, 0, tiled=True, axis_index_groups=groups)]
    ppermute x8 -> x16, starting transfers between devices: 21.4 us -> 24.3 us  [from_y(): return lax.ppermute(value, 'heads', pairs)]
    pallas_call x9 -> x12, Pallas kernels: 15.6 us -> 16.7 us  [the longest x2 8.39 us: local(): pl.pallas_call(make_recur_kernel(layer, tokens, draft, own_cols, taps, la...]
    ppermute x9 -> x6, waiting for transfers between devices: 10.6 us -> 10.6 us  [swap_cores(): return lax.ppermute(value, 'heads', PARTNER)]
  transfers between devices with their start and end apart: 17 -> 23, of which waited for: 9 -> 15; matrix products, arithmetic and copies ran while one was open for 0% -> 0% of each run, Pallas kernels for 2% -> 2%
where the time goes in v3:
time: 190 us; the launch traced here: 189 us
  blocking collectives  80.7 us (42%)
  waiting for transfers between devices  53.5 us (28%)
  starting transfers between devices  28.2 us (15%)
  Pallas kernels  24.9 us (13%)
    all_to_all x5, blocking collectives, exchange(): lax.all_to_all(value, 'heads', 0, 0, tiled=True, axis_index_groups=groups)  80.7 us
    ppermute x16, waiting for transfers between devices, from_y(): return lax.ppermute(value, 'heads', pairs)  28.7 us
    ppermute x16, starting transfers between devices, from_y(): return lax.ppermute(value, 'heads', pairs)  24.3 us
    all_to_all x1, waiting for transfers between devices, exchange(): lax.all_to_all(value, 'heads', 0, 0, tiled=True, axis_index_groups=groups)  14.1 us
    ppermute x6, waiting for transfers between devices, swap_cores(): return lax.ppermute(value, 'heads', PARTNER)  10.6 us
    pallas_call x2, Pallas kernels, local(): pl.pallas_call(make_recur_kernel(layer, tokens, draft, own_cols, taps, la...  8.39 us
    pallas_call x2, Pallas kernels, local(): pl.pallas_call(make_values_kernel(layer, tokens, seqs, draft, taps, last)...  4.63 us
    pallas_call x1, Pallas kernels, lookup(): pl.pallas_call(lookup_kernel, out_shape=jax.ShapeDtypeStruct((8, rows //...  4.3 us
  transfers between devices with their start and end apart: 23, of which 15 were waited for; matrix products, arithmetic and copies ran while one was open for 0% of the time, Pallas kernels for 2%

profile of v3, /device:TPU:2, one launch (start us, length us, event | category | flops | bytes accessed | tf_op | source)
XLA Modules:
  0.0 189.1 jit_solution(10888681494675712705)
XLA Ops:
  0.6 3.2 %setup.1 = (bf16[8,2944]{1,0:T(8,128)(2,1)S(1)}, bf16[8,2944]{1,0:T(8,128)(2,1)S(1)}, f32[2,128,128]{2,1,0:T(8,128)S(1)}, bf16[2,8,2560]{2,1,0:T(8,128)(2,1)S(1)...) custom-call(f32[1,2]{1,0:T(1,128)} %bitcast.35, ...), custom_call_target="tpu_custom_call" | custom-call | tf_op jit(solution)/shard_map/setup/pallas_call | solution.py:586
  3.9 4.3 %lookup.1.stream_ref = bf16[8,1920]{1,0:T(8,128)(2,1)S(1)} custom-call(s32[8,48]{1,0:T(8,128)S(1)} %bitcast.23, bf16[40,50280]{1,0:T(8,128)(2,1)S(1)} %get-tuple-element.42.table_ref), custom_call_target="tpu_custom_call" | custom-call | tf_op jit(solution)/shard_map/lookup/pallas_call | solution.py:139
  8.2 19.8 %all_to_all.30.here_ref = bf16[8,8,1920]{2,1,0:T(8,128)(2,1)S(1)} all-to-all(bf16[8,8,1920]{2,1,0:T(8,128)(2,1)S(1)} %broadcast_in_dim.8), channel_id=1, replica_groups={{0,2,4,6,8,10,12,14},{1,3,5,7,9,11,13,15},{16,18,20,22,24,26,28,30},{17..., dimensions={0} | all-to-all | bytes 491520 | tf_op jit(solution)/shard_map/all_to_all | solution.py:40
  28.0 3.0 %collective-permute-start.1 = (bf16[8,8,1920]{2,1,0:T(8,128)(2,1)S(1)}, bf16[8,8,1920]{2,1,0:T(8,128)(2,1)S(1)}, u32[]{:S(2)}, u32[]{:S(2)}) collective-permute-start(bf16[8,8,1920]{2,1,0:T(8,128)(2,1)S(1)} %all_to_all.30.here_ref), channel_id=1, source_target_pairs={{16,0},{17,1},{18,2},{19,3},{20,4},{21,5},{22,6},{23,7},{24,8},{25... | collective-permute-start | bytes 737288 | tf_op jit(solution)/shard_map/ppermute | solution.py:32
  31.0 3.7 %collective-permute-done.1.above_ref = bf16[8,8,1920]{2,1,0:T(8,128)(2,1)S(1)} collective-permute-done((bf16[8,8,1920]{2,1,0:T(8,128)(2,1)S(1)}, bf16[8,8,1920]{2,1,0:T(8,128)(2,1)S(1)}, u32[]{:S(2)}, u32[]{:S(2)}) %collective-permute-start.1) | collective-permute-done | bytes 245792 | tf_op jit(solution)/shard_map/ppermute | solution.py:32
  34.8 3.8 %collective-permute-start.3 = (bf16[4,8,1920]{2,1,0:T(8,128)(2,1)S(1)}, bf16[4,8,1920]{2,1,0:T(8,128)(2,1)S(1)}, u32[]{:S(2)}, u32[]{:S(2)}) collective-permute-start(bf16[4,8,1920]{2,1,0:T(8,128)(2,1)S(1)} %slice.9), channel_id=1, source_target_pairs={{16,0},{17,1},{18,2},{19,3},{20,4},{21,5},{22,6},{23,7},{24,8},{25... | collective-permute-start | bytes 368648 | tf_op jit(solution)/shard_map/ppermute | solution.py:32
  38.6 0.1 collective-permute-start.5
  38.7 1.2 collective-permute-done.5.got_ref
  40.0 0.8 broadcast_in_dim.9
  40.7 3.4 %all-to-all-start.1 = ((bf16[8,8,2944]{2,1,0:T(8,128)(2,1)}), bf16[8,8,2944]{2,1,0:T(8,128)(2,1)S(1)}, u32[]{:S(2)}, u32[]{:S(2)}) async-start(bf16[8,8,2944]{2,1,0:T(8,128)(2,1)} %broadcast_in_dim.9), calls=%async_computation.1 | async-start | bytes 753664 | tf_op jit(solution)/shard_map/all_to_all | solution.py:40
  44.2 0.5 collective-permute-done.2.low_ref
  44.8 0.1 collective-permute-start.4
  44.9 14.1 %all-to-all-done.1.wown_ref = bf16[8,8,2944]{2,1,0:T(8,128)(2,1)S(1)} async-done(((bf16[8,8,2944]{2,1,0:T(8,128)(2,1)}), bf16[8,8,2944]{2,1,0:T(8,128)(2,1)S(1)}, u32[]{:S(2)}, u32[]{:S(2)}) %all-to-all-start.1) | async-done | bytes 376864 | tf_op jit(solution)/shard_map/all_to_all | solution.py:40
  59.1 1.7 collective-permute-done.6.woth_ref
  60.8 1.4 shard_map.212
  62.3 4.6 %collective-permute-start.8 = (bf16[64,384]{1,0:T(8,128)(2,1)S(1)}, bf16[64,384]{1,0:T(8,128)(2,1)S(1)}, u32[]{:S(2)}, u32[]{:S(2)}) collective-permute-start(bf16[64,384]{1,0:T(8,128)(2,1)S(1)} %get-tuple-element.47.refs_0_), channel_id=1, source_target_pairs={{32,0},{33,1},{34,2},{35,3},{36,4},{37,5},{38,6},{39,7},{40,8},{41... | collective-permute-start | bytes 147464 | tf_op jit(solution)/shard_map/ppermute | solution.py:32
  66.9 1.9 %shard_map.213 = (f32[64,384]{1,0:T(8,128)S(1)}, f32[64,384]{1,0:T(8,128)S(1)}, f32[8,384]{1,0:T(8,128)S(1)}, bf16[3,48,64]{2,1,0:T(8,128)(2,1)S(1)}, bf16[3,4,48]{2,1,0:T(4,128)(2,1)S(1)}) custom-call(bf16[2560,384]{1,0:T(8,128)(2,1)S(1)} %get-tuple-element.48.refs_0_, bf16[8,384]{1,0:T(8,128)(2,1)S(1)} %get-tuple-element.49.refs_1_, ...), custom_call_target="tpu_custom_call" | custom-call | flops 503316480 | bytes 4194304 | tf_op jit(solution)/shard_map/pallas_call | solution.py:651
  68.8 0.9 collective-permute-done.8.refs_2_
  69.7 1.3 collective-permute-done.7.refs_1_
  70.9 4.2 %shard_map.214 = (f32[4,41,8,384]{3,2,1,0:T(8,128)S(1)}, bf16[4,41,8,384]{3,2,1,0:T(8,128)(2,1)S(1)}, f32[2,48,64,128]{3,2,1,0:T(8,128)}) custom-call(bf16[64,384]{1,0:T(8,128)(2,1)S(1)} %get-tuple-element.47.refs_0_, bf16[64,384]{1,0:T(8,128)(2,1)S(1)} %collective-permute-done.7.refs_1_, bf16[64,384]{1,0:T(8,128)(2,1)S(1)} %collective-permute-done.8.refs_2_, ...), custom_call_target="tpu_custom_call" | custom-call | tf_op jit(solution)/shard_map/pallas_call | solution.py:673
  75.2 2.6 %collective-permute-done.10.got_ref = bf16[4,41,8,384]{3,2,1,0:T(8,128)(2,1)S(1)} collective-permute-done((bf16[4,41,8,384]{3,2,1,0:T(8,128)(2,1)S(1)}, bf16[4,41,8,384]{3,2,1,0:T(8,128)(2,1)S(1)}, u32[]{:S(2)}, u32[]{:S(2)}) %collective-permute-start.10) | collective-permute-done | bytes 1007648 | tf_op jit(solution)/shard_map/ppermute | solution.py:36
  77.8 0.2 shard_map.215
  78.1 2.7 %collective-permute-start.12 = (bf16[41,8,384]{2,1,0:T(8,128)(2,1)S(1)}, bf16[41,8,384]{2,1,0:T(8,128)(2,1)S(1)}, u32[]{:S(2)}, u32[]{:S(2)}) collective-permute-start(bf16[41,8,384]{2,1,0:T(8,128)(2,1)S(1)} %get-tuple-element.60), channel_id=1, source_target_pairs={{32,0},{33,1},{34,2},{35,3},{36,4},{37,5},{38,6},{39,7},{40,8},{41... | collective-permute-start | bytes 755720 | tf_op jit(solution)/shard_map/ppermute | solution.py:32
  80.8 1.5 collective-permute-start.13
  82.3 10.6 %collective-permute-done.11.refs_1_ = bf16[41,8,384]{2,1,0:T(8,128)(2,1)S(1)} collective-permute-done((bf16[41,8,384]{2,1,0:T(8,128)(2,1)S(1)}, bf16[41,8,384]{2,1,0:T(8,128)(2,1)S(1)}, u32[]{:S(2)}, u32[]{:S(2)}) %collective-permute-start.11) | collective-permute-done | bytes 251936 | tf_op jit(solution)/shard_map/ppermute | solution.py:32
  92.9 0.6 collective-permute-done.13.refs_3_
  93.5 0.1 shard_map.216
  93.6 14.4 %all_to_all.31.got_ref = bf16[8,6,8,384]{3,2,1,0:T(8,128)(2,1)S(1)} all-to-all(bf16[8,6,8,384]{3,2,1,0:T(8,128)(2,1)S(1)} %shard_map.216), channel_id=1, replica_groups={{0,2,4,6,8,10,12,14},{1,3,5,7,9,11,13,15},{16,18,20,22,24,26,28,30},{17..., dimensions={0} | all-to-all | bytes 589824 | tf_op jit(solution)/shard_map/all_to_all | solution.py:40
  108.1 12.7 %all_to_all.32 = bf16[8,8,1920]{2,1,0:T(8,128)(2,1)S(1)} all-to-all(bf16[8,8,1920]{2,1,0:T(8,128)(2,1)S(1)} %broadcast_in_dim.10), channel_id=1, replica_groups={{0,2,4,6,8,10,12,14},{1,3,5,7,9,11,13,15},{16,18,20,22,24,26,28,30},{17..., dimensions={0} | all-to-all | bytes 491520 | tf_op jit(solution)/shard_map/all_to_all | solution.py:40
  120.9 19.1 %all_to_all.33 = bf16[4,8,8,1920]{3,2,1,0:T(8,128)(2,1)S(1)} all-to-all(bf16[4,8,8,1920]{3,2,1,0:T(8,128)(2,1)S(1)} %broadcast_in_dim.11), channel_id=1, replica_groups={{0,16,32,48},{1,17,33,49},{2,18,34,50},{3,19,35,51},{4,20,36,52},{5,21,..., dimensions={0} | all-to-all | bytes 1966080 | tf_op jit(solution)/shard_map/all_to_all | solution.py:40
  140.0 2.6 %collective-permute-done.14.oth_ref = bf16[32,8,1920]{2,1,0:T(8,128)(2,1)S(1)} collective-permute-done((bf16[32,8,1920]{2,1,0:T(8,128)(2,1)S(1)}, bf16[32,8,1920]{2,1,0:T(8,128)(2,1)S(1)}, u32[]{:S(2)}, u32[]{:S(2)}) %collective-permute-start.14) | collective-permute-done | bytes 983072 | tf_op jit(solution)/shard_map/ppermute | solution.py:36
  142.6 1.4 shard_map.218
  144.1 0.6 collective-permute-start.17
  144.7 2.1 %collective-permute-start.16 = (bf16[64,384]{1,0:T(8,128)(2,1)S(1)}, bf16[64,384]{1,0:T(8,128)(2,1)S(1)}, u32[]{:S(2)}, u32[]{:S(2)}) collective-permute-start(bf16[64,384]{1,0:T(8,128)(2,1)S(1)} %get-tuple-element.62.refs_0_), channel_id=1, source_target_pairs={{32,0},{33,1},{34,2},{35,3},{36,4},{37,5},{38,6},{39,7},{40,8},{41... | collective-permute-start | bytes 147464 | tf_op jit(solution)/shard_map/ppermute | solution.py:32
  146.8 1.0 collective-permute-start.15
  147.8 2.7 %shard_map.219 = (f32[64,384]{1,0:T(8,128)S(1)}, f32[64,384]{1,0:T(8,128)S(1)}, f32[8,384]{1,0:T(8,128)S(1)}, bf16[2,3,48,64]{3,2,1,0:T(8,128)(2,1)}, bf16[2,3,4,48]{3,2,1,0:T(4,128)(2,1)}) custom-call(bf16[2560,384]{1,0:T(8,128)(2,1)S(1)} %get-tuple-element.63.refs_0_, bf16[8,384]{1,0:T(8,128)(2,1)S(1)} %get-tuple-element.64.refs_1_, ...), custom_call_target="tpu_custom_call" | custom-call | flops 503316480 | bytes 4194304 | tf_op jit(solution)/shard_map/pallas_call | solution.py:651
  150.5 0.4 collective-permute-done.15.refs_1_
  150.9 4.2 %shard_map.220 = (f32[4,41,8,384]{3,2,1,0:T(8,128)S(1)}, bf16[4,41,8,384]{3,2,1,0:T(8,128)(2,1)S(1)}, f32[2,48,64,128]{3,2,1,0:T(8,128)}) custom-call(bf16[64,384]{1,0:T(8,128)(2,1)S(1)} %get-tuple-element.62.refs_0_, bf16[64,384]{1,0:T(8,128)(2,1)S(1)} %collective-permute-done.15.refs_1_, ...), custom_call_target="tpu_custom_call", output_to_operand_aliasing={{2}: (10, {})} | custom-call | tf_op jit(solution)/shard_map/pallas_call | solution.py:673
  155.2 2.6 %collective-permute-done.18.got_ref = bf16[4,41,8,384]{3,2,1,0:T(8,128)(2,1)S(1)} collective-permute-done((bf16[4,41,8,384]{3,2,1,0:T(8,128)(2,1)S(1)}, bf16[4,41,8,384]{3,2,1,0:T(8,128)(2,1)S(1)}, u32[]{:S(2)}, u32[]{:S(2)}) %collective-permute-start.18) | collective-permute-done | bytes 1007648 | tf_op jit(solution)/shard_map/ppermute | solution.py:36
  157.7 0.2 shard_map.221
  158.0 1.5 collective-permute-start.19
  159.5 2.6 %collective-permute-start.20 = (bf16[41,8,384]{2,1,0:T(8,128)(2,1)S(1)}, bf16[41,8,384]{2,1,0:T(8,128)(2,1)S(1)}, u32[]{:S(2)}, u32[]{:S(2)}) collective-permute-start(bf16[41,8,384]{2,1,0:T(8,128)(2,1)S(1)} %get-tuple-element.75), channel_id=1, source_target_pairs={{32,0},{33,1},{34,2},{35,3},{36,4},{37,5},{38,6},{39,7},{40,8},{41... | collective-permute-start | bytes 755720 | tf_op jit(solution)/shard_map/ppermute | solution.py:32
  162.2 0.7 collective-permute-start.21
  162.9 4.5 %collective-permute-done.19.refs_1_ = bf16[41,8,384]{2,1,0:T(8,128)(2,1)S(1)} collective-permute-done((bf16[41,8,384]{2,1,0:T(8,128)(2,1)S(1)}, bf16[41,8,384]{2,1,0:T(8,128)(2,1)S(1)}, u32[]{:S(2)}, u32[]{:S(2)}) %collective-permute-start.19) | collective-permute-done | bytes 251936 | tf_op jit(solution)/shard_map/ppermute | solution.py:32
  167.4 6.3 %collective-permute-done.20.refs_2_ = bf16[41,8,384]{2,1,0:T(8,128)(2,1)S(1)} collective-permute-done((bf16[41,8,384]{2,1,0:T(8,128)(2,1)S(1)}, bf16[41,8,384]{2,1,0:T(8,128)(2,1)S(1)}, u32[]{:S(2)}, u32[]{:S(2)}) %collective-permute-start.20) | collective-permute-done | bytes 251936 | tf_op jit(solution)/shard_map/ppermute | solution.py:32
  173.7 0.1 shard_map.222
  173.8 14.7 %all_to_all.34.got_ref = bf16[8,6,8,384]{3,2,1,0:T(8,128)(2,1)S(1)} all-to-all(bf16[8,6,8,384]{3,2,1,0:T(8,128)(2,1)S(1)} %shard_map.222), channel_id=1, replica_groups={{0,2,4,6,8,10,12,14},{1,3,5,7,9,11,13,15},{16,18,20,22,24,26,28,30},{17..., dimensions={0} | all-to-all | bytes 589824 | tf_op jit(solution)/shard_map/all_to_all | solution.py:40
  188.5 0.7 shard_map.223
  (27 shorter events, 0.8 us)
Async XLA Ops:
  0.6 3.3 %copy-start = (s32[48,8]{0,1:T(8,128)S(1)}, s32[48,8]{0,1:T(8,128)}, u32[]{:S(2)}) copy-start(s32[48,8]{0,1:T(8,128)} %param.19) | copy-start | bytes 4612
  28.0 6.7 %collective-permute-start.1 = (bf16[8,8,1920]{2,1,0:T(8,128)(2,1)S(1)}, bf16[8,8,1920]{2,1,0:T(8,128)(2,1)S(1)}, u32[]{:S(2)}, u32[]{:S(2)}) collective-permute-start(bf16[8,8,1920]{2,1,0:T(8,128)(2,1)S(1)} %all_to_all.30.here_ref), channel_id=1, source_target_pairs={{16,0},{17,1},{18,2},{19,3},{20,4},{21,5},{22,6},{23,7},{24,8},{25... | collective-permute-start | bytes 737288 | tf_op jit(solution)/shard_map/ppermute | solution.py:32
  31.0 7.5 %collective-permute-start = (bf16[8,8,1920]{2,1,0:T(8,128)(2,1)S(1)}, bf16[8,8,1920]{2,1,0:T(8,128)(2,1)S(1)}, u32[]{:S(2)}, u32[]{:S(2)}) collective-permute-start(bf16[8,8,1920]{2,1,0:T(8,128)(2,1)S(1)} %all_to_all.30.here_ref), channel_id=1, source_target_pairs={{48,0},{49,1},{50,2},{51,3},{52,4},{53,5},{54,6},{55,7},{56,8},{57... | collective-permute-start | bytes 737288 | tf_op jit(solution)/shard_map/ppermute | solution.py:32
  34.8 9.4 %collective-permute-start.3 = (bf16[4,8,1920]{2,1,0:T(8,128)(2,1)S(1)}, bf16[4,8,1920]{2,1,0:T(8,128)(2,1)S(1)}, u32[]{:S(2)}, u32[]{:S(2)}) collective-permute-start(bf16[4,8,1920]{2,1,0:T(8,128)(2,1)S(1)} %slice.9), channel_id=1, source_target_pairs={{16,0},{17,1},{18,2},{19,3},{20,4},{21,5},{22,6},{23,7},{24,8},{25... | collective-permute-start | bytes 368648 | tf_op jit(solution)/shard_map/ppermute | solution.py:32
  38.5 6.2 %collective-permute-start.2 = (bf16[4,8,1920]{2,1,0:T(8,128)(2,1)S(1)}, bf16[4,8,1920]{2,1,0:T(8,128)(2,1)S(1)}, u32[]{:S(2)}, u32[]{:S(2)}) collective-permute-start(bf16[4,8,1920]{2,1,0:T(8,128)(2,1)S(1)} %slice.8), channel_id=1, source_target_pairs={{48,0},{49,1},{50,2},{51,3},{52,4},{53,5},{54,6},{55,7},{56,8},{57... | collective-permute-start | bytes 368648 | tf_op jit(solution)/shard_map/ppermute | solution.py:32
  38.6 1.3 collective-permute-start.5
  40.7 18.3 %all-to-all-start.1 = ((bf16[8,8,2944]{2,1,0:T(8,128)(2,1)}), bf16[8,8,2944]{2,1,0:T(8,128)(2,1)S(1)}, u32[]{:S(2)}, u32[]{:S(2)}) async-start(bf16[8,8,2944]{2,1,0:T(8,128)(2,1)} %broadcast_in_dim.9), calls=%async_computation.1 | async-start | bytes 753664 | tf_op jit(solution)/shard_map/all_to_all | solution.py:40
  44.8 15.9 %collective-permute-start.4 = (bf16[32,8,1920]{2,1,0:T(8,128)(2,1)S(1)}, bf16[32,8,1920]{2,1,0:T(8,128)(2,1)S(1)}, u32[]{:S(2)}, u32[]{:S(2)}) collective-permute-start(bf16[32,8,1920]{2,1,0:T(8,128)(2,1)S(1)} %shard_map.210.own_ref), channel_id=1, source_target_pairs={{0,1},{1,0},{2,3},{3,2},{4,5},{5,4},{6,7},{7,6},{8,9},{9,8},{10,11... | collective-permute-start | bytes 2949128 | tf_op jit(solution)/shard_map/ppermute | solution.py:36
  59.0 1.7 collective-permute-start.6
  62.2 6.6 %collective-permute-start.9 = (bf16[64,384]{1,0:T(8,128)(2,1)S(1)}, bf16[64,384]{1,0:T(8,128)(2,1)S(1)}, u32[]{:S(2)}, u32[]{:S(2)}) collective-permute-start(bf16[64,384]{1,0:T(8,128)(2,1)S(1)} %get-tuple-element.47.refs_0_), channel_id=1, source_target_pairs={{48,0},{49,1},{50,2},{51,3},{52,4},{53,5},{54,6},{55,7},{56,8},{57... | collective-permute-start | bytes 147464 | tf_op jit(solution)/shard_map/ppermute | solution.py:32
  62.3 7.4 %collective-permute-start.8 = (bf16[64,384]{1,0:T(8,128)(2,1)S(1)}, bf16[64,384]{1,0:T(8,128)(2,1)S(1)}, u32[]{:S(2)}, u32[]{:S(2)}) collective-permute-start(bf16[64,384]{1,0:T(8,128)(2,1)S(1)} %get-tuple-element.47.refs_0_), channel_id=1, source_target_pairs={{32,0},{33,1},{34,2},{35,3},{36,4},{37,5},{38,6},{39,7},{40,8},{41... | collective-permute-start | bytes 147464 | tf_op jit(solution)/shard_map/ppermute | solution.py:32
  66.8 4.1 %collective-permute-start.7 = (bf16[64,384]{1,0:T(8,128)(2,1)S(1)}, bf16[64,384]{1,0:T(8,128)(2,1)S(1)}, u32[]{:S(2)}, u32[]{:S(2)}) collective-permute-start(bf16[64,384]{1,0:T(8,128)(2,1)S(1)} %get-tuple-element.47.refs_0_), channel_id=1, source_target_pairs={{16,0},{17,1},{18,2},{19,3},{20,4},{21,5},{22,6},{23,7},{24,8},{25... | collective-permute-start | bytes 147464 | tf_op jit(solution)/shard_map/ppermute | solution.py:32
  75.1 2.7 %collective-permute-start.10 = (bf16[4,41,8,384]{3,2,1,0:T(8,128)(2,1)S(1)}, bf16[4,41,8,384]{3,2,1,0:T(8,128)(2,1)S(1)}, u32[]{:S(2)}, u32[]{:S(2)}) collective-permute-start(bf16[4,41,8,384]{3,2,1,0:T(8,128)(2,1)S(1)} %get-tuple-element.57), channel_id=1, source_target_pairs={{0,1},{1,0},{2,3},{3,2},{4,5},{5,4},{6,7},{7,6},{8,9},{9,8},{10,11... | collective-permute-start | bytes 3022856 | tf_op jit(solution)/shard_map/ppermute | solution.py:36
  78.0 14.8 %collective-permute-start.11 = (bf16[41,8,384]{2,1,0:T(8,128)(2,1)S(1)}, bf16[41,8,384]{2,1,0:T(8,128)(2,1)S(1)}, u32[]{:S(2)}, u32[]{:S(2)}) collective-permute-start(bf16[41,8,384]{2,1,0:T(8,128)(2,1)S(1)} %get-tuple-element.59), channel_id=1, source_target_pairs={{48,0},{49,1},{50,2},{51,3},{52,4},{53,5},{54,6},{55,7},{56,8},{57... | collective-permute-start | bytes 755720 | tf_op jit(solution)/shard_map/ppermute | solution.py:32
  78.1 14.7 %collective-permute-start.12 = (bf16[41,8,384]{2,1,0:T(8,128)(2,1)S(1)}, bf16[41,8,384]{2,1,0:T(8,128)(2,1)S(1)}, u32[]{:S(2)}, u32[]{:S(2)}) collective-permute-start(bf16[41,8,384]{2,1,0:T(8,128)(2,1)S(1)} %get-tuple-element.60), channel_id=1, source_target_pairs={{32,0},{33,1},{34,2},{35,3},{36,4},{37,5},{38,6},{39,7},{40,8},{41... | collective-permute-start | bytes 755720 | tf_op jit(solution)/shard_map/ppermute | solution.py:32
  80.8 12.7 %collective-permute-start.13 = (bf16[41,8,384]{2,1,0:T(8,128)(2,1)S(1)}, bf16[41,8,384]{2,1,0:T(8,128)(2,1)S(1)}, u32[]{:S(2)}, u32[]{:S(2)}) collective-permute-start(bf16[41,8,384]{2,1,0:T(8,128)(2,1)S(1)} %get-tuple-element.61), channel_id=1, source_target_pairs={{16,0},{17,1},{18,2},{19,3},{20,4},{21,5},{22,6},{23,7},{24,8},{25... | collective-permute-start | bytes 755720 | tf_op jit(solution)/shard_map/ppermute | solution.py:32
  140.0 2.6 %collective-permute-start.14 = (bf16[32,8,1920]{2,1,0:T(8,128)(2,1)S(1)}, bf16[32,8,1920]{2,1,0:T(8,128)(2,1)S(1)}, u32[]{:S(2)}, u32[]{:S(2)}) collective-permute-start(bf16[32,8,1920]{2,1,0:T(8,128)(2,1)S(1)} %bitcast.21), channel_id=1, source_target_pairs={{0,1},{1,0},{2,3},{3,2},{4,5},{5,4},{6,7},{7,6},{8,9},{9,8},{10,11... | collective-permute-start | bytes 2949128 | tf_op jit(solution)/shard_map/ppermute | solution.py:36
  144.1 6.4 %collective-permute-start.17 = (bf16[64,384]{1,0:T(8,128)(2,1)S(1)}, bf16[64,384]{1,0:T(8,128)(2,1)S(1)}, u32[]{:S(2)}, u32[]{:S(2)}) collective-permute-start(bf16[64,384]{1,0:T(8,128)(2,1)S(1)} %get-tuple-element.62.refs_0_), channel_id=1, source_target_pairs={{48,0},{49,1},{50,2},{51,3},{52,4},{53,5},{54,6},{55,7},{56,8},{57... | collective-permute-start | bytes 147464 | tf_op jit(solution)/shard_map/ppermute | solution.py:32
  144.7 5.8 %collective-permute-start.16 = (bf16[64,384]{1,0:T(8,128)(2,1)S(1)}, bf16[64,384]{1,0:T(8,128)(2,1)S(1)}, u32[]{:S(2)}, u32[]{:S(2)}) collective-permute-start(bf16[64,384]{1,0:T(8,128)(2,1)S(1)} %get-tuple-element.62.refs_0_), channel_id=1, source_target_pairs={{32,0},{33,1},{34,2},{35,3},{36,4},{37,5},{38,6},{39,7},{40,8},{41... | collective-permute-start | bytes 147464 | tf_op jit(solution)/shard_map/ppermute | solution.py:32
  146.8 4.1 %collective-permute-start.15 = (bf16[64,384]{1,0:T(8,128)(2,1)S(1)}, bf16[64,384]{1,0:T(8,128)(2,1)S(1)}, u32[]{:S(2)}, u32[]{:S(2)}) collective-permute-start(bf16[64,384]{1,0:T(8,128)(2,1)S(1)} %get-tuple-element.62.refs_0_), channel_id=1, source_target_pairs={{16,0},{17,1},{18,2},{19,3},{20,4},{21,5},{22,6},{23,7},{24,8},{25... | collective-permute-start | bytes 147464 | tf_op jit(solution)/shard_map/ppermute | solution.py:32
  155.1 2.7 %collective-permute-start.18 = (bf16[4,41,8,384]{3,2,1,0:T(8,128)(2,1)S(1)}, bf16[4,41,8,384]{3,2,1,0:T(8,128)(2,1)S(1)}, u32[]{:S(2)}, u32[]{:S(2)}) collective-permute-start(bf16[4,41,8,384]{3,2,1,0:T(8,128)(2,1)S(1)} %get-tuple-element.72), channel_id=1, source_target_pairs={{0,1},{1,0},{2,3},{3,2},{4,5},{5,4},{6,7},{7,6},{8,9},{9,8},{10,11... | collective-permute-start | bytes 3022856 | tf_op jit(solution)/shard_map/ppermute | solution.py:36
  158.0 9.4 %collective-permute-start.19 = (bf16[41,8,384]{2,1,0:T(8,128)(2,1)S(1)}, bf16[41,8,384]{2,1,0:T(8,128)(2,1)S(1)}, u32[]{:S(2)}, u32[]{:S(2)}) collective-permute-start(bf16[41,8,384]{2,1,0:T(8,128)(2,1)S(1)} %get-tuple-element.74), channel_id=1, source_target_pairs={{48,0},{49,1},{50,2},{51,3},{52,4},{53,5},{54,6},{55,7},{56,8},{57... | collective-permute-start | bytes 755720 | tf_op jit(solution)/shard_map/ppermute | solution.py:32
  159.5 14.1 %collective-permute-start.20 = (bf16[41,8,384]{2,1,0:T(8,128)(2,1)S(1)}, bf16[41,8,384]{2,1,0:T(8,128)(2,1)S(1)}, u32[]{:S(2)}, u32[]{:S(2)}) collective-permute-start(bf16[41,8,384]{2,1,0:T(8,128)(2,1)S(1)} %get-tuple-element.75), channel_id=1, source_target_pairs={{32,0},{33,1},{34,2},{35,3},{36,4},{37,5},{38,6},{39,7},{40,8},{41... | collective-permute-start | bytes 755720 | tf_op jit(solution)/shard_map/ppermute | solution.py:32
  162.2 11.5 %collective-permute-start.21 = (bf16[41,8,384]{2,1,0:T(8,128)(2,1)S(1)}, bf16[41,8,384]{2,1,0:T(8,128)(2,1)S(1)}, u32[]{:S(2)}, u32[]{:S(2)}) collective-permute-start(bf16[41,8,384]{2,1,0:T(8,128)(2,1)S(1)} %get-tuple-element.76), channel_id=1, source_target_pairs={{16,0},{17,1},{18,2},{19,3},{20,4},{21,5},{22,6},{23,7},{24,8},{25... | collective-permute-start | bytes 755720 | tf_op jit(solution)/shard_map/ppermute | solution.py:32

commit v4 on v3

--- a/solution.py
+++ b/solution.py
@@ -20,7 +20,6 @@
 
 
 Z_GROUPS = [[device_at(y, z, c) for z in range(ZS)] for y in range(YS) for c in range(CS)]
-Y_GROUPS = [[device_at(y, z, c) for y in range(YS)] for z in range(ZS) for c in range(CS)]
 PARTNER = [(i, i ^ 1) for i in range(YS * ZS * CS)]
 
 
@@ -32,6 +31,14 @@
     return lax.ppermute(value, "heads", pairs)
 
 
+def to_y(value, shift):
+    pairs = [
+        (device_at(y, z, c), device_at((y + (shift if c == 0 else -shift)) % YS, z, c))
+        for y, z, c in PLACES
+    ]
+    return lax.ppermute(value, "heads", pairs)
+
+
 def swap_cores(value):
     return lax.ppermute(value, "heads", PARTNER)
 
@@ -45,31 +52,21 @@
     return exchange(jnp.broadcast_to(value[None], (count, *value.shape)), groups)
 
 
-def gather_planes(piece, ring):
+def gather_planes(piece):
     rows, width = piece.shape
-    half = ZS // 2
     over_z = spread(piece, Z_GROUPS)
-    if ring:
-        below = from_y(over_z, -1)
-        above = from_y(over_z, 1)
-        far_low = from_y(below[:half], -1)
-        far_high = from_y(above[half:], 1)
-        own = call(
-            ring_join_kernel, jax.ShapeDtypeStruct((YS * ZS, rows, width), BF), 5
-        )(over_z, below, above, far_low, far_high)
-    else:
-        own = spread(over_z, Y_GROUPS).reshape(YS * ZS, rows, width)
+    own = call(
+        join_y_kernel, jax.ShapeDtypeStruct((YS * ZS, rows, width), BF), YS
+    )(over_z, *[to_y(over_z, d) for d in range(1, YS)])
     return own, swap_cores(own)
 
 
-def ring_join_kernel(here_ref, below_ref, above_ref, low_ref, high_ref, out_ref):
-    y = position()[0]
-    half = ZS // 2
-    for shift, ref in ((0, here_ref), (1, above_ref), (3, below_ref)):
-        out_ref[pl.ds(lax.rem(y + shift, YS) * ZS, ZS)] = ref[...]
-    far = lax.rem(y + 2, YS) * ZS
-    out_ref[pl.ds(far, half)] = low_ref[...]
-    out_ref[pl.ds(far + half, half)] = high_ref[...]
+def join_y_kernel(*refs):
+    *got_refs, out_ref = refs
+    y, _, core = position()
+    turn = jnp.where(core == 0, YS - 1, 1)
+    for d, ref in enumerate(got_refs):
+        out_ref[pl.ds(lax.rem(y + d * turn, YS) * ZS, ZS)] = ref[...]
 
 
 VMEM = pl.BlockSpec(memory_space=pltpu.VMEM)
@@ -323,13 +320,16 @@
 
     def kernel(*refs):
         (
-            nb_ref, mine_ref, table_ref, beforex_ref, beforebc_ref, spread_ref, zx_ref, *rest,
+            nb_ref, mine_ref, table_ref, beforex_ref, beforebc_ref, spread_ref, zx_ref,
+            ssm_ref, *rest,
         ) = refs
         if last:
             old_x_ref, old_bc_ref, *rest = rest
-        gate_ref, xc_ref, rows_ref, newx_ref, newbc_ref, zx_w, sem = rest
-        load_w = pltpu.make_async_copy(zx_ref.at[layer], zx_w, sem)
+        gate_ref, xc_ref, rows_ref, h_ref, newx_ref, newbc_ref, zx_w, sems = rest
+        load_w = pltpu.make_async_copy(zx_ref.at[layer], zx_w, sems.at[0])
+        load_h = pltpu.make_async_copy(ssm_ref.at[layer], h_ref, sems.at[1])
         load_w.start()
+        load_h.start()
         turned = table_ref[layer]
         width = beforex_ref.shape[1]
         here = newbc_ref.shape[-2]
@@ -382,6 +382,7 @@
                     newx_ref[l, i], newbc_ref[l, i] = old_x_ref[i], old_bc_ref[i]
             else:
                 newx_ref[i], newbc_ref[i] = rows_x, rows_bc
+        load_h.wait()
 
     return kernel
 
@@ -391,20 +392,13 @@
 
     def kernel(*refs):
         got_refs = refs[:YS]
-        gate_ref, xc_ref, rows_ref, table_ref, outw_ref, ssm_ref, *rest = refs[YS:]
+        gate_ref, xc_ref, rows_ref, h_in, table_ref, outw_ref, *rest = refs[YS:]
         if last:
             _, *rest = rest
-        keep_ref, send_ref, newssm_ref, h_in, h_out, xw_all, out_w, channels, sems = rest
+        keep_ref, send_ref, newssm_ref, h_out, xw_all, out_w, channels, sems = rest
         y_here, _, core = position()
         first = core == 0
-        tiles = xc_ref.shape[1] // LANES
-        part = h_in.shape[0] // tiles
-        loads = []
-        for i in range(tiles):
-            at = pl.ds(i * part, part)
-            loads.append(pltpu.make_async_copy(ssm_ref.at[layer, at], h_in.at[at], sems.at[i]))
-            loads[-1].start()
-        load_o = pltpu.make_async_copy(outw_ref.at[layer], out_w, sems.at[tiles])
+        load_o = pltpu.make_async_copy(outw_ref.at[layer], out_w, sems.at[0])
         load_o.start()
         turned = table_ref[layer]
         width = xc_ref.shape[0]
@@ -442,7 +436,6 @@
             y_old = jnp.zeros((width, LANES), F32)
             falls = jnp.sum(jnp.where(pick16, fall_cut[:, ls], 0.0), axis=1, keepdims=True)
             xw = xw_all[:, ls]
-            loads[tile].wait()
             for s in range(per_tile):
                 n = tile * per_tile + s
                 h0 = h_in[n]
@@ -451,7 +444,7 @@
                 add = ndot(jnp.where(here, xw, jnp.zeros_like(xw)), bmat)
                 h_out[n] = h0 * falls[s : s + 1, :] + add
             parts.append(fall[:, ls] * y_old + y_new)
-        store = pltpu.make_async_copy(h_out, newssm_ref.at[layer], sems.at[tiles + 1])
+        store = pltpu.make_async_copy(h_out, newssm_ref.at[layer], sems.at[1])
         store.start()
         y = jnp.concatenate(parts, axis=1) + skip * xc
         gated = y * gate_ref[...]
@@ -481,10 +474,11 @@
 
 def add_cores_kernel(keep_ref, got_ref, *out_refs):
     tiles = keep_ref.shape[1]
-    y = position()[0]
+    y, _, core = position()
+    turn = jnp.where(core == 0, 1, YS - 1)
     tail = split_tail(keep_ref[0, tiles - 1] + got_ref[0, tiles - 1].astype(F32))
     for shift, out_ref in enumerate(out_refs):
-        at = lax.rem(y + shift, YS)
+        at = lax.rem(y + shift * turn, YS)
         out_ref[: tiles - 1] = (
             keep_ref[at, : tiles - 1] + got_ref[at, : tiles - 1].astype(F32)
         ).astype(BF)
@@ -624,7 +618,7 @@
     stream = lookup(tokens_ids, vocab)
     w_own = spread(pair_rows, Z_GROUPS)
     w_oth = swap_cores(w_own)
-    own, oth = gather_planes(stream, True)
+    own, oth = gather_planes(stream)
 
     zx_w, outer_w, state_in = [
         pltpu.with_memory_space_constraint(v, pltpu.HBM)
@@ -645,30 +639,31 @@
             in_specs=[VMEM] * 6,
             out_specs=(VMEM,) * 3,
             scratch_shapes=[pltpu.VMEM((model, tokens), F32)],
-            compiler_params=limit(20),
+            compiler_params=limit(14),
         )(own, oth, w_own, w_oth, table, own8)
         got = [bcc] + [from_y(bcc, d) for d in range(1, YS)]
-        gate, xc, rows, *saved = pl.pallas_call(
+        gate, xc, rows, h_in, *saved = pl.pallas_call(
             make_values_kernel(layer, tokens, seqs, draft, taps, last),
             out_shape=(
                 jax.ShapeDtypeStruct((width, tokens), F32),
                 jax.ShapeDtypeStruct((width, tokens), F32),
                 jax.ShapeDtypeStruct((8, tokens), F32),
+                jax.ShapeDtypeStruct(state_shape[1:], F32),
                 jax.ShapeDtypeStruct((*lead, kept, seqs, width), BF),
                 jax.ShapeDtypeStruct((*lead, kept, bc_here, seqs), BF),
             ),
-            in_specs=[VMEM] * 6 + [HBM] + [VMEM] * len(saved),
-            out_specs=(VMEM,) * 5,
+            in_specs=[VMEM] * 6 + [HBM] * 2 + [VMEM] * len(saved),
+            out_specs=(VMEM,) * 6,
             scratch_shapes=[
                 pltpu.VMEM((model, 2 * width), BF),
-                pltpu.SemaphoreType.DMA,
+                pltpu.SemaphoreType.DMA((2,)),
             ],
-            compiler_params=limit(16),
+            compiler_params=limit(10),
             cost_estimate=pl.CostEstimate(
                 flops=2 * model * tokens * 4 * width, bytes_accessed=4 << 20, transcendentals=0
             ),
         )(
-            normed, mine, table, before_x, before_bc, spread_acc, zx_w, *saved
+            normed, mine, table, before_x, before_bc, spread_acc, zx_w, state_in, *saved
         )
         keep, send, *saved_ssm = pl.pallas_call(
             make_recur_kernel(layer, tokens, draft, own_cols, taps, last),
@@ -677,22 +672,21 @@
                 jax.ShapeDtypeStruct((YS, tiles, 8, tokens), BF),
                 jax.ShapeDtypeStruct(state_shape, F32),
             ),
-            in_specs=[VMEM] * 8 + [HBM] * (2 + len(saved_ssm)),
+            in_specs=[VMEM] * 9 + [HBM] * (1 + len(saved_ssm)),
             out_specs=(VMEM, VMEM, HBM),
             scratch_shapes=[
-                pltpu.VMEM(state_shape[1:], F32),
                 pltpu.VMEM(state_shape[1:], F32),
                 pltpu.VMEM((width, tokens), BF),
                 pltpu.VMEM((width, model), BF),
                 pltpu.VMEM((YS, ZS * 8, tokens), F32),
-                pltpu.SemaphoreType.DMA((tokens // LANES + 2,)),
+                pltpu.SemaphoreType.DMA((2,)),
             ],
             input_output_aliases={10: 2} if last else {},
-            compiler_params=limit(24),
-        )(*got, gate, xc, rows, table, outer_w, state_in, *saved_ssm)
+            compiler_params=limit(14),
+        )(*got, gate, xc, rows, h_in, table, outer_w, *saved_ssm)
         block = jax.ShapeDtypeStruct((tiles, 8, tokens), BF)
         here, *blocks = call(add_cores_kernel, (block,) * YS, 2)(keep, swap_cores(send))
-        got = {d: from_y(blocks[d - 1], -d) for d in (2, 1, 3)}
+        got = {d: to_y(blocks[d - 1], d) for d in range(1, YS)}
         summed = call(
             add_y_kernel, jax.ShapeDtypeStruct((ZS, pieces + 1, 8, tokens), BF), YS
         )(here, *[got[d] for d in range(1, YS)])
@@ -701,7 +695,7 @@
             make_finish_kernel(inner, last), jax.ShapeDtypeStruct(shape, BF), 2
         )(exchange(summed, Z_GROUPS), stream)
         if not last:
-            own, oth = gather_planes(stream, False)
+            own, oth = gather_planes(stream)
     (new_x, new_bc), (new_ssm,) = saved, saved_ssm
     hidden = stream.reshape(own_cols, tokens).T
     kept_x = jnp.swapaxes(new_x, 1, 2)

time: 190 us -> 181 us (0.953)
  blocking collectives: 80.7 us -> 65.6 us
  waiting for transfers between devices: 53.5 us -> 59.9 us
    ppermute x0 -> x12, waiting for transfers between devices: none -> 35.6 us  [to_y(): return lax.ppermute(value, 'heads', pairs)]
    ppermute x16 -> x6, waiting for transfers between devices: 28.7 us -> 2.7 us  [from_y(): return lax.ppermute(value, 'heads', pairs)]
    ppermute x0 -> x12, starting transfers between devices: none -> 15.3 us  [to_y(): return lax.ppermute(value, 'heads', pairs)]
    all_to_all x5 -> x4, blocking collectives: 80.7 us -> 65.6 us  [exchange(): lax.all_to_all(value, 'heads', 0, 0, tiled=True, axis_index_groups=groups)]
    ppermute x16 -> x6, starting transfers between devices: 24.3 us -> 9.53 us  [from_y(): return lax.ppermute(value, 'heads', pairs)]
    all_to_all x1, waiting for transfers between devices: 14.1 us -> 11 us  [exchange(): lax.all_to_all(value, 'heads', 0, 0, tiled=True, axis_index_groups=groups)]
  transfers between devices with their start and end apart: 23 -> 25, of which waited for: 15 -> 17; matrix products, arithmetic and copies ran while one was open for 0% -> 0% of each run, Pallas kernels for 2% -> 3%
where the time goes in v4:
time: 181 us; the launch traced here: 179 us
  blocking collectives  65.6 us (36%)
  waiting for transfers between devices  59.9 us (33%)
  starting transfers between devices  29.1 us (16%)
  Pallas kernels  23.2 us (13%)
    all_to_all x4, blocking collectives, exchange(): lax.all_to_all(value, 'heads', 0, 0, tiled=True, axis_index_groups=groups)  65.6 us
    ppermute x12, waiting for transfers between devices, to_y(): return lax.ppermute(value, 'heads', pairs)  35.6 us
    ppermute x12, starting transfers between devices, to_y(): return lax.ppermute(value, 'heads', pairs)  15.3 us
    all_to_all x1, waiting for transfers between devices, exchange(): lax.all_to_all(value, 'heads', 0, 0, tiled=True, axis_index_groups=groups)  11 us
    ppermute x6, waiting for transfers between devices, swap_cores(): return lax.ppermute(value, 'heads', PARTNER)  10.6 us
    ppermute x6, starting transfers between devices, from_y(): return lax.ppermute(value, 'heads', pairs)  9.53 us
    pallas_call x2, Pallas kernels, local(): pl.pallas_call(make_recur_kernel(layer, tokens, draft, own_cols, taps, la...  6.68 us
    pallas_call x2, Pallas kernels, local(): pl.pallas_call(make_values_kernel(layer, tokens, seqs, draft, taps, last)...  4.52 us
  transfers between devices with their start and end apart: 25, of which 17 were waited for; matrix products, arithmetic and copies ran while one was open for 0% of the time, Pallas kernels for 3%

profile of v4, /device:TPU:2, one launch (start us, length us, event | category | flops | bytes accessed | tf_op | source)
XLA Modules:
  0.0 179.4 jit_solution(10833797289227754502)
XLA Ops:
  0.6 3.2 %setup.1 = (bf16[8,2944]{1,0:T(8,128)(2,1)S(1)}, bf16[8,2944]{1,0:T(8,128)(2,1)S(1)}, f32[2,128,128]{2,1,0:T(8,128)S(1)}, bf16[2,8,2560]{2,1,0:T(8,128)(2,1)S(1)...) custom-call(f32[1,2]{1,0:T(1,128)} %bitcast.32, ...), custom_call_target="tpu_custom_call" | custom-call | tf_op jit(solution)/shard_map/setup/pallas_call | solution.py:580
  3.9 4.3 %lookup.1.stream_ref = bf16[8,1920]{1,0:T(8,128)(2,1)S(1)} custom-call(s32[8,48]{1,0:T(8,128)S(1)} %bitcast.20, bf16[40,50280]{1,0:T(8,128)(2,1)S(1)} %get-tuple-element.44.table_ref), custom_call_target="tpu_custom_call" | custom-call | tf_op jit(solution)/shard_map/lookup/pallas_call | solution.py:136
  8.2 19.8 %all_to_all.25.refs_0_ = bf16[8,8,1920]{2,1,0:T(8,128)(2,1)S(1)} all-to-all(bf16[8,8,1920]{2,1,0:T(8,128)(2,1)S(1)} %broadcast_in_dim.6), channel_id=1, replica_groups={{0,2,4,6,8,10,12,14},{1,3,5,7,9,11,13,15},{16,18,20,22,24,26,28,30},{17..., dimensions={0} | all-to-all | bytes 491520 | tf_op jit(solution)/shard_map/all_to_all | solution.py:47
  28.0 3.0 %collective-permute-start.2 = (bf16[8,8,1920]{2,1,0:T(8,128)(2,1)S(1)}, bf16[8,8,1920]{2,1,0:T(8,128)(2,1)S(1)}, u32[]{:S(2)}, u32[]{:S(2)}) collective-permute-start(bf16[8,8,1920]{2,1,0:T(8,128)(2,1)S(1)} %all_to_all.25.refs_0_), channel_id=1, source_target_pairs={{0,48},{1,17},{2,50},{3,19},{4,52},{5,21},{6,54},{7,23},{8,56},{9,... | collective-permute-start | bytes 737288 | tf_op jit(solution)/shard_map/ppermute | solution.py:39
  31.0 0.6 collective-permute-start.1
  31.7 1.0 collective-permute-start
  32.6 1.2 collective-permute-done.4.got_ref
  33.9 0.8 broadcast_in_dim.7
  34.6 3.4 %all-to-all-start.1 = ((bf16[8,8,2944]{2,1,0:T(8,128)(2,1)}), bf16[8,8,2944]{2,1,0:T(8,128)(2,1)S(1)}, u32[]{:S(2)}, u32[]{:S(2)}) async-start(bf16[8,8,2944]{2,1,0:T(8,128)(2,1)} %broadcast_in_dim.7), calls=%async_computation.1 | async-start | bytes 753664 | tf_op jit(solution)/shard_map/all_to_all | solution.py:47
  38.1 2.5 %collective-permute-done.2.refs_3_ = bf16[8,8,1920]{2,1,0:T(8,128)(2,1)S(1)} collective-permute-done((bf16[8,8,1920]{2,1,0:T(8,128)(2,1)S(1)}, bf16[8,8,1920]{2,1,0:T(8,128)(2,1)S(1)}, u32[]{:S(2)}, u32[]{:S(2)}) %collective-permute-start.2) | collective-permute-done | bytes 245792 | tf_op jit(solution)/shard_map/ppermute | solution.py:39
  40.6 1.1 collective-permute-done.refs_1_
  41.9 11.0 %all-to-all-done.1.wown_ref = bf16[8,8,2944]{2,1,0:T(8,128)(2,1)S(1)} async-done(((bf16[8,8,2944]{2,1,0:T(8,128)(2,1)}), bf16[8,8,2944]{2,1,0:T(8,128)(2,1)S(1)}, u32[]{:S(2)}, u32[]{:S(2)}) %all-to-all-start.1) | async-done | bytes 376864 | tf_op jit(solution)/shard_map/all_to_all | solution.py:47
  53.0 1.7 collective-permute-done.5.woth_ref
  54.7 1.4 shard_map.212
  56.1 2.0 %collective-permute-start.8 = (bf16[64,384]{1,0:T(8,128)(2,1)S(1)}, bf16[64,384]{1,0:T(8,128)(2,1)S(1)}, u32[]{:S(2)}, u32[]{:S(2)}) collective-permute-start(bf16[64,384]{1,0:T(8,128)(2,1)S(1)} %get-tuple-element.49.refs_0_), channel_id=1, source_target_pairs={{48,0},{49,1},{50,2},{51,3},{52,4},{53,5},{54,6},{55,7},{56,8},{57... | collective-permute-start | bytes 147464 | tf_op jit(solution)/shard_map/ppermute | solution.py:31
  58.0 1.8 %collective-permute-start.7 = (bf16[64,384]{1,0:T(8,128)(2,1)S(1)}, bf16[64,384]{1,0:T(8,128)(2,1)S(1)}, u32[]{:S(2)}, u32[]{:S(2)}) collective-permute-start(bf16[64,384]{1,0:T(8,128)(2,1)S(1)} %get-tuple-element.49.refs_0_), channel_id=1, source_target_pairs={{32,0},{33,1},{34,2},{35,3},{36,4},{37,5},{38,6},{39,7},{40,8},{41... | collective-permute-start | bytes 147464 | tf_op jit(solution)/shard_map/ppermute | solution.py:31
  59.9 0.9 collective-permute-start.6
  60.8 1.9 %shard_map.213 = (f32[64,384]{1,0:T(8,128)S(1)}, f32[64,384]{1,0:T(8,128)S(1)}, f32[8,384]{1,0:T(8,128)S(1)}, f32[48,64,128]{2,1,0:T(8,128)S(1)}, bf16[3,48,64]{...) custom-call(bf16[2560,384]{1,0:T(8,128)(2,1)S(1)} %get-tuple-element.50.refs_0_, ...), custom_call_target="tpu_custom_call" | custom-call | flops 503316480 | bytes 4194304 | tf_op jit(solution)/shard_map/pallas_call | solution.py:645
  62.8 0.9 collective-permute-done.7.refs_2_
  63.6 0.3 collective-permute-done.6.refs_1_
  64.0 3.6 %shard_map.214 = (f32[4,41,8,384]{3,2,1,0:T(8,128)S(1)}, bf16[4,41,8,384]{3,2,1,0:T(8,128)(2,1)S(1)}, f32[2,48,64,128]{3,2,1,0:T(8,128)}) custom-call(bf16[64,384]{1,0:T(8,128)(2,1)S(1)} %get-tuple-element.49.refs_0_, bf16[64,384]{1,0:T(8,128)(2,1)S(1)} %collective-permute-done.6.refs_1_, bf16[64,384]{1,0:T(8,128)(2,1)S(1)} %collective-permute-done.7.refs_2_, ...), custom_call_target="tpu_custom_call" | custom-call | tf_op jit(solution)/shard_map/pallas_call | solution.py:668
  67.8 2.6 %collective-permute-done.9.got_ref = bf16[4,41,8,384]{3,2,1,0:T(8,128)(2,1)S(1)} collective-permute-done((bf16[4,41,8,384]{3,2,1,0:T(8,128)(2,1)S(1)}, bf16[4,41,8,384]{3,2,1,0:T(8,128)(2,1)S(1)}, u32[]{:S(2)}, u32[]{:S(2)}) %collective-permute-start.9) | collective-permute-done | bytes 1007648 | tf_op jit(solution)/shard_map/ppermute | solution.py:43
  70.6 0.7 collective-permute-start.10
  71.3 3.0 %collective-permute-start.11 = (bf16[41,8,384]{2,1,0:T(8,128)(2,1)S(1)}, bf16[41,8,384]{2,1,0:T(8,128)(2,1)S(1)}, u32[]{:S(2)}, u32[]{:S(2)}) collective-permute-start(bf16[41,8,384]{2,1,0:T(8,128)(2,1)S(1)} %get-tuple-element.63), channel_id=1, source_target_pairs={{0,32},{1,33},{2,34},{3,35},{4,36},{5,37},{6,38},{7,39},{8,40},{9,... | collective-permute-start | bytes 755720 | tf_op jit(solution)/shard_map/ppermute | solution.py:39
  74.3 0.7 collective-permute-start.12
  75.0 9.2 %collective-permute-done.10.refs_1_ = bf16[41,8,384]{2,1,0:T(8,128)(2,1)S(1)} collective-permute-done((bf16[41,8,384]{2,1,0:T(8,128)(2,1)S(1)}, bf16[41,8,384]{2,1,0:T(8,128)(2,1)S(1)}, u32[]{:S(2)}, u32[]{:S(2)}) %collective-permute-start.10) | collective-permute-done | bytes 251936 | tf_op jit(solution)/shard_map/ppermute | solution.py:39
  84.3 1.5 collective-permute-done.11.refs_2_
  85.9 15.8 %all_to_all.26.got_ref = bf16[8,6,8,384]{3,2,1,0:T(8,128)(2,1)S(1)} all-to-all(bf16[8,6,8,384]{3,2,1,0:T(8,128)(2,1)S(1)} %shard_map.216), channel_id=1, replica_groups={{0,2,4,6,8,10,12,14},{1,3,5,7,9,11,13,15},{16,18,20,22,24,26,28,30},{17..., dimensions={0} | all-to-all | bytes 589824 | tf_op jit(solution)/shard_map/all_to_all | solution.py:47
  101.7 14.0 %all_to_all.27.refs_0_ = bf16[8,8,1920]{2,1,0:T(8,128)(2,1)S(1)} all-to-all(bf16[8,8,1920]{2,1,0:T(8,128)(2,1)S(1)} %broadcast_in_dim.8), channel_id=1, replica_groups={{0,2,4,6,8,10,12,14},{1,3,5,7,9,11,13,15},{16,18,20,22,24,26,28,30},{17..., dimensions={0} | all-to-all | bytes 491520 | tf_op jit(solution)/shard_map/all_to_all | solution.py:47
  115.7 0.6 collective-permute-start.15
  116.3 1.1 collective-permute-start.14
  117.4 0.4 collective-permute-start.13
  117.8 8.6 %collective-permute-done.15.refs_3_ = bf16[8,8,1920]{2,1,0:T(8,128)(2,1)S(1)} collective-permute-done((bf16[8,8,1920]{2,1,0:T(8,128)(2,1)S(1)}, bf16[8,8,1920]{2,1,0:T(8,128)(2,1)S(1)}, u32[]{:S(2)}, u32[]{:S(2)}) %collective-permute-start.15) | collective-permute-done | bytes 245792 | tf_op jit(solution)/shard_map/ppermute | solution.py:39
  126.4 2.0 %collective-permute-done.13.refs_1_ = bf16[8,8,1920]{2,1,0:T(8,128)(2,1)S(1)} collective-permute-done((bf16[8,8,1920]{2,1,0:T(8,128)(2,1)S(1)}, bf16[8,8,1920]{2,1,0:T(8,128)(2,1)S(1)}, u32[]{:S(2)}, u32[]{:S(2)}) %collective-permute-start.13) | collective-permute-done | bytes 245792 | tf_op jit(solution)/shard_map/ppermute | solution.py:39
  128.6 2.6 %collective-permute-done.16.oth_ref = bf16[32,8,1920]{2,1,0:T(8,128)(2,1)S(1)} collective-permute-done((bf16[32,8,1920]{2,1,0:T(8,128)(2,1)S(1)}, bf16[32,8,1920]{2,1,0:T(8,128)(2,1)S(1)}, u32[]{:S(2)}, u32[]{:S(2)}) %collective-permute-start.16) | collective-permute-done | bytes 983072 | tf_op jit(solution)/shard_map/ppermute | solution.py:43
  131.2 1.4 shard_map.219
  132.6 0.9 collective-permute-start.19
  133.6 3.9 %collective-permute-start.18 = (bf16[64,384]{1,0:T(8,128)(2,1)S(1)}, bf16[64,384]{1,0:T(8,128)(2,1)S(1)}, u32[]{:S(2)}, u32[]{:S(2)}) collective-permute-start(bf16[64,384]{1,0:T(8,128)(2,1)S(1)} %get-tuple-element.65.refs_0_), channel_id=1, source_target_pairs={{32,0},{33,1},{34,2},{35,3},{36,4},{37,5},{38,6},{39,7},{40,8},{41... | collective-permute-start | bytes 147464 | tf_op jit(solution)/shard_map/ppermute | solution.py:31
  137.4 2.6 %shard_map.220 = (f32[64,384]{1,0:T(8,128)S(1)}, f32[64,384]{1,0:T(8,128)S(1)}, f32[8,384]{1,0:T(8,128)S(1)}, f32[48,64,128]{2,1,0:T(8,128)S(1)}, bf16[2,3,48,64...) custom-call(bf16[2560,384]{1,0:T(8,128)(2,1)S(1)} %get-tuple-element.66.refs_0_, ...), custom_call_target="tpu_custom_call" | custom-call | flops 503316480 | bytes 4194304 | tf_op jit(solution)/shard_map/pallas_call | solution.py:645
  140.2 1.3 collective-permute-done.17.refs_1_
  141.5 3.1 %shard_map.221 = (f32[4,41,8,384]{3,2,1,0:T(8,128)S(1)}, bf16[4,41,8,384]{3,2,1,0:T(8,128)(2,1)S(1)}, f32[2,48,64,128]{3,2,1,0:T(8,128)}) custom-call(bf16[64,384]{1,0:T(8,128)(2,1)S(1)} %get-tuple-element.65.refs_0_, bf16[64,384]{1,0:T(8,128)(2,1)S(1)} %collective-permute-done.17.refs_1_, ...), custom_call_target="tpu_custom_call", output_to_operand_aliasing={{2}: (10, {})} | custom-call | tf_op jit(solution)/shard_map/pallas_call | solution.py:668
  145.0 2.6 %collective-permute-done.20.got_ref = bf16[4,41,8,384]{3,2,1,0:T(8,128)(2,1)S(1)} collective-permute-done((bf16[4,41,8,384]{3,2,1,0:T(8,128)(2,1)S(1)}, bf16[4,41,8,384]{3,2,1,0:T(8,128)(2,1)S(1)}, u32[]{:S(2)}, u32[]{:S(2)}) %collective-permute-start.20) | collective-permute-done | bytes 1007648 | tf_op jit(solution)/shard_map/ppermute | solution.py:43
  147.8 0.6 collective-permute-start.21
  148.4 2.1 %collective-permute-start.22 = (bf16[41,8,384]{2,1,0:T(8,128)(2,1)S(1)}, bf16[41,8,384]{2,1,0:T(8,128)(2,1)S(1)}, u32[]{:S(2)}, u32[]{:S(2)}) collective-permute-start(bf16[41,8,384]{2,1,0:T(8,128)(2,1)S(1)} %get-tuple-element.79), channel_id=1, source_target_pairs={{0,32},{1,33},{2,34},{3,35},{4,36},{5,37},{6,38},{7,39},{8,40},{9,... | collective-permute-start | bytes 755720 | tf_op jit(solution)/shard_map/ppermute | solution.py:39
  150.5 1.5 collective-permute-start.23
  152.0 10.6 %collective-permute-done.21.refs_1_ = bf16[41,8,384]{2,1,0:T(8,128)(2,1)S(1)} collective-permute-done((bf16[41,8,384]{2,1,0:T(8,128)(2,1)S(1)}, bf16[41,8,384]{2,1,0:T(8,128)(2,1)S(1)}, u32[]{:S(2)}, u32[]{:S(2)}) %collective-permute-start.21) | collective-permute-done | bytes 251936 | tf_op jit(solution)/shard_map/ppermute | solution.py:39
  162.8 16.0 %all_to_all.28.got_ref = bf16[8,6,8,384]{3,2,1,0:T(8,128)(2,1)S(1)} all-to-all(bf16[8,6,8,384]{3,2,1,0:T(8,128)(2,1)S(1)} %shard_map.223), channel_id=1, replica_groups={{0,2,4,6,8,10,12,14},{1,3,5,7,9,11,13,15},{16,18,20,22,24,26,28,30},{17..., dimensions={0} | all-to-all | bytes 589824 | tf_op jit(solution)/shard_map/all_to_all | solution.py:47
  178.8 0.7 shard_map.224
  (28 shorter events, 2.0 us)
Async XLA Ops:
  0.6 3.3 %copy-start = (s32[48,8]{0,1:T(8,128)S(1)}, s32[48,8]{0,1:T(8,128)}, u32[]{:S(2)}) copy-start(s32[48,8]{0,1:T(8,128)} %param.19) | copy-start | bytes 4612
  28.0 12.6 %collective-permute-start.2 = (bf16[8,8,1920]{2,1,0:T(8,128)(2,1)S(1)}, bf16[8,8,1920]{2,1,0:T(8,128)(2,1)S(1)}, u32[]{:S(2)}, u32[]{:S(2)}) collective-permute-start(bf16[8,8,1920]{2,1,0:T(8,128)(2,1)S(1)} %all_to_all.25.refs_0_), channel_id=1, source_target_pairs={{0,48},{1,17},{2,50},{3,19},{4,52},{5,21},{6,54},{7,23},{8,56},{9,... | collective-permute-start | bytes 737288 | tf_op jit(solution)/shard_map/ppermute | solution.py:39
  31.0 9.6 %collective-permute-start.1 = (bf16[8,8,1920]{2,1,0:T(8,128)(2,1)S(1)}, bf16[8,8,1920]{2,1,0:T(8,128)(2,1)S(1)}, u32[]{:S(2)}, u32[]{:S(2)}) collective-permute-start(bf16[8,8,1920]{2,1,0:T(8,128)(2,1)S(1)} %all_to_all.25.refs_0_), channel_id=1, source_target_pairs={{0,32},{1,33},{2,34},{3,35},{4,36},{5,37},{6,38},{7,39},{8,40},{9,... | collective-permute-start | bytes 737288 | tf_op jit(solution)/shard_map/ppermute | solution.py:39
  31.7 10.1 %collective-permute-start = (bf16[8,8,1920]{2,1,0:T(8,128)(2,1)S(1)}, bf16[8,8,1920]{2,1,0:T(8,128)(2,1)S(1)}, u32[]{:S(2)}, u32[]{:S(2)}) collective-permute-start(bf16[8,8,1920]{2,1,0:T(8,128)(2,1)S(1)} %all_to_all.25.refs_0_), channel_id=1, source_target_pairs={{0,16},{1,49},{2,18},{3,51},{4,20},{5,53},{6,22},{7,55},{8,24},{9,... | collective-permute-start | bytes 737288 | tf_op jit(solution)/shard_map/ppermute | solution.py:39
  32.6 1.2 collective-permute-start.4
  34.6 18.3 %all-to-all-start.1 = ((bf16[8,8,2944]{2,1,0:T(8,128)(2,1)}), bf16[8,8,2944]{2,1,0:T(8,128)(2,1)S(1)}, u32[]{:S(2)}, u32[]{:S(2)}) async-start(bf16[8,8,2944]{2,1,0:T(8,128)(2,1)} %broadcast_in_dim.7), calls=%async_computation.1 | async-start | bytes 753664 | tf_op jit(solution)/shard_map/all_to_all | solution.py:47
  41.8 12.8 %collective-permute-start.3 = (bf16[32,8,1920]{2,1,0:T(8,128)(2,1)S(1)}, bf16[32,8,1920]{2,1,0:T(8,128)(2,1)S(1)}, u32[]{:S(2)}, u32[]{:S(2)}) collective-permute-start(bf16[32,8,1920]{2,1,0:T(8,128)(2,1)S(1)} %shard_map.210.own_ref), channel_id=1, source_target_pairs={{0,1},{1,0},{2,3},{3,2},{4,5},{5,4},{6,7},{7,6},{8,9},{9,8},{10,11... | collective-permute-start | bytes 2949128 | tf_op jit(solution)/shard_map/ppermute | solution.py:43
  53.0 1.7 collective-permute-start.5
  56.1 6.7 %collective-permute-start.8 = (bf16[64,384]{1,0:T(8,128)(2,1)S(1)}, bf16[64,384]{1,0:T(8,128)(2,1)S(1)}, u32[]{:S(2)}, u32[]{:S(2)}) collective-permute-start(bf16[64,384]{1,0:T(8,128)(2,1)S(1)} %get-tuple-element.49.refs_0_), channel_id=1, source_target_pairs={{48,0},{49,1},{50,2},{51,3},{52,4},{53,5},{54,6},{55,7},{56,8},{57... | collective-permute-start | bytes 147464 | tf_op jit(solution)/shard_map/ppermute | solution.py:31
  58.0 5.6 %collective-permute-start.7 = (bf16[64,384]{1,0:T(8,128)(2,1)S(1)}, bf16[64,384]{1,0:T(8,128)(2,1)S(1)}, u32[]{:S(2)}, u32[]{:S(2)}) collective-permute-start(bf16[64,384]{1,0:T(8,128)(2,1)S(1)} %get-tuple-element.49.refs_0_), channel_id=1, source_target_pairs={{32,0},{33,1},{34,2},{35,3},{36,4},{37,5},{38,6},{39,7},{40,8},{41... | collective-permute-start | bytes 147464 | tf_op jit(solution)/shard_map/ppermute | solution.py:31
  59.9 4.1 %collective-permute-start.6 = (bf16[64,384]{1,0:T(8,128)(2,1)S(1)}, bf16[64,384]{1,0:T(8,128)(2,1)S(1)}, u32[]{:S(2)}, u32[]{:S(2)}) collective-permute-start(bf16[64,384]{1,0:T(8,128)(2,1)S(1)} %get-tuple-element.49.refs_0_), channel_id=1, source_target_pairs={{16,0},{17,1},{18,2},{19,3},{20,4},{21,5},{22,6},{23,7},{24,8},{25... | collective-permute-start | bytes 147464 | tf_op jit(solution)/shard_map/ppermute | solution.py:31
  67.5 2.9 %collective-permute-start.9 = (bf16[4,41,8,384]{3,2,1,0:T(8,128)(2,1)S(1)}, bf16[4,41,8,384]{3,2,1,0:T(8,128)(2,1)S(1)}, u32[]{:S(2)}, u32[]{:S(2)}) collective-permute-start(bf16[4,41,8,384]{3,2,1,0:T(8,128)(2,1)S(1)} %get-tuple-element.60), channel_id=1, source_target_pairs={{0,1},{1,0},{2,3},{3,2},{4,5},{5,4},{6,7},{7,6},{8,9},{9,8},{10,11... | collective-permute-start | bytes 3022856 | tf_op jit(solution)/shard_map/ppermute | solution.py:43
  70.6 13.6 %collective-permute-start.10 = (bf16[41,8,384]{2,1,0:T(8,128)(2,1)S(1)}, bf16[41,8,384]{2,1,0:T(8,128)(2,1)S(1)}, u32[]{:S(2)}, u32[]{:S(2)}) collective-permute-start(bf16[41,8,384]{2,1,0:T(8,128)(2,1)S(1)} %get-tuple-element.62), channel_id=1, source_target_pairs={{0,16},{1,49},{2,18},{3,51},{4,20},{5,53},{6,22},{7,55},{8,24},{9,... | collective-permute-start | bytes 755720 | tf_op jit(solution)/shard_map/ppermute | solution.py:39
  71.3 14.4 %collective-permute-start.11 = (bf16[41,8,384]{2,1,0:T(8,128)(2,1)S(1)}, bf16[41,8,384]{2,1,0:T(8,128)(2,1)S(1)}, u32[]{:S(2)}, u32[]{:S(2)}) collective-permute-start(bf16[41,8,384]{2,1,0:T(8,128)(2,1)S(1)} %get-tuple-element.63), channel_id=1, source_target_pairs={{0,32},{1,33},{2,34},{3,35},{4,36},{5,37},{6,38},{7,39},{8,40},{9,... | collective-permute-start | bytes 755720 | tf_op jit(solution)/shard_map/ppermute | solution.py:39
  74.3 11.4 %collective-permute-start.12 = (bf16[41,8,384]{2,1,0:T(8,128)(2,1)S(1)}, bf16[41,8,384]{2,1,0:T(8,128)(2,1)S(1)}, u32[]{:S(2)}, u32[]{:S(2)}) collective-permute-start(bf16[41,8,384]{2,1,0:T(8,128)(2,1)S(1)} %get-tuple-element.64), channel_id=1, source_target_pairs={{0,48},{1,17},{2,50},{3,19},{4,52},{5,21},{6,54},{7,23},{8,56},{9,... | collective-permute-start | bytes 755720 | tf_op jit(solution)/shard_map/ppermute | solution.py:39
  115.7 10.7 %collective-permute-start.15 = (bf16[8,8,1920]{2,1,0:T(8,128)(2,1)S(1)}, bf16[8,8,1920]{2,1,0:T(8,128)(2,1)S(1)}, u32[]{:S(2)}, u32[]{:S(2)}) collective-permute-start(bf16[8,8,1920]{2,1,0:T(8,128)(2,1)S(1)} %all_to_all.27.refs_0_), channel_id=1, source_target_pairs={{0,48},{1,17},{2,50},{3,19},{4,52},{5,21},{6,54},{7,23},{8,56},{9,... | collective-permute-start | bytes 737288 | tf_op jit(solution)/shard_map/ppermute | solution.py:39
  116.3 10.1 %collective-permute-start.14 = (bf16[8,8,1920]{2,1,0:T(8,128)(2,1)S(1)}, bf16[8,8,1920]{2,1,0:T(8,128)(2,1)S(1)}, u32[]{:S(2)}, u32[]{:S(2)}) collective-permute-start(bf16[8,8,1920]{2,1,0:T(8,128)(2,1)S(1)} %all_to_all.27.refs_0_), channel_id=1, source_target_pairs={{0,32},{1,33},{2,34},{3,35},{4,36},{5,37},{6,38},{7,39},{8,40},{9,... | collective-permute-start | bytes 737288 | tf_op jit(solution)/shard_map/ppermute | solution.py:39
  117.4 11.0 %collective-permute-start.13 = (bf16[8,8,1920]{2,1,0:T(8,128)(2,1)S(1)}, bf16[8,8,1920]{2,1,0:T(8,128)(2,1)S(1)}, u32[]{:S(2)}, u32[]{:S(2)}) collective-permute-start(bf16[8,8,1920]{2,1,0:T(8,128)(2,1)S(1)} %all_to_all.27.refs_0_), channel_id=1, source_target_pairs={{0,16},{1,49},{2,18},{3,51},{4,20},{5,53},{6,22},{7,55},{8,24},{9,... | collective-permute-start | bytes 737288 | tf_op jit(solution)/shard_map/ppermute | solution.py:39
  128.5 2.7 %collective-permute-start.16 = (bf16[32,8,1920]{2,1,0:T(8,128)(2,1)S(1)}, bf16[32,8,1920]{2,1,0:T(8,128)(2,1)S(1)}, u32[]{:S(2)}, u32[]{:S(2)}) collective-permute-start(bf16[32,8,1920]{2,1,0:T(8,128)(2,1)S(1)} %shard_map.218.own_ref), channel_id=1, source_target_pairs={{0,1},{1,0},{2,3},{3,2},{4,5},{5,4},{6,7},{7,6},{8,9},{9,8},{10,11... | collective-permute-start | bytes 2949128 | tf_op jit(solution)/shard_map/ppermute | solution.py:43
  132.6 7.4 %collective-permute-start.19 = (bf16[64,384]{1,0:T(8,128)(2,1)S(1)}, bf16[64,384]{1,0:T(8,128)(2,1)S(1)}, u32[]{:S(2)}, u32[]{:S(2)}) collective-permute-start(bf16[64,384]{1,0:T(8,128)(2,1)S(1)} %get-tuple-element.65.refs_0_), channel_id=1, source_target_pairs={{48,0},{49,1},{50,2},{51,3},{52,4},{53,5},{54,6},{55,7},{56,8},{57... | collective-permute-start | bytes 147464 | tf_op jit(solution)/shard_map/ppermute | solution.py:31
  133.6 6.7 %collective-permute-start.18 = (bf16[64,384]{1,0:T(8,128)(2,1)S(1)}, bf16[64,384]{1,0:T(8,128)(2,1)S(1)}, u32[]{:S(2)}, u32[]{:S(2)}) collective-permute-start(bf16[64,384]{1,0:T(8,128)(2,1)S(1)} %get-tuple-element.65.refs_0_), channel_id=1, source_target_pairs={{32,0},{33,1},{34,2},{35,3},{36,4},{37,5},{38,6},{39,7},{40,8},{41... | collective-permute-start | bytes 147464 | tf_op jit(solution)/shard_map/ppermute | solution.py:31
  137.4 4.1 %collective-permute-start.17 = (bf16[64,384]{1,0:T(8,128)(2,1)S(1)}, bf16[64,384]{1,0:T(8,128)(2,1)S(1)}, u32[]{:S(2)}, u32[]{:S(2)}) collective-permute-start(bf16[64,384]{1,0:T(8,128)(2,1)S(1)} %get-tuple-element.65.refs_0_), channel_id=1, source_target_pairs={{16,0},{17,1},{18,2},{19,3},{20,4},{21,5},{22,6},{23,7},{24,8},{25... | collective-permute-start | bytes 147464 | tf_op jit(solution)/shard_map/ppermute | solution.py:31
  144.6 2.9 %collective-permute-start.20 = (bf16[4,41,8,384]{3,2,1,0:T(8,128)(2,1)S(1)}, bf16[4,41,8,384]{3,2,1,0:T(8,128)(2,1)S(1)}, u32[]{:S(2)}, u32[]{:S(2)}) collective-permute-start(bf16[4,41,8,384]{3,2,1,0:T(8,128)(2,1)S(1)} %get-tuple-element.76), channel_id=1, source_target_pairs={{0,1},{1,0},{2,3},{3,2},{4,5},{5,4},{6,7},{7,6},{8,9},{9,8},{10,11... | collective-permute-start | bytes 3022856 | tf_op jit(solution)/shard_map/ppermute | solution.py:43
  147.8 14.8 %collective-permute-start.21 = (bf16[41,8,384]{2,1,0:T(8,128)(2,1)S(1)}, bf16[41,8,384]{2,1,0:T(8,128)(2,1)S(1)}, u32[]{:S(2)}, u32[]{:S(2)}) collective-permute-start(bf16[41,8,384]{2,1,0:T(8,128)(2,1)S(1)} %get-tuple-element.78), channel_id=1, source_target_pairs={{0,16},{1,49},{2,18},{3,51},{4,20},{5,53},{6,22},{7,55},{8,24},{9,... | collective-permute-start | bytes 755720 | tf_op jit(solution)/shard_map/ppermute | solution.py:39
  148.4 14.2 %collective-permute-start.22 = (bf16[41,8,384]{2,1,0:T(8,128)(2,1)S(1)}, bf16[41,8,384]{2,1,0:T(8,128)(2,1)S(1)}, u32[]{:S(2)}, u32[]{:S(2)}) collective-permute-start(bf16[41,8,384]{2,1,0:T(8,128)(2,1)S(1)} %get-tuple-element.79), channel_id=1, source_target_pairs={{0,32},{1,33},{2,34},{3,35},{4,36},{5,37},{6,38},{7,39},{8,40},{9,... | collective-permute-start | bytes 755720 | tf_op jit(solution)/shard_map/ppermute | solution.py:39
  150.5 12.1 %collective-permute-start.23 = (bf16[41,8,384]{2,1,0:T(8,128)(2,1)S(1)}, bf16[41,8,384]{2,1,0:T(8,128)(2,1)S(1)}, u32[]{:S(2)}, u32[]{:S(2)}) collective-permute-start(bf16[41,8,384]{2,1,0:T(8,128)(2,1)S(1)} %get-tuple-element.80), channel_id=1, source_target_pairs={{0,48},{1,17},{2,50},{3,19},{4,52},{5,21},{6,54},{7,23},{8,56},{9,... | collective-permute-start | bytes 755720 | tf_op jit(solution)/shard_map/ppermute | solution.py:39
